TPU v7x, 32 devices: a whole 2x2x4 slice. The times are simulated.
32 devices in a mesh: dp: 4 (over z), row: 4 (over y, x), col: 2 (over core).
Axes of the slice: x: 2, y: 2, z: 4, core: 2. Of those that a mesh axis runs over, the one named last changes fastest.
Arguments:
- tokens: bfloat16 [4096, 1600], P(('dp', 'row'), 'col'), may hold values from -6 to 6
- segment_ids: int32 [4, 1024], P('dp'), may hold values from 0 to 3, as said below
- first_gain: float32 [1600], replicated, may hold values from 0.1 to 1.9
- first_shift: float32 [1600], replicated, may hold values from -3 to 3
- triple_weight: bfloat16 [1600, 4800], P('col', 'row'), may hold values from -1 to 1
- query_bias: float32 [1600], replicated, may hold values from -3 to 3
- value_bias: float32 [1600], replicated, may hold values from -3 to 3
- proj_weight: bfloat16 [1600, 1600], P('row', 'col'), may hold values from -0.4375 to 0.4375
- proj_bias: float32 [1600], replicated, may hold values from -3 to 3
- second_gain: float32 [1600], replicated, may hold values from 0.1 to 1.9
- second_shift: float32 [1600], replicated, may hold values from -3 to 3
- expand_weight: bfloat16 [1600, 6400], P('col', 'row'), may hold values from -0.15625 to 0.15625
- expand_bias: float32 [6400], replicated, may hold values from -3 to 3
- shrink_weight: bfloat16 [6400, 1600], P('row', 'col'), may hold values from -0.078125 to 0.078125
- shrink_bias: float32 [1600], replicated, may hold values from -3 to 3
- cotangent: bfloat16 [4096, 1600], P(('dp', 'row'), 'col'), may hold values from -6 to 6
Outputs:
- block_out: bfloat16 [4096, 1600], P(('dp', 'row'), 'col')
- input_grad: float32 [4096, 1600], P(('dp', 'row'), 'col')
- first_gain_grad: float32 [1600], replicated
- first_shift_grad: float32 [1600], replicated
- triple_grad: float32 [2, 800, 4800], P('col', 'dp', 'row')
- query_bias_grad: float32 [1600], replicated
- value_bias_grad: float32 [1600], replicated
- proj_grad: float32 [4, 400, 1600], P('row', 'dp', 'col')
- proj_bias_grad: float32 [1600], replicated
- second_gain_grad: float32 [1600], replicated
- second_shift_grad: float32 [1600], replicated
- expand_grad: float32 [2, 800, 6400], P('col', 'dp', 'row')
- expand_bias_grad: float32 [6400], replicated
- shrink_grad: float32 [4, 1600, 1600], P('row', 'dp', 'col')
- shrink_bias_grad: float32 [1600], replicated
Inputs may be any that keep to these rules, and one draw needn't show every extreme that they name: `segment_ids`: each row lists the sequences of one data group in order: it starts at 0 and rises by one where a new sequence starts. A row holds 1 to 4 sequences; in every draw some row holds exactly 4 and another holds a single sequence of 1024 tokens.
All inputs are finite; a program needn't handle non-finite values.
Results may differ from a plain program's by a relative error of at most 0.014.
Values may be sent and summed in bfloat16 or wider, within the bound.
A program may use at most 192 MiB of HBM per device.

v0:
```python
import math

import jax
import jax.numpy as jnp
from jax import lax
from jax.sharding import PartitionSpec as P

HEADS = 25
HEAD_DIM = 64
FF = 6400


EPS = 1e-05
NEG = -1e30


def gelu_tanh(values):
    return (
        0.5
        * values
        * (1.0 + jnp.tanh(0.7978845608028654 * (values + 0.044715 * values * values * values)))
    )


def spread_rows(own_part):
    return lax.all_gather(own_part, "row", axis=0, tiled=True)


def reduce_cols(partial_sum):
    return lax.psum_scatter(partial_sum, "col", scatter_dimension=0, tiled=True)


def spread_cols(own_part):
    return lax.all_gather(own_part, "col", axis=0, tiled=True)


def reduce_rows(partial_sum):
    return lax.psum_scatter(partial_sum, "row", scatter_dimension=0, tiled=True)


def to_heads(hidden):
    return lax.all_to_all(hidden, "row", split_axis=0, concat_axis=1, tiled=True)


def to_hidden(headed):
    return lax.all_to_all(headed, "row", split_axis=1, concat_axis=0, tiled=True)


def gather_keys(own_part):
    return lax.all_gather(own_part, ("row", "col"), axis=0, tiled=True)


def feature_totals(first_term, second_term):
    return lax.psum(
        (jnp.sum(first_term, axis=1, keepdims=True), jnp.sum(second_term, axis=1, keepdims=True)),
        "col",
    )


def norm_local(matrix, gain, shift):
    width = HEADS * HEAD_DIM
    total, square = feature_totals(matrix, matrix * matrix)
    average = total / width
    rstd = lax.rsqrt(square / width - average * average + EPS)
    normed_hat = (matrix - average) * rstd
    return (normed_hat * gain + shift, normed_hat, rstd)


def norm_back(grad_in, normed_hat, rstd, gain):
    width = HEADS * HEAD_DIM
    scaled = grad_in * gain
    total, mixed = feature_totals(scaled, scaled * normed_hat)
    return rstd * (scaled - total / width - normed_hat * mixed / width)


def head_split(matrix):
    rows = matrix.shape[0]
    group_size = math.gcd(HEADS, 5)
    return matrix.reshape(rows, HEADS // group_size, group_size, HEAD_DIM).transpose(1, 0, 2, 3)


def head_join(blocks):
    rows = blocks.shape[1]
    return blocks.transpose(1, 0, 2, 3).reshape(rows, HEADS * HEAD_DIM)


def attention_forward(query_part, key_part, value_part, allowed):
    scaling = HEAD_DIM ** (-0.5)

    def one_group(blocks):
        query_block, key_block, value_block = blocks
        scores = (
            jnp.einsum("qhd,khd->hqk", query_block, key_block, preferred_element_type=jnp.float32)
            * scaling
        )
        scores = jnp.where(allowed[None], scores, NEG)
        highest = jnp.max(scores, axis=-1)
        log_total = highest + jnp.log(jnp.sum(jnp.exp(scores - highest[..., None]), axis=-1))
        weights = jnp.exp(scores - log_total[..., None]).astype(jnp.bfloat16)
        combined = jnp.einsum(
            "hqk,khd->qhd", weights, value_block, preferred_element_type=jnp.float32
        ).astype(jnp.bfloat16)
        return (combined, log_total)

    combined, log_total = lax.map(
        one_group, (head_split(query_part), head_split(key_part), head_split(value_part))
    )
    return (head_join(combined), log_total)


def attention_backward(
    query_part, key_part, value_part, attended, attended_grad, log_total, allowed
):
    scaling = HEAD_DIM ** (-0.5)

    def one_group(blocks):
        query_block, key_block, value_block, out_block, grad_block, lse_block = blocks
        scores = (
            jnp.einsum("qhd,khd->hqk", query_block, key_block, preferred_element_type=jnp.float32)
            * scaling
        )
        scores = jnp.where(allowed[None], scores, NEG)
        weights = jnp.exp(scores - lse_block[..., None])
        weights_half = weights.astype(jnp.bfloat16)
        value_grad = jnp.einsum(
            "hqk,qhd->khd", weights_half, grad_block, preferred_element_type=jnp.float32
        )
        weight_grad = jnp.einsum(
            "qhd,khd->hqk", grad_block, value_block, preferred_element_type=jnp.float32
        )
        delta = jnp.sum(
            grad_block.astype(jnp.float32) * out_block.astype(jnp.float32), axis=-1
        ).transpose(1, 0)
        mix_half = (weights * (weight_grad - delta[..., None])).astype(jnp.bfloat16)
        query_grad = (
            jnp.einsum("hqk,khd->qhd", mix_half, key_block, preferred_element_type=jnp.float32)
            * scaling
        )
        key_grad = (
            jnp.einsum("hqk,qhd->khd", mix_half, query_block, preferred_element_type=jnp.float32)
            * scaling
        )
        return (query_grad, key_grad, value_grad)

    query_grad, key_grad, value_grad = lax.map(
        one_group,
        (
            head_split(query_part),
            head_split(key_part),
            head_split(value_part),
            head_split(attended),
            head_split(attended_grad),
            log_total,
        ),
    )
    return (head_join(query_grad), head_join(key_grad), head_join(value_grad))


def shards(
    tokens,
    segment_ids,
    first_gain,
    first_shift,
    triple_weight,
    query_bias,
    value_bias,
    proj_weight,
    proj_bias,
    second_gain,
    second_shift,
    expand_weight,
    expand_bias,
    shrink_weight,
    shrink_bias,
    cotangent,
):
    width = HEADS * HEAD_DIM
    row_count = lax.axis_size("row")
    col_count = lax.axis_size("col")
    row_index = lax.axis_index("row")
    col_index = lax.axis_index("col")
    col_width = tokens.shape[1]
    group_rows = segment_ids.shape[1]
    query_rows = group_rows // (row_count * col_count)
    hidden_width = expand_weight.shape[1]
    triple_width = triple_weight.shape[1]

    def col_slice(vector):
        return lax.dynamic_slice_in_dim(vector, col_index * col_width, col_width)

    def col_place(vector):
        return lax.dynamic_update_slice_in_dim(
            jnp.zeros((width,), jnp.float32), vector, col_index * col_width, 0
        )

    tokens_wide = tokens.astype(jnp.float32)
    first_normed, first_hat, first_rstd = norm_local(
        tokens_wide, col_slice(first_gain), col_slice(first_shift)
    )
    first_half = first_normed.astype(jnp.bfloat16)
    first_all = spread_rows(first_half)
    full_bias = jnp.concatenate([query_bias, jnp.zeros((width,), jnp.float32), value_bias])
    triple_sum = reduce_cols(jnp.dot(first_all, triple_weight, preferred_element_type=jnp.float32))
    triple_local = (
        triple_sum + lax.dynamic_slice_in_dim(full_bias, row_index * triple_width, triple_width)
    ).astype(jnp.bfloat16)
    headed = to_heads(triple_local)
    query_part = headed[:, :width]
    pair_local = headed[:, width:]
    pair_all = gather_keys(pair_local)
    segment_row = segment_ids[0]
    query_start = col_index * (group_rows // col_count) + row_index * query_rows
    query_places = query_start + jnp.arange(query_rows, dtype=jnp.int32)
    query_segments = lax.dynamic_slice_in_dim(segment_row, query_start, query_rows)
    key_places = (
        jnp.arange(group_rows, dtype=jnp.int32)
        .reshape(col_count, row_count, query_rows)
        .transpose(1, 0, 2)
        .reshape(group_rows)
    )
    key_segments = (
        segment_row.reshape(col_count, row_count, query_rows).transpose(1, 0, 2).reshape(group_rows)
    )
    allowed = (query_segments[:, None] == key_segments[None, :]) & (
        key_places[None, :] <= query_places[:, None]
    )
    attended, log_total = attention_forward(
        query_part, pair_all[:, :width], pair_all[:, width:], allowed
    )
    attended_hidden = to_hidden(attended)
    attended_all = spread_cols(attended_hidden)
    middle = (
        tokens_wide
        + reduce_rows(jnp.dot(attended_all, proj_weight, preferred_element_type=jnp.float32))
        + col_slice(proj_bias)
    )
    second_normed, second_hat, second_rstd = norm_local(
        middle, col_slice(second_gain), col_slice(second_shift)
    )
    second_half = second_normed.astype(jnp.bfloat16)
    second_all = spread_rows(second_half)
    before_act = reduce_cols(
        jnp.dot(second_all, expand_weight, preferred_element_type=jnp.float32)
    ) + lax.dynamic_slice_in_dim(expand_bias, row_index * hidden_width, hidden_width)
    activated = gelu_tanh(before_act).astype(jnp.bfloat16)
    activated_all = spread_cols(activated)
    block_out = (
        middle
        + reduce_rows(jnp.dot(activated_all, shrink_weight, preferred_element_type=jnp.float32))
        + col_slice(shrink_bias)
    ).astype(jnp.bfloat16)
    pair_back = gather_keys(pair_local)
    activated_back = spread_cols(activated)
    second_back = spread_rows(second_half)
    attended_back = spread_cols(attended_hidden)
    first_back = spread_rows(first_half)
    cot_wide = cotangent.astype(jnp.float32)
    cot_all = spread_rows(cotangent)
    shrink_grad = jnp.einsum(
        "tf,td->fd", activated_back, cot_all, preferred_element_type=jnp.float32
    )
    shrink_bias_part = jnp.sum(cot_wide, axis=0)
    act_grad = reduce_cols(
        jnp.einsum("td,fd->tf", cot_all, shrink_weight, preferred_element_type=jnp.float32)
    )
    gelu_back = jax.vjp(gelu_tanh, before_act)[1]
    before_grad = gelu_back(act_grad)[0]
    expand_bias_part = jnp.sum(before_grad, axis=0)
    hidden_grad = before_grad.astype(jnp.bfloat16)
    hidden_all = spread_cols(hidden_grad)
    expand_grad = jnp.einsum(
        "td,tf->df", second_back, hidden_all, preferred_element_type=jnp.float32
    )
    second_normed_grad = reduce_rows(
        jnp.einsum("tf,df->td", hidden_all, expand_weight, preferred_element_type=jnp.float32)
    )
    middle_grad = cot_wide + norm_back(
        second_normed_grad, second_hat, second_rstd, col_slice(second_gain)
    )
    second_gain_part = jnp.sum(second_normed_grad * second_hat, axis=0)
    second_shift_part = jnp.sum(second_normed_grad, axis=0)
    middle_half = middle_grad.astype(jnp.bfloat16)
    middle_all = spread_rows(middle_half)
    proj_grad = jnp.einsum(
        "tc,td->cd", attended_back, middle_all, preferred_element_type=jnp.float32
    )
    proj_bias_part = jnp.sum(middle_grad, axis=0)
    attended_grad_hidden = reduce_cols(
        jnp.einsum("td,cd->tc", middle_all, proj_weight, preferred_element_type=jnp.float32)
    ).astype(jnp.bfloat16)
    attended_grad = to_heads(attended_grad_hidden)
    query_grad, key_grad, value_grad = attention_backward(
        query_part,
        pair_back[:, :width],
        pair_back[:, width:],
        attended,
        attended_grad,
        log_total,
        allowed,
    )
    pair_grad = lax.psum_scatter(
        jnp.concatenate([key_grad, value_grad], axis=1).astype(jnp.bfloat16),
        ("row", "col"),
        scatter_dimension=0,
        tiled=True,
    ).astype(jnp.float32)
    query_bias_part = jnp.sum(query_grad, axis=0)
    value_bias_part = jnp.sum(pair_grad[:, width:], axis=0)
    triple_half = jnp.concatenate([query_grad, pair_grad], axis=1).astype(jnp.bfloat16)
    triple_hidden = to_hidden(triple_half)
    triple_all = spread_cols(triple_hidden)
    triple_grad = jnp.einsum(
        "tc,tk->ck", first_back, triple_all, preferred_element_type=jnp.float32
    )
    first_normed_grad = reduce_rows(
        jnp.einsum("tk,ck->tc", triple_all, triple_weight, preferred_element_type=jnp.float32)
    )
    input_grad = middle_grad + norm_back(
        first_normed_grad, first_hat, first_rstd, col_slice(first_gain)
    )
    first_gain_part = jnp.sum(first_normed_grad * first_hat, axis=0)
    first_shift_part = jnp.sum(first_normed_grad, axis=0)
    shrink_owned, expand_owned, proj_owned, triple_owned = (
        lax.psum_scatter(
            shrink_grad.astype(jnp.bfloat16), "dp", scatter_dimension=0, tiled=True
        ).astype(jnp.float32),
        lax.psum_scatter(
            expand_grad.astype(jnp.bfloat16), "dp", scatter_dimension=0, tiled=True
        ).astype(jnp.float32),
        lax.psum_scatter(
            proj_grad.astype(jnp.bfloat16), "dp", scatter_dimension=0, tiled=True
        ).astype(jnp.float32),
        lax.psum_scatter(
            triple_grad.astype(jnp.bfloat16), "dp", scatter_dimension=0, tiled=True
        ).astype(jnp.float32),
    )
    expand_bias_full = lax.dynamic_update_slice_in_dim(
        jnp.zeros((FF,), jnp.float32), expand_bias_part, row_index * hidden_width, 0
    )
    (
        first_gain_grad,
        first_shift_grad,
        query_bias_grad,
        value_bias_grad,
        proj_bias_grad,
        second_gain_grad,
        second_shift_grad,
        expand_bias_grad,
        shrink_bias_grad,
    ) = lax.psum(
        (
            col_place(first_gain_part),
            col_place(first_shift_part),
            query_bias_part,
            value_bias_part,
            col_place(proj_bias_part),
            col_place(second_gain_part),
            col_place(second_shift_part),
            expand_bias_full,
            col_place(shrink_bias_part),
        ),
        ("dp", "row", "col"),
    )
    return (
        block_out,
        input_grad,
        first_gain_grad,
        first_shift_grad,
        triple_owned[None],
        query_bias_grad,
        value_bias_grad,
        proj_owned[None],
        proj_bias_grad,
        second_gain_grad,
        second_shift_grad,
        expand_owned[None],
        expand_bias_grad,
        shrink_owned[None],
        shrink_bias_grad,
    )


def solution(mesh):
    in_specs = (
        P(("dp", "row"), "col"),
        P("dp", None),
        P(),
        P(),
        P("col", "row"),
        P(),
        P(),
        P("row", "col"),
        P(),
        P(),
        P(),
        P("col", "row"),
        P(),
        P("row", "col"),
        P(),
        P(("dp", "row"), "col"),
    )
    out_specs = (
        P(("dp", "row"), "col"),
        P(("dp", "row"), "col"),
        P(),
        P(),
        P("col", "dp", "row"),
        P(),
        P(),
        P("row", "dp", "col"),
        P(),
        P(),
        P(),
        P("col", "dp", "row"),
        P(),
        P("row", "dp", "col"),
        P(),
    )
    return jax.shard_map(shards, mesh=mesh, in_specs=in_specs, out_specs=out_specs, check_vma=False)
```

profile of v0, /device:TPU:25, one launch (start us, length us, event | category | flops | bytes accessed | tf_op | source)
XLA Modules:
  0.0 1060.5 jit_solution(4812785820477544003)
XLA Ops:
  10.1 2.8 all-reduce.7
  15.0 31.8 %all-gather.9.cloned.1.call-done = bf16[1024,800]{0,1:T(8,128)(2,1)} async-done(((bf16[256,800]{0,1:T(8,128)(2,1)}), bf16[1024,800]{0,1:T(8,128)(2,1)}) %all-gather.9.cloned.1.call-update) | async-done | bytes 1638416 | tf_op jit(solution)/shard_map/all_gather | solution.py:26
  46.8 7.0 fusion.84
  54.7 12.7 %reduce-scatter.19.cloned.1.call-done = f32[512,1200]{0,1:T(8,128)} async-done(((f32[1024,1200]{0,1:T(8,128)}), f32[512,1200]{0,1:T(8,128)}) %reduce-scatter.19.cloned.1.call-update) | async-done | bytes 2457616 | tf_op jit(solution)/shard_map/reduce_scatter | solution.py:30
  69.4 18.6 %all_to_all.70 = bf16[4,128,1200]{1,2,0:T(8,128)(2,1)S(1)} all-to-all(bf16[4,128,1200]{1,2,0:T(8,128)(2,1)S(1)} %copy_bitcast_fusion.1), channel_id=1, replica_groups=mesh['dp'=4,'row'=4,'col'=2] {'row'}, dimensions={0} | all-to-all | bytes 2457600 | tf_op jit(solution)/shard_map/all_to_all | solution.py:42
  91.2 47.5 %all-gather.11.cloned.1.call-done = bf16[1024,3200]{0,1:T(8,128)(2,1)} async-done(((bf16[128,3200]{0,1:T(8,128)(2,1)}), bf16[1024,3200]{0,1:T(8,128)(2,1)}) %all-gather.11.cloned.1.call-update) | async-done | bytes 6553616 | tf_op jit(solution)/shard_map/all_gather | solution.py:50
  138.7 6.3 fusion.83
  145.0 23.5 %while.28 = (s32[]{:T(128)}, bf16[5,128,5,64]{1,3,2,0:T(8,128)(2,1)S(1)}, f32[5,5,128]{2,1,0:T(8,128)S(1)}, bf16[5,1024,5,64]{1,3,2,0:T(8,128)(2,1)}, bf16[5,128...) while((s32[]{:T(128)}, ...), condition=%wide.region_8.9_spmd.clone, body=%wide.region_5.8_spmd.clone.sunk | while | flops 175414656 | bytes 9902713 | solution.py:105
  168.5 9.4 all_to_all.71
  178.0 3.6 all_gather.34
  182.5 2.7 fusion.85
  186.2 42.9 %reduce-scatter.21.cloned.1.call-done = f32[256,800]{0,1:T(8,128)} async-done(((f32[1024,800]{0,1:T(8,128)}), f32[256,800]{0,1:T(8,128)}) %reduce-scatter.21.cloned.1.call-update) | async-done | bytes 819216 | tf_op jit(solution)/shard_map/reduce_scatter | solution.py:38
  230.6 3.5 all-reduce.6
  236.1 26.0 %all-gather.17.cloned.1.call-done = bf16[1024,800]{0,1:T(8,128)(2,1)} async-done(((bf16[256,800]{0,1:T(8,128)(2,1)}), bf16[1024,800]{0,1:T(8,128)(2,1)}) %all-gather.17.cloned.1.call-update) | async-done | bytes 1638416 | tf_op jit(solution)/shard_map/all_gather | solution.py:26
  262.0 8.6 fusion.87
  270.7 24.9 %all-gather.13.cloned.1.call-done = bf16[1024,800]{0,1:T(8,128)(2,1)} async-done(((bf16[256,800]{0,1:T(8,128)(2,1)}), bf16[1024,800]{0,1:T(8,128)(2,1)}) %all-gather.13.cloned.1.call-update) | async-done | bytes 1638416 | tf_op jit(solution)/shard_map/all_gather | solution.py:26
  295.6 7.7 fusion.86
  304.2 8.7 reduce-scatter.27.cloned.1.call-done
  312.8 17.7 %reduce-scatter.23.cloned.1.call-done = f32[512,1600]{0,1:T(8,128)} async-done(((f32[1024,1600]{0,1:T(8,128)}), f32[512,1600]{0,1:T(8,128)}) %reduce-scatter.23.cloned.1.call-update) | async-done | bytes 3276816 | tf_op jit(solution)/shard_map/reduce_scatter | solution.py:30
  330.5 6.5 fusion.79
  337.6 13.1 %all-gather.19.cloned.1.call-done = bf16[1024,1600]{0,1:T(8,128)(2,1)} async-done(((bf16[512,1600]{0,1:T(8,128)(2,1)}), bf16[1024,1600]{0,1:T(8,128)(2,1)}) %all-gather.19.cloned.1.call-update) | async-done | bytes 3276816 | tf_op jit(solution)/shard_map/all_gather | solution.py:34
  350.8 6.7 fusion.89
  357.8 7.9 all-gather.15.cloned.1.call-done
  365.7 6.8 fusion.88
  373.2 40.8 %reduce-scatter.29.cloned.1.call-done = f32[256,800]{0,1:T(8,128)} async-done(((f32[1024,800]{0,1:T(8,128)}), f32[256,800]{0,1:T(8,128)}) %reduce-scatter.29.cloned.1.call-update) | async-done | bytes 819216 | tf_op jit(solution)/shard_map/reduce_scatter | solution.py:38
  415.7 3.0 all-reduce.5
  418.6 43.3 %reduce-scatter.25.cloned.1.call-done = f32[256,800]{0,1:T(8,128)} async-done(((f32[1024,800]{0,1:T(8,128)}), f32[256,800]{0,1:T(8,128)}) %reduce-scatter.25.cloned.1.call-update) | async-done | bytes 819216 | tf_op jit(solution)/shard_map/reduce_scatter | solution.py:38
  465.5 31.4 %all-gather.21.cloned.1.call-done = bf16[1024,800]{0,1:T(8,128)(2,1)} async-done(((bf16[256,800]{0,1:T(8,128)(2,1)}), bf16[1024,800]{0,1:T(8,128)(2,1)}) %all-gather.21.cloned.1.call-update) | async-done | bytes 1638416 | tf_op jit(solution)/shard_map/all_gather | solution.py:26
  496.9 3.6 fusion.90
  500.5 10.0 reduce-scatter.31.cloned.1.call-done
  512.5 3.5 all-to-all-start.2
  516.1 6.3 all-to-all-done.2
  522.3 52.5 %while.29 = (s32[]{:T(128)}, f32[5,128,5,64]{1,3,2,0:T(8,128)S(1)}, bf16[5,1024,5,64]{1,3,2,0:T(8,128)(2,1)}, bf16[5,1024,5,64]{1,3,2,0:T(8,128)(2,1)}, bf16[5,1...) while((s32[]{:T(128)}, f32[5,128,5,64]{1,3,2,0:T(8,128)S(1)}, ...), condition=%wide.region_25.26_spmd.clone, body=%wide.region_23.25_spmd.clone.sunk | while | flops 426909056 | bytes 17467036 | solution.py:145
  574.8 6.7 pad_maximum_fusion
  581.5 9.3 copy.50
  591.0 63.6 %reduce-scatter.39.cloned.1.call-done = bf16[128,3200]{1,0:T(8,128)(2,1)} async-done(((bf16[1024,3200]{1,0:T(8,128)(2,1)}), bf16[128,3200]{1,0:T(8,128)(2,1)}) %reduce-scatter.39.cloned.1.call-update) | async-done | bytes 819216
  656.3 17.7 %all_to_all.72 = bf16[128,4,1200]{0,2,1:T(8,128)(2,1)S(1)} all-to-all(bf16[128,4,1200]{0,2,1:T(8,128)(2,1)S(1)} %bitcast.226), channel_id=1, replica_groups=mesh['dp'=4,'row'=4,'col'=2] {'row'}, dimensions={1} | all-to-all | bytes 2457600 | tf_op jit(solution)/shard_map/all_to_all | solution.py:46
  675.9 6.5 convolution_convert_fusion.1
  684.0 7.2 convolution_convert_fusion
  692.6 5.4 convolution_convert_fusion.2
  698.1 6.3 fusion.91
  706.6 35.3 %reduce-scatter.41.cloned.1.call-done = bf16[200,1600]{1,0:T(8,128)(2,1)} async-done(((bf16[800,1600]{1,0:T(8,128)(2,1)}), bf16[200,1600]{1,0:T(8,128)(2,1)}) %reduce-scatter.41.cloned.1.call-update) | async-done | bytes 640016
  746.6 34.3 %fusion.4 = bf16[112,800]{1,0:T(8,128)(2,1)S(1)} fusion(bf16[400,800]{1,0:T(8,128)(2,1)S(1)} %convolution_convert_fusion.3), kind=kCustom, calls=%all-reduce-scatter | all-reduce-scatter fusion | flops 358401 | bytes 819712
  782.3 32.0 %reduce-scatter.37.cloned.1.call-done = bf16[400,800]{1,0:T(8,128)(2,1)} async-done(((bf16[1600,800]{1,0:T(8,128)(2,1)}), bf16[400,800]{1,0:T(8,128)(2,1)}) %reduce-scatter.37.cloned.1.call-update) | async-done | bytes 640016 | tf_op jit(solution)/shard_map/reduce_scatter | solution.py:324
  821.1 38.2 %reduce-scatter.35.cloned.1.call-done = bf16[200,1200]{1,0:T(8,128)(2,1)} async-done(((bf16[800,1200]{1,0:T(8,128)(2,1)}), bf16[200,1200]{1,0:T(8,128)(2,1)}) %reduce-scatter.35.cloned.1.call-update) | async-done | bytes 480016 | tf_op jit(solution)/shard_map/reduce_scatter | solution.py:333
  861.5 46.1 %reduce-scatter.33.cloned.1.call-done = f32[256,800]{0,1:T(8,128)} async-done(((f32[1024,800]{0,1:T(8,128)}), f32[256,800]{0,1:T(8,128)}) %reduce-scatter.33.cloned.1.call-update) | async-done | bytes 819216 | tf_op jit(solution)/shard_map/reduce_scatter | solution.py:38
  909.3 3.0 all-reduce.4
  916.0 125.4 %all-reduce.10.cloned.1.call-done = (f32[1600]{0:T(1024)}, f32[1600]{0:T(1024)}, f32[1600]{0:T(1024)}, f32[1600]{0:T(1024)}, f32[1600]{0:T(1024)}, /*index=5*/f3...) async-done(((f32[1600]{0:T(1024)}, f32[1600]{0:T(1024)}, f32[1600]{0:T(1024)}, f32[1600]{0:T(1024)}, f32[1600]{0:T(1024)}, /*index=5*/f32[1600]{0:T(1024)}, ...) | async-done | bytes 76816 | tf_op jit(solution)/shard_map/psum | solution.py:350
  (256 shorter events, 142.1 us)
Async XLA Ops:
  7.2 288.4 %copy-start = (bf16[800,1600]{1,0:T(8,128)(2,1)S(1)}, bf16[800,1600]{1,0:T(8,128)(2,1)}, u32[]{:S(2)}) copy-start(bf16[800,1600]{1,0:T(8,128)(2,1)} %param.31) | copy-start | bytes 7680004
  7.2 39.6 %all-gather.9.cloned.1.call-start = ((), (), s32[]{:S(2)}) async-start(), calls=%async_computation.16 | async-start | bytes 2048000 | tf_op jit(solution)/shard_map/all_gather | solution.py:26
  15.0 52.5 %reduce-scatter.19.cloned.1.call-start = ((), (), s32[]{:S(2)}) async-start(), calls=%async_computation.17 | async-start | bytes 7372800 | tf_op jit(solution)/shard_map/reduce_scatter | solution.py:30
  53.9 84.8 %all-gather.11.cloned.1.call-start = ((), (), s32[]{:S(2)}) async-start(), calls=%async_computation.18 | async-start | bytes 7372800 | tf_op jit(solution)/shard_map/all_gather | solution.py:50
  69.4 20.7 %copy-start.23 = (s32[1,1024]{1,0:T(1,128)S(1)}, s32[1,1024]{1,0:T(1,128)}, u32[]{:S(2)}) copy-start(s32[1,1024]{1,0:T(1,128)} %param.21) | copy-start | bytes 12292
  88.0 1.0 copy-start.5
  90.0 139.1 %reduce-scatter.21.cloned.1.call-start = ((), (), s32[]{:S(2)}) async-start(), calls=%async_computation.19 | async-start | bytes 4096000 | tf_op jit(solution)/shard_map/reduce_scatter | solution.py:38
  168.5 16.8 %copy-start.9 = (bf16[5,128,5,64]{1,3,2,0:T(8,128)(2,1)}, bf16[5,128,5,64]{1,3,2,0:T(8,128)(2,1)S(1)}, u32[]{:S(2)}) copy-start(bf16[5,128,5,64]{1,3,2,0:T(8,128)(2,1)S(1)} %get-tuple-element.531) | copy-start | bytes 1228804
  168.5 17.7 %copy-start.4 = (bf16[5,128,5,64]{1,3,2,0:T(8,128)(2,1)}, bf16[5,128,5,64]{1,3,2,0:T(8,128)(2,1)S(1)}, u32[]{:S(2)}) copy-start(bf16[5,128,5,64]{1,3,2,0:T(8,128)(2,1)S(1)} %get-tuple-element.623) | copy-start | bytes 1228804
  168.5 14.0 %copy-start.33 = (bf16[400,800]{1,0:T(8,128)(2,1)S(1)}, bf16[400,800]{1,0:T(8,128)(2,1)}, u32[]{:S(2)}) copy-start(bf16[400,800]{1,0:T(8,128)(2,1)} %param.27) | copy-start | bytes 1920004
  185.3 76.8 %all-gather.17.cloned.1.call-start = ((), (), s32[]{:S(2)}) async-start(), calls=%async_computation.24 | async-start | bytes 2048000 | tf_op jit(solution)/shard_map/all_gather | solution.py:26
  185.9 109.7 %all-gather.13.cloned.1.call-start = ((), (), s32[]{:S(2)}) async-start(), calls=%async_computation.20 | async-start | bytes 2048000 | tf_op jit(solution)/shard_map/all_gather | solution.py:26
  234.8 35.9 %copy-start.19 = (f32[256,1]{0,1:T(1,128)}, f32[256,1]{0,1:T(1,128)S(1)}, u32[]{:S(2)}) copy-start(f32[256,1]{0,1:T(1,128)S(1)} %get-tuple-element.329) | copy-start | bytes 3076
  235.8 77.0 %reduce-scatter.27.cloned.1.call-start = ((), (), s32[]{:S(2)}) async-start(), calls=%async_computation.25 | async-start | bytes 9830400 | tf_op jit(solution)/shard_map/reduce_scatter | solution.py:30
  270.7 59.8 %reduce-scatter.23.cloned.1.call-start = ((), (), s32[]{:S(2)}) async-start(), calls=%async_computation.21 | async-start | bytes 9830400 | tf_op jit(solution)/shard_map/reduce_scatter | solution.py:30
  303.3 47.4 %all-gather.19.cloned.1.call-start = ((), (), s32[]{:S(2)}) async-start(), calls=%async_computation.26 | async-start | bytes 4915200 | tf_op jit(solution)/shard_map/all_gather | solution.py:34
  337.0 28.7 %all-gather.15.cloned.1.call-start = ((), (), s32[]{:S(2)}) async-start(), calls=%async_computation.22 | async-start | bytes 4915200 | tf_op jit(solution)/shard_map/all_gather | solution.py:34
  337.6 76.4 %reduce-scatter.29.cloned.1.call-start = ((), (), s32[]{:S(2)}) async-start(), calls=%async_computation.27 | async-start | bytes 4096000 | tf_op jit(solution)/shard_map/reduce_scatter | solution.py:38
  357.5 8.2 copy-start.29
  357.5 104.4 %reduce-scatter.25.cloned.1.call-start = ((), (), s32[]{:S(2)}) async-start(), calls=%async_computation.23 | async-start | bytes 4096000 | tf_op jit(solution)/shard_map/reduce_scatter | solution.py:38
  372.4 41.6 %copy-start.20 = (f32[256,1]{0,1:T(1,128)S(1)}, f32[256,1]{0,1:T(1,128)}, u32[]{:S(2)}) copy-start(f32[256,1]{0,1:T(1,128)} %copy-done.19) | copy-start | bytes 3076
  372.4 89.4 %copy-start.8 = (bf16[256,800]{0,1:T(8,128)(2,1)S(1)}, bf16[256,800]{0,1:T(8,128)(2,1)}, u32[]{:S(2)}) copy-start(bf16[256,800]{0,1:T(8,128)(2,1)} %param.35) | copy-start | bytes 1228804
  372.5 124.4 %all-gather.21.cloned.1.call-start = ((), (), s32[]{:S(2)}) async-start(), calls=%async_computation.28 | async-start | bytes 2048000 | tf_op jit(solution)/shard_map/all_gather | solution.py:26
  461.9 35.0 %copy-start.34 = (bf16[400,800]{1,0:T(8,128)(2,1)S(1)}, bf16[400,800]{1,0:T(8,128)(2,1)}, u32[]{:S(2)}) copy-start(bf16[400,800]{1,0:T(8,128)(2,1)} %param.27) | copy-start | bytes 1920004
  464.6 35.9 %copy-start.3 = (f32[256,800]{0,1:T(8,128)}, f32[256,800]{0,1:T(8,128)S(1)}, u32[]{:S(2)}) copy-start(f32[256,800]{0,1:T(8,128)S(1)} %get-tuple-element.319) | copy-start | bytes 2457604
  465.5 45.1 %reduce-scatter.31.cloned.1.call-start = ((), (), s32[]{:S(2)}) async-start(), calls=%async_computation.29 | async-start | bytes 2457600 | tf_op jit(solution)/shard_map/reduce_scatter | solution.py:30
  512.5 9.8 all-to-all-start.2
  516.0 138.5 %reduce-scatter.39.cloned.1.call-start = ((), (), s32[]{:S(2)}) async-start(), calls=%async_computation.34 | async-start | bytes 7372800
  574.8 16.1 %copy-start.6 = (f32[5,128,5,64]{1,3,2,0:T(8,128)}, f32[5,128,5,64]{1,3,2,0:T(8,128)S(1)}, u32[]{:S(2)}) copy-start(f32[5,128,5,64]{1,3,2,0:T(8,128)S(1)} %get-tuple-element.114) | copy-start | bytes 2457604
  590.8 100.5 %all-gather.23.cloned.1.call-start = ((), (), s32[]{:S(2)}) async-start(), calls=%async_computation.30 | async-start | bytes 3686400 | tf_op jit(solution)/shard_map/all_gather | solution.py:34
  674.0 1.9 copy-start.32
  675.2 66.7 %reduce-scatter.41.cloned.1.call-start = ((), (), s32[]{:S(2)}) async-start(), calls=%async_computation.35 | async-start | bytes 3328000
  682.3 1.6 copy-start.31
  682.4 131.8 %reduce-scatter.37.cloned.1.call-start = ((), (), s32[]{:S(2)}) async-start(), calls=%async_computation.33 | async-start | bytes 3584000 | tf_op jit(solution)/shard_map/reduce_scatter | solution.py:324
  691.2 1.4 copy-start.30
  691.2 168.1 %reduce-scatter.35.cloned.1.call-start = ((), (), s32[]{:S(2)}) async-start(), calls=%async_computation.32 | async-start | bytes 2560000 | tf_op jit(solution)/shard_map/reduce_scatter | solution.py:333
  698.1 209.6 %reduce-scatter.33.cloned.1.call-start = ((), (), s32[]{:S(2)}) async-start(), calls=%async_computation.31 | async-start | bytes 4096000 | tf_op jit(solution)/shard_map/reduce_scatter | solution.py:38
  704.4 39.8 %copy-start.11 = (bf16[1024,400]{0,1:T(8,128)(2,1)S(1)}, bf16[1024,400]{0,1:T(8,128)(2,1)}, u32[]{:S(2)}) copy-start(bf16[1024,400]{0,1:T(8,128)(2,1)} %copy-done.10) | copy-start | bytes 2457604
  704.4 337.1 %all-reduce.10.cloned.1.call-start = ((), (), s32[]{:S(2)}) async-start(), calls=%async_computation.36 | async-start | bytes 188416 | tf_op jit(solution)/shard_map/psum | solution.py:350
  706.6 40.0 %copy-start.12 = (f32[6400]{0:T(1024)}, f32[6400]{0:T(1024)S(1)}, u32[]{:S(2)}) copy-start(f32[6400]{0:T(1024)S(1)} %dynamic_update_slice.45) | copy-start | bytes 76804
  746.6 72.7 %copy-start.7 = (f32[5,128,5,64]{1,3,2,0:T(8,128)S(1)}, f32[5,128,5,64]{1,3,2,0:T(8,128)}, u32[]{:S(2)}) copy-start(f32[5,128,5,64]{1,3,2,0:T(8,128)} %copy-done.6) | copy-start | bytes 2457604
  781.0 36.7 %collective-permute-start = (bf16[36,800]{1,0:T(8,128)(2,1)S(1)}, bf16[36,800]{1,0:T(8,128)(2,1)S(1)}, u32[]{:S(2)}, u32[]{:S(2)}) collective-permute-start(bf16[36,800]{1,0:T(8,128)(2,1)S(1)} %slice.31), channel_id=1, source_target_pairs={{0,8},{8,16},{16,24},{1,9},{9,17},{17,25},{2,10},{10,18},{18,26},{... | collective-permute-start | bytes 172808
  816.5 91.1 %copy-start.2 = (bf16[256,800]{0,1:T(8,128)(2,1)S(1)}, bf16[256,800]{0,1:T(8,128)(2,1)}, u32[]{:S(2)}) copy-start(bf16[256,800]{0,1:T(8,128)(2,1)} %param.20) | copy-start | bytes 1228804
  816.7 92.5 %copy-start.14 = (f32[1600]{0:T(1024)}, f32[1600]{0:T(1024)S(1)}, u32[]{:S(2)}) copy-start(f32[1600]{0:T(1024)S(1)} %dynamic_update_slice.44) | copy-start | bytes 19204
  817.0 92.3 %copy-start.15 = (f32[1600]{0:T(1024)}, f32[1600]{0:T(1024)S(1)}, u32[]{:S(2)}) copy-start(f32[1600]{0:T(1024)S(1)} %dynamic_update_slice.43) | copy-start | bytes 19204
  817.3 92.0 %copy-start.16 = (f32[1600]{0:T(1024)}, f32[1600]{0:T(1024)S(1)}, u32[]{:S(2)}) copy-start(f32[1600]{0:T(1024)S(1)} %dynamic_update_slice.46) | copy-start | bytes 19204
  817.6 91.7 %copy-start.17 = (f32[1600]{0:T(1024)}, f32[1600]{0:T(1024)S(1)}, u32[]{:S(2)}) copy-start(f32[1600]{0:T(1024)S(1)} %dynamic_update_slice.42) | copy-start | bytes 19204
  859.3 193.9 %copy-start.1 = (bf16[800,1600]{1,0:T(8,128)(2,1)S(1)}, bf16[800,1600]{1,0:T(8,128)(2,1)}, u32[]{:S(2)}) copy-start(bf16[800,1600]{1,0:T(8,128)(2,1)} %param.31) | copy-start | bytes 7680004
  (10 other events, 7.2 us)
Sparse Core Ops, SparseCore 0:
  15.1 31.7 all-gather.8
  54.0 13.3 reduce-scatter.18
  90.1 48.5 all-gather.10
  185.4 43.6 reduce-scatter.20
  230.8 31.2 all-gather.16
  264.3 31.2 all-gather.12
  297.9 14.9 reduce-scatter.26
  315.1 15.3 reduce-scatter.22
  337.1 13.5 all-gather.18
  352.1 13.4 all-gather.14
  368.7 45.2 reduce-scatter.28
  416.9 44.9 reduce-scatter.24
  465.6 31.2 all-gather.20
  500.7 9.8 reduce-scatter.30
  590.9 63.5 reduce-scatter.38
  675.3 12.3 all-gather.22
  689.8 52.0 reduce-scatter.40
  744.0 70.1 reduce-scatter.36
  816.5 42.7 reduce-scatter.34
  862.2 45.4 reduce-scatter.32
  915.2 126.2 all-reduce.9
where the time goes:
time: 1070 us; the launch traced here: 1060 us
  waiting for transfers between devices  707 us (66%)
  matrix products  137 us (13%)
  blocking collectives  95.9 us (9%)
  other arithmetic  51.1 us (5%)
  local copies, waits for them, and re-layouts  47.6 us (4%)
  between operations  15.9 us (1%)
    reduce_scatter x4, waiting for transfers between devices, reduce_rows(): return lax.psum_scatter(partial_sum, 'row', scatter_dimension=0, tiled=True)  173 us
    psum x1, waiting for transfers between devices, shards(): lax.psum((col_place(first_gain_part), col_place(first_shift_part), query_...  125 us
    all_gather x4, waiting for transfers between devices, spread_rows(): return lax.all_gather(own_part, 'row', axis=0, tiled=True)  114 us
    unnamed x24, waiting for transfers between devices  100 us
    reduce_scatter x4, waiting for transfers between devices, reduce_cols(): return lax.psum_scatter(partial_sum, 'col', scatter_dimension=0, tiled=True)  49.1 us
    all_gather x1, waiting for transfers between devices, gather_keys(): return lax.all_gather(own_part, ('row', 'col'), axis=0, tiled=True)  47.5 us
    reduce_scatter x1, waiting for transfers between devices, shards(): lax.psum_scatter(triple_grad.astype(jnp.bfloat16), 'dp', scatter_dimensio...  38.2 us
    unnamed x1, blocking collectives  34.3 us
  transfers between devices with their start and end apart: 23, of which 21 were waited for; matrix products, arithmetic and copies ran while one was open for 11% of the time, Pallas kernels for 0%

commit v1 on v0

v1 whole, which is shorter than its diff:
```python
import functools

import jax
import jax.numpy as jnp
from jax import lax
from jax.experimental import pallas as pl
from jax.experimental.pallas import tpu as pltpu
from jax.sharding import PartitionSpec as P

HEADS = 25
HEAD_DIM = 64
EPS = 1e-05
NEG = -1e30
GRAIN = 16
AXES = ("dp", "row", "col")
MESH = pl.DeviceIdType.MESH
F32 = jnp.float32
BF16 = jnp.bfloat16
VMEM_BYTES = 60 * 1024 * 1024

NN = (((1,), (0,)), ((), ()))
NT = (((1,), (1,)), ((), ()))
TN = (((0,), (0,)), ((), ()))


def dot(left, right, dims):
    return lax.dot_general(left, right, dims, preferred_element_type=F32)


class Place:
    def __init__(self):
        self.d = lax.axis_index("dp")
        self.r = lax.axis_index("row")
        self.c = lax.axis_index("col")
        one = self.r + 1 - 2 * lax.rem(self.r, 2)
        two = lax.rem(self.r + 2, 4)
        self.a = 1 + self.c
        self.b = 2 - self.c
        self.ra = (1 - self.c) * one + self.c * two
        self.rb = self.c * one + (1 - self.c) * two
        self.r3 = 3 - self.r

    def dev(self, row, col=None):
        return (self.d, row, self.c if col is None else col)

    def mate(self):
        return (self.d, self.r, 1 - self.c)

    def barrier(self, devices):
        semaphore = pltpu.get_barrier_semaphore()
        for device in devices:
            pl.semaphore_signal(semaphore, inc=1, device_id=device, device_id_type=MESH)
        pl.semaphore_wait(semaphore, len(devices))

    def group(self):
        flat = 2 * self.r + self.c
        found = []
        for step in range(1, 8):
            other = lax.rem(flat + step, 8)
            found.append((self.d, other // 2, lax.rem(other, 2)))
        return found

    def square(self):
        return [self.mate(), self.dev(self.ra), self.dev(self.rb)]


def rcopy(src, dst, send, recv, device):
    return pltpu.make_async_remote_copy(
        src_ref=src, dst_ref=dst, send_sem=send, recv_sem=recv, device_id=device,
        device_id_type=MESH,
    )


def lanes(index, size):
    return pl.ds(pl.multiple_of(index * size, size), size)


def call(kernel, out_shapes, out_specs, in_specs, scratch, cid, flops=0, bytes_accessed=0):
    return pl.pallas_call(
        kernel,
        out_shape=out_shapes,
        in_specs=in_specs,
        out_specs=out_specs,
        scratch_shapes=scratch,
        compiler_params=pltpu.CompilerParams(
            collective_id=cid, has_side_effects=True, vmem_limit_bytes=VMEM_BYTES
        ),
    )


VM = pl.BlockSpec(memory_space=pltpu.VMEM)
ANY = pl.BlockSpec(memory_space=pl.ANY)
DMA = pltpu.SemaphoreType.DMA


def gather_scratch(rows, cols):
    return [pltpu.VMEM((2, 4, rows, cols), BF16), DMA((7,)), DMA((2, 4)), DMA((4,))]


def run_gather(place, x_ref, all_ref, got, send, recv, out_sem, work):
    mate = place.mate()
    to_mate = rcopy(x_ref, got.at[1, 0], send.at[0], recv.at[1, 0], mate)
    to_a = rcopy(x_ref, got.at[0, place.a], send.at[1], recv.at[0, place.a], place.dev(place.ra))
    to_b = rcopy(x_ref, got.at[0, place.b], send.at[2], recv.at[0, place.b], place.dev(place.rb))
    to_a.start()
    to_b.start()
    to_mate.start()
    got[0, 0] = x_ref[...]
    own_out = pltpu.make_async_copy(x_ref, all_ref.at[place.r], out_sem.at[0])
    own_out.start()

    def forward(slot, number):
        copy = rcopy(got.at[0, slot], got.at[1, slot], send.at[number], recv.at[1, slot], mate)
        copy.start()
        return copy

    def keep(slot, row, number):
        copy = pltpu.make_async_copy(got.at[0, slot], all_ref.at[row], out_sem.at[number])
        copy.start()
        return copy

    to_mate.wait_recv()
    work(0, place.r)
    to_a.wait_recv()
    relay = rcopy(
        got.at[0, place.a], got.at[0, 3], send.at[3], recv.at[0, 3], place.dev(place.rb)
    )
    relay.start()
    fwd_a = forward(place.a, 4)
    keep_a = keep(place.a, place.ra, 1)
    to_b.wait_recv()
    fwd_b = forward(place.b, 5)
    keep_b = keep(place.b, place.rb, 2)
    fwd_b.wait_recv()
    work(place.b, place.rb)
    fwd_a.wait_recv()
    work(place.a, place.ra)
    relay.wait_recv()
    fwd_3 = forward(3, 6)
    keep_3 = keep(3, place.r3, 3)
    fwd_3.wait_recv()
    work(3, place.r3)
    for copy in (to_mate, to_a, to_b, relay, fwd_a, fwd_b, fwd_3):
        copy.wait_send()
    for copy in (own_out, keep_a, keep_b, keep_3):
        copy.wait()


def gather_linear(x, w_own, w_oth, dims, transposed, out_dtype, cid):
    rows, cols = x.shape
    feats = w_own.shape[0] if dims == NT else w_own.shape[1]
    shape = (feats, 4 * rows) if transposed else (4, rows, feats)

    def kernel(x_ref, wo_ref, wn_ref, all_ref, y_ref, got, send, recv, out_sem):
        place = Place()
        place.barrier(place.square())

        def work(slot, row):
            if transposed:
                total = dot(wo_ref[...], got[0, slot], NT) + dot(wn_ref[...], got[1, slot], NT)
                y_ref[:, lanes(row, rows)] = total.astype(out_dtype)
            else:
                total = dot(got[0, slot], wo_ref[...], dims) + dot(got[1, slot], wn_ref[...], dims)
                y_ref[row] = total.astype(out_dtype)

        run_gather(place, x_ref, all_ref, got, send, recv, out_sem, work)

    return call(
        kernel,
        (jax.ShapeDtypeStruct((4, rows, cols), BF16), jax.ShapeDtypeStruct(shape, out_dtype)),
        (ANY, VM), [VM, VM, VM], gather_scratch(rows, cols), cid,
    )(x, w_own, w_oth)


def gather_triple(x, w_own, w_oth, bias, width, triple_width, cid):
    rows, cols = x.shape
    feats = w_own.shape[0]
    grains = feats // GRAIN
    shift = triple_width - feats
    per = 3 * HEAD_DIM

    def kernel(x_ref, wo_ref, wn_ref, b_ref, all_ref, h_ref, got, tt, send, recv, out_sem, gs, gr):
        place = Place()
        place.barrier(place.group())
        me = 2 * place.r + place.c

        def target(j):
            feature = triple_width * place.r + shift * place.c + GRAIN * j
            part = feature // width
            inner = feature - part * width
            head = inner // HEAD_DIM
            owner = jnp.minimum(head // 3, 7)
            row = (head - 3 * owner) * per + part * HEAD_DIM + (inner - head * HEAD_DIM)
            return owner, pl.ds(pl.multiple_of(row, GRAIN), GRAIN)

        def work(slot, row):
            total = dot(wo_ref[...], got[0, slot], NT) + dot(wn_ref[...], got[1, slot], NT)
            tt[:, lanes(row, rows)] = (total + b_ref[...]).astype(BF16)

            def send_grain(j, carry):
                owner, place_rows = target(j)
                src = tt.at[pl.ds(pl.multiple_of(GRAIN * j, GRAIN), GRAIN), lanes(row, rows)]
                dst = h_ref.at[place_rows, lanes(row, rows)]

                @pl.when(owner == me)
                def _():
                    pltpu.make_async_copy(src, dst, gr).start()

                @pl.when(owner != me)
                def _():
                    rcopy(src, dst, gs, gr, (place.d, owner // 2, lax.rem(owner, 2))).start()

                return carry

            lax.fori_loop(place.c, grains, send_grain, 0)

        run_gather(place, x_ref, all_ref, got, send, recv, out_sem, work)

        def sent(j, count):
            return count + jnp.where(target(j)[0] == me, 0, 1)

        def drain(j, carry):
            @pl.when(target(j)[0] != me)
            def _():
                src = tt.at[pl.ds(0, GRAIN)]
                pltpu.make_async_copy(src, src, gs).wait()

            return carry

        lax.fori_loop(place.c, grains, drain, 0)

        @pl.when(me == 7)
        def _():
            pltpu.make_async_copy(h_ref, h_ref, gr).wait()

        @pl.when(me != 7)
        def _():
            part = h_ref.at[pl.ds(0, 3 * per)]
            pltpu.make_async_copy(part, part, gr).wait()

    scratch = gather_scratch(rows, cols)
    scratch.insert(1, pltpu.VMEM((feats, 4 * rows), BF16))
    return call(
        kernel,
        (
            jax.ShapeDtypeStruct((4, rows, cols), BF16),
            jax.ShapeDtypeStruct((4 * per, 4 * rows), BF16),
        ),
        (ANY, ANY), [VM] * 4, scratch + [DMA, DMA], cid,
    )(x, w_own, w_oth, bias)


def gather_hidden(x, w_own, w_oth, bias, act_grad, cid):
    rows, cols = x.shape
    feats = w_own.shape[1]

    def kernel(
        x_ref, wo_ref, wn_ref, b_ref, g_ref, all_ref, act_ref, hid_ref, sum_ref,
        got, act, hid, send, recv, out_sem, swap_send, swap_recv, swap_out,
    ):
        place = Place()
        place.barrier(place.square())
        mate = place.mate()
        sum_ref[...] = jnp.zeros_like(sum_ref)
        pending = []

        def work(slot, row):
            number = len(pending)
            p = dot(got[0, slot], wo_ref[...], NN) + dot(got[1, slot], wn_ref[...], NN) + b_ref[...]
            square = p * p
            t = jnp.tanh(0.7978845608028654 * (p + 0.044715 * (square * p)))
            act[number] = (0.5 * p * (1.0 + t)).astype(BF16)
            slope = 0.5 * (1.0 + t) + 0.5 * p * (1.0 - t * t) * (
                0.7978845608028654 * (1.0 + 3.0 * 0.044715 * square)
            )
            grad = g_ref[row] * slope
            hid[number] = grad.astype(BF16)
            sum_ref[...] += jnp.sum(grad, axis=0, keepdims=True)
            copies = []
            for k, (buf, out) in enumerate(((act, act_ref), (hid, hid_ref))):
                there = out.at[place.c, row]
                out_copy = pltpu.make_async_copy(buf.at[number], there, swap_out.at[k, number])
                swap = rcopy(
                    buf.at[number], there, swap_send.at[k, number], swap_recv.at[k, number], mate
                )
                out_copy.start()
                swap.start()
                copies += [out_copy, swap]
            pending.append(copies)

        run_gather(place, x_ref, all_ref, got, send, recv, out_sem, work)
        for copies in pending:
            for copy in copies:
                copy.wait()

    full = jax.ShapeDtypeStruct((2, 4, rows, feats), BF16)
    return call(
        kernel,
        (
            jax.ShapeDtypeStruct((4, rows, cols), BF16), full, full,
            jax.ShapeDtypeStruct((1, feats), F32),
        ),
        (ANY, ANY, ANY, VM), [VM] * 5,
        [gather_scratch(rows, cols)[0], pltpu.VMEM((4, rows, feats), BF16),
         pltpu.VMEM((4, rows, feats), BF16)] + gather_scratch(rows, cols)[1:]
        + [DMA((2, 4)), DMA((2, 4)), DMA((2, 4))],
        cid,
    )(x, w_own, w_oth, bias, act_grad)


def scatter_scratch(rows, cols):
    return [
        pltpu.VMEM((3, rows, cols), BF16), pltpu.VMEM((3, rows, cols), BF16), DMA((3,)), DMA((3,))
    ]


def run_scatter(place, block, out_ref, outbox, inbox, send, recv):
    dev_a, dev_b = place.dev(place.ra), place.dev(place.rb)
    outbox[0] = block(place.r3).astype(BF16)
    first = rcopy(outbox.at[0], inbox.at[0], send.at[0], recv.at[0], dev_a)
    first.start()
    outbox[1] = block(place.ra).astype(BF16)
    second = rcopy(outbox.at[1], inbox.at[1], send.at[1], recv.at[1], dev_a)
    second.start()
    passed = block(place.rb)
    first.wait_recv()
    outbox[2] = (passed + inbox[0].astype(F32)).astype(BF16)
    third = rcopy(outbox.at[2], inbox.at[2], send.at[2], recv.at[2], dev_b)
    third.start()
    own = block(place.r)
    second.wait_recv()
    own = own + inbox[1].astype(F32)
    third.wait_recv()
    out_ref[...] = own + inbox[2].astype(F32)
    for copy in (first, second, third):
        copy.wait_send()


def pair_scatter(left, w_own, w_oth, dims, cid):
    rows = left.shape[2]
    cols = w_own.shape[0] if dims == NT else w_own.shape[1]

    def kernel(l_ref, wo_ref, wn_ref, out_ref, outbox, inbox, send, recv):
        place = Place()
        place.barrier([place.dev(place.ra), place.dev(place.rb)])

        def block(row):
            return dot(l_ref[place.c, row], wo_ref[...], dims) + dot(
                l_ref[1 - place.c, row], wn_ref[...], dims
            )

        run_scatter(place, block, out_ref, outbox, inbox, send, recv)

    return call(
        kernel, jax.ShapeDtypeStruct((rows, cols), F32), VM, [VM] * 3,
        scatter_scratch(rows, cols), cid,
    )(left, w_own, w_oth)


def attended_scatter(heads, weight, cid):
    feats, cols = weight.shape
    tokens = heads.shape[1]
    rows = tokens // 4

    def kernel(h_ref, w_ref, all_ref, out_ref, full, outbox, inbox, send, recv, gs, gr, keep):
        place = Place()
        place.barrier(place.group())
        me = 2 * place.r + place.c
        count = jnp.where(me == 7, 4, 3) * (HEAD_DIM // GRAIN)

        def send_grain(j, carry):
            feature = 3 * HEAD_DIM * me + GRAIN * j
            owner = feature // feats
            src = h_ref.at[pl.ds(pl.multiple_of(GRAIN * j, GRAIN), GRAIN)]
            dst = full.at[pl.ds(pl.multiple_of(feature - owner * feats, GRAIN), GRAIN)]
            rcopy(src, dst, gs, gr, (place.d, owner, 1 - place.c)).start()

            @pl.when(owner == place.r)
            def _():
                pltpu.make_async_copy(src, dst, gr).start()

            @pl.when(owner != place.r)
            def _():
                rcopy(src, dst, gs, gr, (place.d, owner, place.c)).start()

            return carry

        lax.fori_loop(0, count, send_grain, 0)

        def drain(j, carry):
            feature = 3 * HEAD_DIM * me + GRAIN * j
            src = h_ref.at[pl.ds(0, GRAIN)]
            pltpu.make_async_copy(src, src, gs).wait()

            @pl.when(feature // feats != place.r)
            def _():
                pltpu.make_async_copy(src, src, gs).wait()

            return carry

        lax.fori_loop(0, count, drain, 0)
        pltpu.make_async_copy(full, full, gr).wait()
        kept = pltpu.make_async_copy(full, all_ref, keep)
        kept.start()

        def block(row):
            return dot(full[:, lanes(row, rows)], w_ref[...], TN)

        run_scatter(place, block, out_ref, outbox, inbox, send, recv)
        kept.wait()

    return call(
        kernel,
        (jax.ShapeDtypeStruct((feats, tokens), BF16), jax.ShapeDtypeStruct((rows, cols), F32)),
        (ANY, VM), [VM, VM],
        [pltpu.VMEM((feats, tokens), BF16)] + scatter_scratch(rows, cols) + [DMA, DMA, DMA], cid,
    )(heads, weight)


def triple_scatter(heads, weight, width, cid):
    feats, cols = weight.shape
    tokens = heads.shape[1]
    rows = tokens // 4
    per = 3 * HEAD_DIM
    low = (feats // GRAIN + 1) // 2 * GRAIN

    def kernel(h_ref, w_ref, all_ref, out_ref, full, outbox, inbox, send, recv, gs, gr, ms, mr, keep):
        place = Place()
        place.barrier(place.group())
        me = 2 * place.r + place.c
        count = jnp.where(me == 7, 4, 3) * (per // GRAIN)

        def target(j):
            row = GRAIN * j
            head = row // per
            rest = row - head * per
            part = rest // HEAD_DIM
            feature = part * width + (3 * me + head) * HEAD_DIM + rest - part * HEAD_DIM
            owner = feature // feats
            inner = feature - owner * feats
            return 2 * owner + inner // low, inner

        def send_grain(j, carry):
            owner, inner = target(j)
            src = h_ref.at[pl.ds(pl.multiple_of(GRAIN * j, GRAIN), GRAIN)]
            dst = full.at[pl.ds(pl.multiple_of(inner, GRAIN), GRAIN)]

            @pl.when(owner == me)
            def _():
                pltpu.make_async_copy(src, dst, gr).start()

            @pl.when(owner != me)
            def _():
                rcopy(src, dst, gs, gr, (place.d, owner // 2, lax.rem(owner, 2))).start()

            return carry

        lax.fori_loop(0, count, send_grain, 0)

        def drain(j, carry):
            @pl.when(target(j)[0] != me)
            def _():
                src = h_ref.at[pl.ds(0, GRAIN)]
                pltpu.make_async_copy(src, src, gs).wait()

            return carry

        lax.fori_loop(0, count, drain, 0)
        lower, upper = full.at[pl.ds(0, low)], full.at[pl.ds(low, feats - low)]

        def swap(mine, theirs):
            pltpu.make_async_copy(mine, mine, gr).wait()
            copy = rcopy(mine, mine, ms, mr, place.mate())
            copy.start()
            copy.wait_send()
            pltpu.make_async_copy(theirs, theirs, mr).wait()

        @pl.when(place.c == 0)
        def _():
            swap(lower, upper)

        @pl.when(place.c == 1)
        def _():
            swap(upper, lower)

        kept = pltpu.make_async_copy(full, all_ref, keep)
        kept.start()

        def block(row):
            return dot(full[:, lanes(row, rows)], w_ref[...], TN)

        run_scatter(place, block, out_ref, outbox, inbox, send, recv)
        kept.wait()

    return call(
        kernel,
        (jax.ShapeDtypeStruct((feats, tokens), BF16), jax.ShapeDtypeStruct((rows, cols), F32)),
        (ANY, VM), [VM, VM],
        [pltpu.VMEM((feats, tokens), BF16)] + scatter_scratch(rows, cols)
        + [DMA, DMA, DMA, DMA, DMA], cid,
    )(heads, weight)


def attention_bias(seg_col, seg_row, bias_ref):
    tokens = seg_row.shape[1]
    key = lax.broadcasted_iota(jnp.int32, (tokens, tokens), 0)
    query = lax.broadcasted_iota(jnp.int32, (tokens, tokens), 1)
    allowed = (seg_col[...] == seg_row[...]) & (key <= query)
    bias_ref[...] = jnp.where(allowed, 0.0, NEG)


def holds(head):
    return (head < 3) | ((lax.axis_index("row") == 3) & (lax.axis_index("col") == 1))


def attention_forward(triple, seg_col, seg_row):
    per = 3 * HEAD_DIM
    tokens = triple.shape[1]
    span = tokens // 4

    def kernel(sc_ref, sr_ref, t_ref, o_ref, l_ref, bias_ref):
        @pl.when(pl.program_id(0) == 0)
        def _():
            attention_bias(sc_ref, sr_ref, bias_ref)

        @pl.when(holds(pl.program_id(0)))
        def _():
            for j in range(4):
                reach, here = (j + 1) * span, slice(j * span, (j + 1) * span)
                query = t_ref[0:HEAD_DIM, here] * BF16(HEAD_DIM ** (-0.5))
                score = dot(t_ref[HEAD_DIM : 2 * HEAD_DIM, 0:reach], query, TN)
                score = score + bias_ref[0:reach, here]
                top = jnp.max(score, axis=0, keepdims=True)
                weight = jnp.exp(score - top)
                total = jnp.sum(weight, axis=0, keepdims=True)
                mixed = dot(t_ref[2 * HEAD_DIM : per, 0:reach], weight.astype(BF16), NN)
                o_ref[:, here] = (mixed / total).astype(BF16)
                l_ref[0, :, here] = top + jnp.log(total)

    return pl.pallas_call(
        kernel,
        grid=(4,),
        out_shape=(
            jax.ShapeDtypeStruct((4 * HEAD_DIM, tokens), BF16),
            jax.ShapeDtypeStruct((4, 1, tokens), F32),
        ),
        in_specs=[
            pl.BlockSpec((tokens, 1), lambda h: (0, 0)),
            pl.BlockSpec((1, tokens), lambda h: (0, 0)),
            pl.BlockSpec((per, tokens), lambda h: (h, 0)),
        ],
        out_specs=(
            pl.BlockSpec((HEAD_DIM, tokens), lambda h: (h, 0)),
            pl.BlockSpec((1, 1, tokens), lambda h: (h, 0, 0)),
        ),
        scratch_shapes=[pltpu.VMEM((tokens, tokens), F32)],
        compiler_params=pltpu.CompilerParams(vmem_limit_bytes=VMEM_BYTES),
    )(seg_col, seg_row, triple)


def attention_backward(triple, seg_col, seg_row, attended, attended_grad, lse):
    per = 3 * HEAD_DIM
    tokens = triple.shape[1]
    span = tokens // 4

    def kernel(sc_ref, sr_ref, t_ref, o_ref, g_ref, l_ref, d_ref, bias_ref, kg_ref, vg_ref):
        @pl.when(pl.program_id(0) == 0)
        def _():
            attention_bias(sc_ref, sr_ref, bias_ref)

        @pl.when(holds(pl.program_id(0)))
        def _():
            kg_ref[...] = jnp.zeros_like(kg_ref)
            vg_ref[...] = jnp.zeros_like(vg_ref)
            for j in range(4):
                reach, here = (j + 1) * span, slice(j * span, (j + 1) * span)
                query = t_ref[0:HEAD_DIM, here] * BF16(HEAD_DIM ** (-0.5))
                key = t_ref[HEAD_DIM : 2 * HEAD_DIM, 0:reach]
                grad = g_ref[:, here]
                delta = jnp.sum(
                    grad.astype(F32) * o_ref[:, here].astype(F32), axis=0, keepdims=True
                )
                score = dot(key, query, TN) + bias_ref[0:reach, here]
                prob = jnp.exp(score - l_ref[0, :, here])
                vg_ref[:, 0:reach] += dot(grad, prob.astype(BF16), NT)
                back = dot(t_ref[2 * HEAD_DIM : per, 0:reach], grad, TN)
                mix = (prob * (back - delta)).astype(BF16)
                d_ref[0:HEAD_DIM, here] = (dot(key, mix, NN) * HEAD_DIM ** (-0.5)).astype(BF16)
                kg_ref[:, 0:reach] += dot(query, mix, NT)
            d_ref[HEAD_DIM : 2 * HEAD_DIM, :] = kg_ref[...].astype(BF16)
            d_ref[2 * HEAD_DIM : per, :] = vg_ref[...].astype(BF16)

    return pl.pallas_call(
        kernel,
        grid=(4,),
        out_shape=jax.ShapeDtypeStruct((4 * per, tokens), BF16),
        in_specs=[
            pl.BlockSpec((tokens, 1), lambda h: (0, 0)),
            pl.BlockSpec((1, tokens), lambda h: (0, 0)),
            pl.BlockSpec((per, tokens), lambda h: (h, 0)),
            pl.BlockSpec((HEAD_DIM, tokens), lambda h: (h, 0)),
            pl.BlockSpec((HEAD_DIM, tokens), lambda h: (h, 0)),
            pl.BlockSpec((1, 1, tokens), lambda h: (h, 0, 0)),
        ],
        out_specs=pl.BlockSpec((per, tokens), lambda h: (h, 0)),
        scratch_shapes=[
            pltpu.VMEM((tokens, tokens), F32),
            pltpu.VMEM((HEAD_DIM, tokens), F32),
            pltpu.VMEM((HEAD_DIM, tokens), F32),
        ],
        compiler_params=pltpu.CompilerParams(vmem_limit_bytes=VMEM_BYTES),
    )(seg_col, seg_row, triple, attended, attended_grad, lse)


def sum_all(pieces, sizes, cid):
    count = pieces.shape[0]
    rows, cols = sizes

    def kernel(x_ref, out_ref, inbox, piece, sems):
        me = (lax.axis_index("dp") * rows + lax.axis_index("row")) * cols + lax.axis_index("col")

        def dev(step):
            flat = lax.rem(me + step, count)
            return flat, (flat // (rows * cols), lax.rem(flat // cols, rows), lax.rem(flat, cols))

        semaphore = pltpu.get_barrier_semaphore()

        def greet(step, carry):
            pl.semaphore_signal(semaphore, inc=1, device_id=dev(step)[1], device_id_type=MESH)
            return carry

        lax.fori_loop(1, count, greet, 0)
        pl.semaphore_wait(semaphore, count - 1)

        def spread(step, carry):
            flat, device = dev(step)
            rcopy(x_ref.at[flat], inbox.at[me], sems.at[0], sems.at[1], device).start()
            return carry

        lax.fori_loop(1, count, spread, 0)
        inbox[me] = x_ref[me]
        rest = inbox.at[pl.ds(0, count - 1)]
        pltpu.make_async_copy(rest, rest, sems.at[1]).wait()
        pltpu.make_async_copy(rest, rest, sems.at[0]).wait()
        piece[...] = jnp.sum(inbox[...], axis=0)

        def share(step, carry):
            rcopy(piece, out_ref.at[me], sems.at[2], sems.at[3], dev(step)[1]).start()
            return carry

        lax.fori_loop(1, count, share, 0)
        out_ref[me] = piece[...]
        rest = out_ref.at[pl.ds(0, count - 1)]
        pltpu.make_async_copy(rest, rest, sems.at[3]).wait()
        pltpu.make_async_copy(rest, rest, sems.at[2]).wait()

    return call(
        kernel, jax.ShapeDtypeStruct(pieces.shape, F32), VM, [VM],
        [pltpu.VMEM(pieces.shape, F32), pltpu.VMEM(pieces.shape[1:], F32), DMA((4,))], cid,
    )(pieces)


def feature_totals(first_term, second_term):
    return lax.psum(
        (jnp.sum(first_term, axis=1, keepdims=True), jnp.sum(second_term, axis=1, keepdims=True)),
        "col",
    )


def norm_local(matrix, gain, shift):
    width = HEADS * HEAD_DIM
    total, square = feature_totals(matrix, matrix * matrix)
    average = total / width
    rstd = lax.rsqrt(square / width - average * average + EPS)
    normed_hat = (matrix - average) * rstd
    return (normed_hat * gain + shift, normed_hat, rstd)


def norm_back(grad_in, normed_hat, rstd, gain):
    width = HEADS * HEAD_DIM
    scaled = grad_in * gain
    total, mixed = feature_totals(scaled, scaled * normed_hat)
    return rstd * (scaled - total / width - normed_hat * mixed / width)


def swap(block):
    return lax.ppermute(block, "col", [(0, 1), (1, 0)])


def shards(
    tokens, segment_ids, first_gain, first_shift, triple_weight, query_bias, value_bias,
    proj_weight, proj_bias, second_gain, second_shift, expand_weight, expand_bias,
    shrink_weight, shrink_bias, cotangent, *, axis_sizes,
):
    width = HEADS * HEAD_DIM
    dp_count, row_count, col_count = axis_sizes
    row, col = lax.axis_index("row"), lax.axis_index("col")
    rows, col_width = tokens.shape
    triple_width = triple_weight.shape[1]
    proj_rows = proj_weight.shape[0]
    hidden = expand_weight.shape[1] // 2

    def col_slice(vector):
        return lax.dynamic_slice_in_dim(vector, col * col_width, col_width)

    def halves(matrix, size, axis):
        step = matrix.shape[axis] - size
        return (
            lax.dynamic_slice_in_dim(matrix, col * step, size, axis),
            lax.dynamic_slice_in_dim(matrix, (1 - col) * step, size, axis),
        )

    triple_t = triple_weight.T
    core_feats = (triple_width // GRAIN + 1) // 2 * GRAIN
    triple_own, triple_theirs = halves(triple_t, core_feats, 0)
    triple_oth = swap(triple_theirs)
    expand_own, expand_theirs = halves(expand_weight, hidden, 1)
    expand_oth = swap(expand_theirs)
    shrink_own, shrink_theirs = halves(shrink_weight, hidden, 0)
    shrink_oth = swap(shrink_theirs)
    head_rows = 3 * HEAD_DIM
    lag = (row_count - 1) * (proj_rows - 2 * head_rows)
    before = lax.ppermute(
        proj_weight[proj_rows - lag :], "row", [(i, i + 1) for i in range(row_count - 1)]
    )
    padded = jnp.concatenate(
        [before, proj_weight, jnp.zeros((2 * HEAD_DIM, col_width), BF16)], axis=0
    )
    start = lag - (proj_rows - 2 * head_rows) * row
    proj_own = lax.dynamic_slice_in_dim(padded, start + head_rows * col, 4 * HEAD_DIM, 0)
    proj_theirs = lax.dynamic_slice_in_dim(
        padded, start + head_rows * (1 - col), 4 * HEAD_DIM, 0
    )
    proj_oth = swap(proj_theirs)
    full_bias = jnp.concatenate([query_bias, jnp.zeros((width,), F32), value_bias])
    core_bias = lax.dynamic_slice_in_dim(
        full_bias, row * triple_width + col * (triple_width - core_feats), core_feats
    )[:, None]
    core_expand_bias = lax.dynamic_slice_in_dim(
        expand_bias, (row * 2 + col) * hidden, hidden
    )[None, :]
    seg_row = segment_ids
    seg_col = segment_ids.reshape(-1, 1)

    tokens_wide = tokens.astype(F32)
    first_normed, first_hat, first_rstd = norm_local(
        tokens_wide, col_slice(first_gain), col_slice(first_shift)
    )
    first_all, triple = gather_triple(
        first_normed.astype(BF16), triple_own, triple_oth, core_bias, width, triple_width, 0
    )
    cot_all, act_grad = gather_linear(cotangent, shrink_own, shrink_oth, NT, False, F32, 1)
    attended, lse = attention_forward(triple, seg_col, seg_row)
    attended_all, proj_out = attended_scatter(attended, proj_weight, 2)
    middle = tokens_wide + proj_out + col_slice(proj_bias)
    second_normed, second_hat, second_rstd = norm_local(
        middle, col_slice(second_gain), col_slice(second_shift)
    )
    second_all, act_all, hid_all, expand_bias_part = gather_hidden(
        second_normed.astype(BF16), expand_own, expand_oth, core_expand_bias, act_grad, 3
    )

    second_normed_grad = pair_scatter(hid_all, expand_own, expand_theirs, NT, 4)
    cot_wide = cotangent.astype(F32)
    middle_grad = cot_wide + norm_back(
        second_normed_grad, second_hat, second_rstd, col_slice(second_gain)
    )
    middle_all, attended_grad = gather_linear(
        middle_grad.astype(BF16), proj_own, proj_oth, NT, True, BF16, 5
    )
    triple_head_grad = attention_backward(
        triple, seg_col, seg_row, attended, attended_grad, lse
    )
    triple_all, first_normed_grad = triple_scatter(triple_head_grad, triple_t, width, 6)
    input_grad = middle_grad + norm_back(
        first_normed_grad, first_hat, first_rstd, col_slice(first_gain)
    )
    shrink_out = pair_scatter(act_all, shrink_own, shrink_theirs, NN, 7)
    block_out = (middle + shrink_out + col_slice(shrink_bias)).astype(BF16)

    def owned(grad, axis):
        return lax.psum_scatter(
            grad.astype(BF16), "dp", scatter_dimension=axis, tiled=True
        ).astype(F32)

    def flat(blocks):
        return blocks.reshape(-1, blocks.shape[-1])

    cot_flat, second_flat = flat(cot_all), flat(second_all)
    act_flat = act_all.reshape(2, -1, hidden)
    hid_flat = hid_all.reshape(2, -1, hidden)
    shrink_grad = jnp.einsum("ctf,td->cfd", act_flat, cot_flat, preferred_element_type=F32)
    shrink_owned = owned(shrink_grad.reshape(2 * hidden, col_width), 0)
    expand_grad = jnp.concatenate(
        [
            jnp.einsum("td,tf->df", second_flat, hid_flat[c], preferred_element_type=F32)
            for c in range(2)
        ],
        axis=1,
    )
    expand_owned = owned(expand_grad, 0)
    proj_grad = jnp.einsum("kt,td->kd", attended_all, flat(middle_all), preferred_element_type=F32)
    proj_owned = owned(proj_grad, 0)
    triple_grad = jnp.einsum(
        "td,kt->dk", flat(first_all), triple_all, preferred_element_type=F32
    )
    triple_owned = owned(triple_grad, 0)

    by_col = jnp.stack(
        [
            jnp.sum(first_normed_grad * first_hat, axis=0),
            jnp.sum(first_normed_grad, axis=0),
            jnp.sum(middle_grad, axis=0),
            jnp.sum(second_normed_grad * second_hat, axis=0),
            jnp.sum(second_normed_grad, axis=0),
            jnp.sum(cot_wide, axis=0),
        ]
    )
    is_col = (jnp.arange(2) == col).astype(F32)
    by_col = by_col[:, None, :] * is_col[None, :, None]
    is_core = (jnp.arange(2 * row_count) == 2 * row + col).astype(F32)
    by_core = expand_bias_part * is_core[:, None]
    triple_sum = jnp.sum(triple_all.astype(F32), axis=1)
    is_row = ((jnp.arange(row_count) == row) & (col == 0)).astype(F32)
    by_row = triple_sum[None, :] * is_row[:, None]
    vector = jnp.concatenate([by_col.reshape(-1), by_core.reshape(-1), by_row.reshape(-1)])
    devices = dp_count * row_count * col_count
    tile = 8 * 128
    size = -(-vector.shape[0] // (devices * tile)) * tile
    vector = jnp.pad(vector, (0, devices * size - vector.shape[0]))
    total = sum_all(
        vector.reshape(devices, size // 128, 128), (row_count, col_count), 8
    ).reshape(-1)
    col_totals = total[: 6 * width].reshape(6, width)
    expand_bias_grad = total[6 * width : 6 * width + 2 * row_count * hidden]
    rest = total[6 * width + 2 * row_count * hidden :]
    return (
        block_out,
        input_grad,
        col_totals[0],
        col_totals[1],
        triple_owned[None],
        rest[:width],
        rest[2 * width : 3 * width],
        proj_owned[None],
        col_totals[2],
        col_totals[3],
        col_totals[4],
        expand_owned[None],
        expand_bias_grad,
        shrink_owned[None],
        col_totals[5],
    )


def solution(mesh):
    assert mesh.shape["row"] == 4 and mesh.shape["col"] == 2
    sizes = tuple(mesh.shape[name] for name in AXES)
    tok, mat, mat_t = P(("dp", "row"), "col"), P("row", "col"), P("col", "row")
    in_specs = (
        tok, P("dp", None), P(), P(), mat_t, P(), P(), mat, P(), P(), P(), mat_t, P(), mat, P(), tok,
    )
    grad, grad_t = P("row", "dp", "col"), P("col", "dp", "row")
    out_specs = (
        tok, tok, P(), P(), grad_t, P(), P(), grad, P(), P(), P(), grad_t, P(), grad, P(),
    )
    return jax.shard_map(
        functools.partial(shards, axis_sizes=sizes),
        mesh=mesh, in_specs=in_specs, out_specs=out_specs, check_vma=False,
    )
```

time: 1070 us -> 508 us (0.47)
  waiting for transfers between devices: 707 us -> 71.5 us
  Pallas kernels: 0 us -> 266 us
  matrix products: 137 us -> 19.1 us
  blocking collectives: 95.9 us -> 45.6 us
  other arithmetic: 51.1 us -> 23.1 us
    pallas_call x0 -> x11, Pallas kernels: none -> 266 us  [the longest x2 50.9 us: gather_linear(): call(kernel, (jax.ShapeDtypeStruct((4, rows, cols), BF16), jax.ShapeDtype...]
    reduce_scatter x10 -> x2, waiting for transfers between devices: 292 us -> 55.5 us  [owned(): lax.psum_scatter(grad.astype(BF16), 'dp', scatter_dimension=axis, tiled=T...]
    all_gather x8 -> x0, waiting for transfers between devices: 183 us -> none  [the longest x4 114 us: spread_rows(): return lax.all_gather(own_part, 'row', axis=0, tiled=True)]
    psum x1 -> x0, waiting for transfers between devices: 125 us -> none  [shards(): lax.psum((col_place(first_gain_part), col_place(first_shift_part), query_...]
    dot_general x47 -> x5, matrix products: 137 us -> 19.1 us  [the longest x1 6.82 us: shards(): jnp.einsum('ctf,td->cfd', act_flat, cot_flat, preferred_element_type=F32)]
    unnamed x24 -> x5, waiting for transfers between devices: 100 us -> 16 us
    all_to_all x3 -> x0, blocking collectives: 45.7 us -> none  [the longest x2 27.1 us: to_hidden(): lax.all_to_all(headed, 'row', split_axis=1, concat_axis=0, tiled=True)]
    reduce_sum x16 -> x4, other arithmetic: 21.7 us -> 6.73 us  [the longest x1 2.46 us: shards(): jnp.sum(middle_grad, axis=0)]
  transfers between devices with their start and end apart: 23 -> 9, of which waited for: 21 -> 2; matrix products, arithmetic and copies ran while one was open for 11% -> 22% of each run, Pallas kernels for 0% -> 38%
where the time goes in v1:
time: 508 us; the launch traced here: 498 us
  Pallas kernels  266 us (52%)
  waiting for transfers between devices  71.5 us (14%)
  local copies, waits for them, and re-layouts  51.3 us (10%)
  blocking collectives  45.6 us (9%)
  other arithmetic  23.1 us (5%)
  matrix products  19.1 us (4%)
  between operations  15.1 us (3%)
  starting transfers between devices  6.3 us (1%)
    reduce_scatter x2, waiting for transfers between devices, owned(): lax.psum_scatter(grad.astype(BF16), 'dp', scatter_dimension=axis, tiled=T...  55.5 us
    pallas_call x2, Pallas kernels, gather_linear(): call(kernel, (jax.ShapeDtypeStruct((4, rows, cols), BF16), jax.ShapeDtype...  50.9 us
    pallas_call x2, Pallas kernels, pair_scatter(): call(kernel, jax.ShapeDtypeStruct((rows, cols), F32), VM, [VM] * 3, scatt...  46.3 us
    pallas_call x1, Pallas kernels, triple_scatter(): call(kernel, (jax.ShapeDtypeStruct((feats, tokens), BF16), jax.ShapeDtype...  38.4 us
    pallas_call x1, Pallas kernels, gather_triple(): call(kernel, (jax.ShapeDtypeStruct((4, rows, cols), BF16), jax.ShapeDtype...  33.1 us
    pallas_call x1, Pallas kernels, gather_hidden(): call(kernel, (jax.ShapeDtypeStruct((4, rows, cols), BF16), full, full, ja...  30.1 us
    unnamed x1, blocking collectives  29.1 us
    pallas_call x1, Pallas kernels, attended_scatter(): call(kernel, (jax.ShapeDtypeStruct((feats, tokens), BF16), jax.ShapeDtype...  26.5 us
  transfers between devices with their start and end apart: 9, of which 2 were waited for; matrix products, arithmetic and copies ran while one was open for 22% of the time, Pallas kernels for 38%

profile of v1, /device:TPU:25, one launch (start us, length us, event | category | flops | bytes accessed | tf_op | source)
XLA Modules:
  0.0 498.2 jit_solution(18409303939150520129)
XLA Ops:
  7.2 2.7 dynamic-slice_bitcast_fusion.1
  10.6 5.1 %constant_dynamic-slice_fusion.4 = (bf16[800,800]{1,0:T(8,128)(2,1)}, bf16[800,800]{1,0:T(8,128)(2,1)}) fusion(bf16[800,1600]{1,0:T(8,128)(2,1)} %param.27, s32[]{:T(128)S(6)} %select_n.38, s32[]{:T(128)S(6)} %select_n.16), kind=kLoop, calls=%fused_computation.55 | loop fusion | bytes 5120008 | tf_op jit(solution)/shard_map/dynamic_slice | solution.py:710
  15.7 2.6 constant_dynamic-slice_fusion.2
  18.4 2.3 copy.73.wn_ref
  21.2 3.3 collective-permute-start.3
  24.5 3.3 copy.58
  27.9 1.4 copy.61.sc_ref
  29.3 1.2 copy.57
  36.2 2.0 copy.64.x_ref
  38.2 3.4 copy.72.wo_ref
  41.7 2.9 all-reduce.7
  48.4 2.4 copy.59.wn_ref
  50.8 33.1 %shard_map.271 = (bf16[4,256,800]{2,1,0:T(8,128)(2,1)}, bf16[768,1024]{1,0:T(8,128)(2,1)}) custom-call(bf16[256,800]{1,0:T(8,128)(2,1)} %fusion.7.x_ref, bf16[608,800]{1,0:T(8,128)(2,1)} %dynamic-slice_bitcast_fusion.wo_ref, bf16[608,800]{1,0:T(8,128)(2,1)} %copy.59.wn_ref, f32[608,1]{1,0:T(8,128)} %broadcast_in_dim.97.b_ref), custom_call_target="tpu_custom_call" | custom-call | tf_op jit(solution)/shard_map/pallas_call | solution.py:243
  83.9 8.3 %shard_map.272 = (bf16[256,1024]{1,0:T(8,128)(2,1)}, f32[4,1,1024]{2,1,0:T(1,128)}) custom-call(s32[1024,1]{1,0:T(8,128)} %copy.61.sc_ref, s32[1,1024]{1,0:T(1,128)} %sr_ref.3, bf16[768,1024]{1,0:T(8,128)(2,1)} %get-tuple-element.31.t_ref), custom_call_target="tpu_custom_call" | custom-call | tf_op jit(solution)/shard_map/pallas_call | solution.py:540
  92.2 26.5 %shard_map.273 = (bf16[400,1024]{1,0:T(8,128)(2,1)}, f32[256,800]{1,0:T(8,128)}) custom-call(bf16[256,1024]{1,0:T(8,128)(2,1)} %get-tuple-element.32.h_ref.o_ref, bf16[400,800]{1,0:T(8,128)(2,1)} %w_ref.1), custom_call_target="tpu_custom_call" | custom-call | tf_op jit(solution)/shard_map/pallas_call | solution.py:412
  118.7 1.4 fusion.18
  120.1 3.8 all-reduce.6
  125.0 25.7 %shard_map.274 = (bf16[4,256,800]{2,1,0:T(8,128)(2,1)}, f32[4,256,800]{2,1,0:T(8,128)}) custom-call(bf16[256,800]{1,0:T(8,128)(2,1)} %copy.64.x_ref, bf16[800,800]{1,0:T(8,128)(2,1)} %copy.72.wo_ref, bf16[800,800]{1,0:T(8,128)(2,1)} %collective-permute-done.2.wn_ref), custom_call_target="tpu_custom_call" | custom-call | tf_op jit(solution)/shard_map/pallas_call | solution.py:168
  150.7 30.1 %shard_map.275 = (bf16[4,256,800]{2,1,0:T(8,128)(2,1)}, bf16[2,4,256,800]{3,2,1,0:T(8,128)(2,1)}, bf16[2,4,256,800]{3,2,1,0:T(8,128)(2,1)}, f32[1,800]{1,0:T(1,128)}) custom-call(bf16[256,800]{1,0:T(8,128)(2,1)} %add_convert_fusion.1.x_ref, bf16[800,800]{1,0:T(8,128)(2,1)} %get-tuple-element.120.wo_ref, bf16[800,800]{1,0:T(8,128)(2,1)} %collective-permute-done.1.wn_ref, ...), custom_call_target="tpu_custom_call" | custom-call | tf_op jit(solution)/shard_map/pallas_call | solution.py:297
  180.8 23.2 %shard_map.277 = f32[256,800]{1,0:T(8,128)} custom-call(bf16[2,4,256,800]{3,2,1,0:T(8,128)(2,1)} %get-tuple-element.36.l_ref, bf16[800,800]{1,0:T(8,128)(2,1)} %get-tuple-element.120.wo_ref, bf16[800,800]{1,0:T(8,128)(2,1)} %get-tuple-element.119.wn_ref), custom_call_target="tpu_custom_call" | custom-call | tf_op jit(solution)/shard_map/pallas_call | solution.py:354
  204.0 1.7 multiply_reduce_fusion
  205.7 2.5 all-reduce.5
  208.2 23.1 %shard_map.276 = f32[256,800]{1,0:T(8,128)} custom-call(bf16[2,4,256,800]{3,2,1,0:T(8,128)(2,1)} %get-tuple-element.35.l_ref, bf16[800,800]{1,0:T(8,128)(2,1)} %copy.72.wo_ref, bf16[800,800]{1,0:T(8,128)(2,1)} %copy.73.wn_ref), custom_call_target="tpu_custom_call" | custom-call | tf_op jit(solution)/shard_map/pallas_call | solution.py:354
  231.3 2.5 fusion.19
  234.6 25.2 %shard_map.278 = (bf16[4,256,800]{2,1,0:T(8,128)(2,1)}, bf16[256,1024]{1,0:T(8,128)(2,1)}) custom-call(bf16[256,800]{1,0:T(8,128)(2,1)} %convert_element_type.63.x_ref, bf16[256,800]{1,0:T(8,128)(2,1)} %get-tuple-element.122.wo_ref, bf16[256,800]{1,0:T(8,128)(2,1)} %collective-permute-done.4.wn_ref), custom_call_target="tpu_custom_call" | custom-call | tf_op jit(solution)/shard_map/pallas_call | solution.py:168
  259.8 11.7 %shard_map.279.h_ref = bf16[768,1024]{1,0:T(8,128)(2,1)} custom-call(s32[1024,1]{1,0:T(8,128)} %copy.61.sc_ref, s32[1,1024]{1,0:T(1,128)} %sr_ref.3, bf16[768,1024]{1,0:T(8,128)(2,1)} %get-tuple-element.31.t_ref, bf16[256,1024]{1,0:T(8,128)(2,1)} %get-tuple-element.32.h_ref.o_ref, bf16[256,1024]{1,0:T(8,128)(2,1)} %get-tuple-element.37.g_ref, ...), custom_call_target="tpu_custom_call" | custom-call | tf_op jit(solution)/shard_map/pallas_call | solution.py:593
  271.5 38.4 %shard_map.280 = (bf16[1200,1024]{1,0:T(8,128)(2,1)}, f32[256,800]{1,0:T(8,128)}) custom-call(bf16[768,1024]{1,0:T(8,128)(2,1)} %shard_map.279.h_ref, bf16[1200,800]{1,0:T(8,128)(2,1)} %bitcast.59), custom_call_target="tpu_custom_call" | custom-call | tf_op jit(solution)/shard_map/pallas_call | solution.py:495
  309.9 5.7 %convolution_convert_fusion.1 = bf16[800,1200]{1,0:T(8,128)(2,1)} fusion(bf16[1024,800]{1,0:T(8,128)(2,1)S(1)} %bitcast.88, bf16[1200,1024]{1,0:T(8,128)(2,1)} %get-tuple-element.41), kind=kOutput, calls=%fused_computation.2 | convolution fusion | flops 1967040000 | bytes 6016000 | tf_op jit(solution)/shard_map/td,kt->dk/dot_general | solution.py:804
  315.8 2.5 fusion.21
  318.3 1.9 convolution_convert_fusion.2
  320.2 1.9 convolution_convert_fusion.3
  322.1 2.4 pad_maximum_fusion
  324.6 6.1 %copy.68 = bf16[2,1024,800]{1,2,0:T(8,128)(2,1)} copy(bf16[2,1024,800]{2,1,0:T(8,128)(2,1)} %bitcast.58) | data formatting | bytes 6553600 | tf_op jit(solution)/shard_map/reshape | solution.py:790
  330.6 6.8 %convolution_convert_fusion = bf16[1600,800]{1,0:T(8,128)(2,1)} fusion(bf16[1600,1024]{1,0:T(8,128)(2,1)} %bitcast.60, bf16[1024,800]{1,0:T(8,128)(2,1)S(1)} %bitcast.87), kind=kOutput, calls=%fused_computation.1 | convolution fusion | flops 2622720000 | bytes 7475200 | tf_op jit(solution)/shard_map/ctf,td->cfd/dot_general | solution.py:792
  339.4 2.1 convert_reduce_fusion
  343.4 20.8 %shard_map.281 = f32[32,8,128]{2,1,0:T(8,128)} custom-call(f32[32,8,128]{2,1,0:T(8,128)} %fusion.17.x_ref), custom_call_target="tpu_custom_call" | custom-call | tf_op jit(solution)/shard_map/pallas_call | solution.py:657
  364.2 2.8 convolution_convert_fusion.4
  367.0 29.1 %fusion = bf16[112,800]{1,0:T(8,128)(2,1)S(1)} fusion(bf16[400,800]{1,0:T(8,128)(2,1)S(1)} %convolution_convert_fusion.4), kind=kCustom, calls=%all-reduce-scatter | all-reduce-scatter fusion | flops 358401 | bytes 819712
  396.8 1.3 collective-permute-start.5
  398.1 7.3 %all-reduce.4 = (f32[256]{0:T(256)}, f32[256,1]{0,1:T(1,128)S(1)}) all-reduce(f32[256]{0:T(256)S(1)} %get-tuple-element.95, f32[256,1]{0,1:T(1,128)S(1)} %bitcast.84), channel_id=1, replica_groups=mesh['dp'=4,'row'=4,'col'=2] {'col'}, use_global_device_ids=true, to_apply=%region_15.0 | all-reduce | flops 512 | bytes 4096 | tf_op jit(solution)/shard_map/psum | solution.py:664
  407.7 1.9 copy.69
  409.7 1.2 copy.70
  410.8 1.4 concatenate.17
  413.4 2.1 bitcast_convert_fusion.2
  415.5 16.0 %reduce-scatter.12.cloned.1.call-done = bf16[200,1600]{1,0:T(8,128)(2,1)} async-done(((bf16[800,1600]{1,0:T(8,128)(2,1)}), bf16[200,1600]{1,0:T(8,128)(2,1)}) %reduce-scatter.12.cloned.1.call-update) | async-done | bytes 640016
  431.5 2.2 bitcast_convert_fusion.1
  433.7 55.5 %reduce-scatter.10.cloned.1.call-done = bf16[400,800]{1,0:T(8,128)(2,1)} async-done(((bf16[1600,800]{1,0:T(8,128)(2,1)}), bf16[400,800]{1,0:T(8,128)(2,1)}) %reduce-scatter.10.cloned.1.call-update) | async-done | bytes 640016 | tf_op jit(solution)/shard_map/reduce_scatter | solution.py:782
  489.2 2.3 bitcast_convert_fusion
  (109 shorter events, 20.1 us)
Async XLA Ops:
  7.2 406.2 %reduce-scatter.8.cloned.1.call-start = ((), (), s32[]{:S(2)}) async-start(), calls=%async_computation.3 | async-start | bytes 2560000 | tf_op jit(solution)/shard_map/reduce_scatter | solution.py:782
  9.9 38.5 %collective-permute-start = (bf16[608,800]{0,1:T(8,128)(2,1)}, bf16[608,800]{0,1:T(8,128)(2,1)}, u32[]{:S(2)}, u32[]{:S(2)}) collective-permute-start(bf16[608,800]{0,1:T(8,128)(2,1)} %dynamic-slice_bitcast_fusion.1), channel_id=1, source_target_pairs={{0,1},{1,0},{2,3},{3,2},{4,5},{5,4},{6,7},{7,6},{8,9},{9,8},{10,11... | collective-permute-start | bytes 2918408 | tf_op jit(solution)/shard_map/ppermute | solution.py:687
  10.6 5.1 %copy-start.5 = (bf16[1600,800]{0,1:T(8,128)(2,1)S(1)}, bf16[1600,800]{0,1:T(8,128)(2,1)}, u32[]{:S(2)}) copy-start(bf16[1600,800]{0,1:T(8,128)(2,1)} %param.29) | copy-start | bytes 7680004
  15.7 135.0 %collective-permute-start.1 = (bf16[800,800]{1,0:T(8,128)(2,1)}, bf16[800,800]{1,0:T(8,128)(2,1)}, u32[]{:S(2)}, u32[]{:S(2)}) collective-permute-start(bf16[800,800]{1,0:T(8,128)(2,1)} %get-tuple-element.119.wn_ref), channel_id=1, source_target_pairs={{0,1},{1,0},{2,3},{3,2},{4,5},{5,4},{6,7},{7,6},{8,9},{9,8},{10,11... | collective-permute-start | bytes 3840008 | tf_op jit(solution)/shard_map/ppermute | solution.py:687
  18.4 2.8 copy-start.4
  20.7 104.3 %collective-permute-start.2 = (bf16[800,800]{1,0:T(8,128)(2,1)}, bf16[800,800]{1,0:T(8,128)(2,1)}, u32[]{:S(2)}, u32[]{:S(2)}) collective-permute-start(bf16[800,800]{1,0:T(8,128)(2,1)} %copy.73.wn_ref), channel_id=1, source_target_pairs={{0,1},{1,0},{2,3},{3,2},{4,5},{5,4},{6,7},{7,6},{8,9},{9,8},{10,11... | collective-permute-start | bytes 3840008 | tf_op jit(solution)/shard_map/ppermute | solution.py:687
  21.2 6.7 %copy-start.12 = (f32[1600]{0:T(1024)S(1)}, f32[1600]{0:T(1024)}, u32[]{:S(2)}) copy-start(f32[1600]{0:T(1024)} %param.24) | copy-start | bytes 19204
  21.2 6.7 %copy-start.7 = (s32[1,1024]{1,0:T(1,128)S(1)}, s32[1,1024]{1,0:T(1,128)}, u32[]{:S(2)}) copy-start(s32[1,1024]{1,0:T(1,128)} %sr_ref.3) | copy-start | bytes 12292
  21.2 9.3 %copy-start.13 = (f32[1600]{0:T(1024)S(1)}, f32[1600]{0:T(1024)}, u32[]{:S(2)}) copy-start(f32[1600]{0:T(1024)} %param.19) | copy-start | bytes 19204
  21.2 9.4 %copy-start.14 = (f32[1600]{0:T(1024)S(1)}, f32[1600]{0:T(1024)}, u32[]{:S(2)}) copy-start(f32[1600]{0:T(1024)} %param.18) | copy-start | bytes 19204
  21.2 25.6 %collective-permute-start.3 = (bf16[48,800]{1,0:T(8,128)(2,1)S(1)}, bf16[48,800]{1,0:T(8,128)(2,1)S(1)}, u32[]{:S(2)}, u32[]{:S(2)}) collective-permute-start(bf16[48,800]{1,0:T(8,128)(2,1)S(1)} %slice.54), channel_id=1, source_target_pairs={{0,2},{2,4},{4,6},{1,3},{3,5},{5,7},{8,10},{10,12},{12,14},{9,11},... | collective-permute-start | bytes 230408 | tf_op jit(solution)/shard_map/ppermute | solution.py:723
  27.8 18.0 %copy-start = (bf16[800,1200]{0,1:T(8,128)(2,1)}, bf16[800,1200]{0,1:T(8,128)(2,1)S(1)}, u32[]{:S(2)}) copy-start(bf16[800,1200]{0,1:T(8,128)(2,1)S(1)} %copy.58) | copy-start | bytes 5760004
  27.8 3.7 copy-start.8
  36.2 5.5 %copy-start.15 = (f32[1600]{0:T(1024)S(1)}, f32[1600]{0:T(1024)}, u32[]{:S(2)}) copy-start(f32[1600]{0:T(1024)} %param.30) | copy-start | bytes 19204
  36.2 5.5 %copy-start.9 = (f32[256]{0:T(256)S(1)}, f32[256]{0:T(256)}, u32[]{:S(2)}) copy-start(f32[256]{0:T(256)} %get-tuple-element.102) | copy-start | bytes 3076
  36.2 5.5 %copy-start.10 = (f32[256]{0:T(256)S(1)}, f32[256]{0:T(256)}, u32[]{:S(2)}) copy-start(f32[256]{0:T(256)} %get-tuple-element.103) | copy-start | bytes 3076
  48.1 186.5 %collective-permute-start.4 = (bf16[256,800]{1,0:T(8,128)(2,1)}, bf16[256,800]{1,0:T(8,128)(2,1)}, u32[]{:S(2)}, u32[]{:S(2)}) collective-permute-start(bf16[256,800]{1,0:T(8,128)(2,1)} %get-tuple-element.121), channel_id=1, source_target_pairs={{0,1},{1,0},{2,3},{3,2},{4,5},{5,4},{6,7},{7,6},{8,9},{9,8},{10,11... | collective-permute-start | bytes 1228808 | tf_op jit(solution)/shard_map/ppermute | solution.py:687
  208.2 23.1 %copy-start.1 = (f32[256,800]{1,0:T(8,128)S(1)}, f32[256,800]{1,0:T(8,128)}, u32[]{:S(2)}) copy-start(f32[256,800]{1,0:T(8,128)} %shard_map.277) | copy-start | bytes 2457604
  208.2 23.1 %copy-start.2 = (bf16[256,800]{1,0:T(8,128)(2,1)S(1)}, bf16[256,800]{1,0:T(8,128)(2,1)}, u32[]{:S(2)}) copy-start(bf16[256,800]{1,0:T(8,128)(2,1)} %copy.64.x_ref) | copy-start | bytes 1228804
  271.5 38.4 %copy-start.18 = (bf16[4,256,800]{2,1,0:T(8,128)(2,1)S(1)}, bf16[4,256,800]{2,1,0:T(8,128)(2,1)}, u32[]{:S(2)}) copy-start(bf16[4,256,800]{2,1,0:T(8,128)(2,1)} %get-tuple-element.42) | copy-start | bytes 4915204
  315.6 2.7 copy-start.19
  315.6 115.9 %reduce-scatter.12.cloned.1.call-start = ((), (), s32[]{:S(2)}) async-start(), calls=%async_computation.5 | async-start | bytes 3328000
  324.5 164.7 %reduce-scatter.10.cloned.1.call-start = ((), (), s32[]{:S(2)}) async-start(), calls=%async_computation.4 | async-start | bytes 3584000 | tf_op jit(solution)/shard_map/reduce_scatter | solution.py:782
  324.5 6.1 %copy-start.17 = (bf16[4,256,800]{2,1,0:T(8,128)(2,1)S(1)}, bf16[4,256,800]{2,1,0:T(8,128)(2,1)}, u32[]{:S(2)}) copy-start(bf16[4,256,800]{2,1,0:T(8,128)(2,1)} %get-tuple-element.46) | copy-start | bytes 4915204
  337.4 0.7 copy-start.16
  337.5 4.2 copy-start.11
  337.5 4.4 copy-start.3
  396.1 10.3 %copy-start.6 = (f32[32,8,128]{2,1,0:T(8,128)S(1)}, f32[32,8,128]{2,1,0:T(8,128)}, u32[]{:S(2)}) copy-start(f32[32,8,128]{2,1,0:T(8,128)} %shard_map.281) | copy-start | bytes 393220
  396.8 14.1 %collective-permute-start.5 = (bf16[36,800]{1,0:T(8,128)(2,1)}, bf16[36,800]{1,0:T(8,128)(2,1)}, u32[]{:S(2)}, u32[]{:S(2)}) collective-permute-start(bf16[36,800]{1,0:T(8,128)(2,1)} %slice.75), channel_id=1, source_target_pairs={{0,8},{8,16},{16,24},{1,9},{9,17},{17,25},{2,10},{10,18},{18,26},{... | collective-permute-start | bytes 172808
Sparse Core Ops, SparseCore 0:
  315.7 46.3 reduce-scatter.7
  364.4 67.0 reduce-scatter.11
  433.8 55.3 reduce-scatter.9

commit v2 on v1

v2 whole, which is shorter than its diff:
```python
import functools

import jax
import jax.numpy as jnp
from jax import lax
from jax.experimental import pallas as pl
from jax.experimental.pallas import tpu as pltpu
from jax.sharding import PartitionSpec as P

HEADS = 25
HEAD_DIM = 64
EPS = 1e-05
NEG = -1e30
GRAIN = 16
AXES = ("dp", "row", "col")
MESH = pl.DeviceIdType.MESH
F32 = jnp.float32
BF16 = jnp.bfloat16
VMEM_BYTES = 60 * 1024 * 1024

NN = (((1,), (0,)), ((), ()))
NT = (((1,), (1,)), ((), ()))
TN = (((0,), (0,)), ((), ()))


def dot(left, right, dims):
    return lax.dot_general(left, right, dims, preferred_element_type=F32)


class Place:
    def __init__(self):
        self.d = lax.axis_index("dp")
        self.r = lax.axis_index("row")
        self.c = lax.axis_index("col")
        one = self.r + 1 - 2 * lax.rem(self.r, 2)
        two = lax.rem(self.r + 2, 4)
        self.a = 1 + self.c
        self.b = 2 - self.c
        self.ra = (1 - self.c) * one + self.c * two
        self.rb = self.c * one + (1 - self.c) * two
        self.r3 = 3 - self.r

    def dev(self, row, col=None):
        return (self.d, row, self.c if col is None else col)

    def mate(self):
        return (self.d, self.r, 1 - self.c)

    def barrier(self, devices):
        semaphore = pltpu.get_barrier_semaphore()
        for device in devices:
            pl.semaphore_signal(semaphore, inc=1, device_id=device, device_id_type=MESH)
        pl.semaphore_wait(semaphore, len(devices))

    def group(self):
        flat = 2 * self.r + self.c
        found = []
        for step in range(1, 8):
            other = lax.rem(flat + step, 8)
            found.append((self.d, other // 2, lax.rem(other, 2)))
        return found

    def square(self):
        return [self.mate(), self.dev(self.ra), self.dev(self.rb)]


def rcopy(src, dst, send, recv, device):
    return pltpu.make_async_remote_copy(
        src_ref=src, dst_ref=dst, send_sem=send, recv_sem=recv, device_id=device,
        device_id_type=MESH,
    )


def lanes(index, size):
    return pl.ds(pl.multiple_of(index * size, size), size)


def call(kernel, out_shapes, out_specs, in_specs, scratch, cid, flops=0, bytes_accessed=0):
    return pl.pallas_call(
        kernel,
        out_shape=out_shapes,
        in_specs=in_specs,
        out_specs=out_specs,
        scratch_shapes=scratch,
        compiler_params=pltpu.CompilerParams(
            collective_id=cid, has_side_effects=True, vmem_limit_bytes=VMEM_BYTES
        ),
    )


VM = pl.BlockSpec(memory_space=pltpu.VMEM)
ANY = pl.BlockSpec(memory_space=pl.ANY)
DMA = pltpu.SemaphoreType.DMA


def struct(shape, dtype):
    return jax.ShapeDtypeStruct(shape, dtype)


def chunks(size):
    count = next(n for n in (5, 4, 2, 1) if size % (n * GRAIN) == 0)
    return [pl.ds(k * (size // count), size // count) for k in range(count)]


def col_sums(matrix):
    ones = jnp.ones((8, matrix.shape[1]), matrix.dtype)
    exact = lax.Precision.HIGHEST if matrix.dtype == F32 else None
    return lax.dot_general(ones, matrix, NT, precision=exact, preferred_element_type=F32)[0:1]


class Totals:
    scratch = [pltpu.VMEM((2, 8, 256), F32), DMA((2,))]

    def __init__(self, place, buf, sems):
        self.place, self.buf, self.sems = place, buf, sems

    def __call__(self, first, second):
        self.buf[0, 0:1] = jnp.sum(first, axis=0, keepdims=True)
        self.buf[0, 1:2] = jnp.sum(second, axis=0, keepdims=True)
        copy = rcopy(
            self.buf.at[0], self.buf.at[1], self.sems.at[0], self.sems.at[1], self.place.mate()
        )
        copy.start()
        copy.wait()
        return (
            self.buf[0, 0:1] + self.buf[1, 0:1],
            self.buf[0, 1:2] + self.buf[1, 1:2],
        )


def moments(totals, matrix, width):
    total, square = totals(matrix, matrix * matrix)
    average = total / width
    return average, lax.rsqrt(square / width - average * average + EPS)


def keep_moments(ref, average, rstd):
    ref[0:1] = average
    ref[1:2] = rstd


def norm_back(totals, grad_in, hat, rstd, gain, width):
    scaled = grad_in * gain
    total, mixed = totals(scaled, scaled * hat)
    return rstd * (scaled - total / width - hat * mixed / width)


def gather_scratch(rows, cols, feats, turned):
    count = len(chunks(rows))
    return [
        pltpu.VMEM((2, 4, rows, cols), BF16), DMA((7, count)), DMA((2, 4, count)), DMA((4,)),
        pltpu.VMEM((rows, turned), BF16), pltpu.VMEM((turned, rows), BF16),
        pltpu.VMEM((feats, rows), BF16), DMA((3,)),
    ]


class Gather:
    def __init__(self, place, all_ref, w_ref, w_step, refs):
        self.place, self.all_ref = place, all_ref
        self.got, self.send, self.recv, self.out_sem = refs[:4]
        self.w_flat, self.turned, self.w_oth, w_sem = refs[4:]
        self.w_load = pltpu.make_async_copy(w_ref, self.w_flat, w_sem.at[2])
        self.w_load.start()
        feats = self.w_oth.shape[0]
        start = w_step[0] + w_step[1] * place.c
        other = w_step[0] + w_step[1] * (1 - place.c)
        self.w_own = self.turned.at[pl.ds(pl.multiple_of(start, GRAIN), feats)]
        theirs = self.turned.at[pl.ds(pl.multiple_of(other, GRAIN), feats)]
        self.w_copy = rcopy(theirs, self.w_oth, w_sem.at[0], w_sem.at[1], place.mate())

    def product(self, slot):
        return dot(self.w_own[...], self.got[0, slot], NN) + dot(
            self.w_oth[...], self.got[1, slot], NN
        )

    def run(self, work, idle=None):
        place, got, send, recv = self.place, self.got, self.send, self.recv
        mate, size = place.mate(), got.shape[3]
        parts = list(enumerate(chunks(got.shape[2])))
        dev_a, dev_b = place.dev(place.ra), place.dev(place.rb)

        def move(number, source, target, device):
            return [
                rcopy(
                    got.at[source[0], source[1], part], got.at[target[0], target[1], part],
                    send.at[number, k], recv.at[target[0], target[1], k], device,
                )
                for k, part in parts
            ]

        def keep(slot, row, number):
            copy = pltpu.make_async_copy(
                got.at[0, slot], self.all_ref.at[:, lanes(row, size)], self.out_sem.at[number]
            )
            copy.start()
            return copy

        to_a = move(0, (0, 0), (0, place.a), dev_a)
        to_b = move(1, (0, 0), (0, place.b), dev_b)
        to_mate = move(2, (0, 0), (1, 0), mate)
        relay = move(3, (0, place.a), (0, 3), dev_b)
        fwd_a = move(4, (0, place.a), (1, place.a), mate)
        fwd_b = move(5, (0, place.b), (1, place.b), mate)
        fwd_3 = move(6, (0, 3), (1, 3), mate)
        for copies in (to_a, to_b, to_mate):
            for copy in copies:
                copy.start()
        kept = [keep(0, place.r, 0)]
        self.w_load.wait()
        self.turned[...] = self.w_flat[...].T
        self.w_copy.start()
        if idle is not None:
            idle()
        self.w_copy.wait()
        for copy in to_mate:
            copy.wait_recv()
        work(0, place.r)
        for k, copy in enumerate(to_a):
            copy.wait_recv()
            relay[k].start()
            fwd_a[k].start()
        kept.append(keep(place.a, place.ra, 1))
        for k, copy in enumerate(to_b):
            copy.wait_recv()
            fwd_b[k].start()
        kept.append(keep(place.b, place.rb, 2))
        for copy in fwd_b:
            copy.wait_recv()
        work(place.b, place.rb)
        for copy in fwd_a:
            copy.wait_recv()
        work(place.a, place.ra)
        for k, copy in enumerate(relay):
            copy.wait_recv()
            fwd_3[k].start()
        kept.append(keep(3, place.r3, 3))
        for copy in fwd_3:
            copy.wait_recv()
        work(3, place.r3)
        for copies in (to_mate, to_a, to_b, relay, fwd_a, fwd_b, fwd_3):
            for copy in copies:
                copy.wait_send()
        for copy in kept:
            copy.wait()


def gather_triple(tokens, cols, bias, weight, width, feats, cid):
    rows, size = tokens.shape
    triple_width = weight.shape[1]
    grains = feats // GRAIN
    shift = triple_width - feats
    per = 3 * HEAD_DIM

    def kernel(x_ref, c_ref, b_ref, w_ref, all_ref, h_ref, st_ref, tt, tb, ts, gs, gr, *refs):
        place = Place()
        place.barrier(place.group())
        me = 2 * place.r + place.c
        gather = Gather(place, all_ref, w_ref, (0, shift), refs)
        wide = x_ref[...].astype(F32)
        average, rstd = moments(Totals(place, tb, ts), wide, width)
        keep_moments(st_ref, average, rstd)
        gather.got[0, 0] = ((wide - average) * rstd * c_ref[:, 0:1] + c_ref[:, 1:2]).astype(BF16)

        def target(j):
            feature = triple_width * place.r + shift * place.c + GRAIN * j
            part = feature // width
            inner = feature - part * width
            head = inner // HEAD_DIM
            owner = jnp.minimum(head // 3, 7)
            row = (head - 3 * owner) * per + part * HEAD_DIM + (inner - head * HEAD_DIM)
            return owner, pl.ds(pl.multiple_of(row, GRAIN), GRAIN)

        def work(slot, row):
            tt[:, lanes(row, size)] = (gather.product(slot) + b_ref[...]).astype(BF16)

            def send_grain(j, carry):
                owner, place_rows = target(j)
                src = tt.at[pl.ds(pl.multiple_of(GRAIN * j, GRAIN), GRAIN), lanes(row, size)]
                dst = h_ref.at[place_rows, lanes(row, size)]

                @pl.when(owner == me)
                def _():
                    pltpu.make_async_copy(src, dst, gr).start()

                @pl.when(owner != me)
                def _():
                    rcopy(src, dst, gs, gr, (place.d, owner // 2, lax.rem(owner, 2))).start()

                return carry

            lax.fori_loop(place.c, grains, send_grain, 0)

        gather.run(work)

        def drain(j, carry):
            @pl.when(target(j)[0] != me)
            def _():
                src = tt.at[pl.ds(0, GRAIN)]
                pltpu.make_async_copy(src, src, gs).wait()

            return carry

        lax.fori_loop(place.c, grains, drain, 0)

        @pl.when(me == 7)
        def _():
            pltpu.make_async_copy(h_ref, h_ref, gr).wait()

        @pl.when(me != 7)
        def _():
            part = h_ref.at[pl.ds(0, 3 * per)]
            pltpu.make_async_copy(part, part, gr).wait()

    return call(
        kernel,
        (struct((rows, 4 * size), BF16), struct((4 * per, 4 * size), BF16), struct((8, size), F32)),
        (ANY, ANY, VM), [VM] * 3 + [ANY],
        [pltpu.VMEM((feats, 4 * size), BF16)] + Totals.scratch + [DMA, DMA]
        + gather_scratch(rows, size, feats, triple_width), cid,
    )(tokens, cols, bias, weight)


def gather_cotangent(cot, weight, cid):
    rows, size = cot.shape
    feats = weight.shape[1] // 2

    def kernel(x_ref, w_ref, all_ref, y_ref, y, y_sem, *refs):
        place = Place()
        place.barrier(place.square())
        gather = Gather(place, all_ref, w_ref, (0, feats), refs)
        gather.got[0, 0] = x_ref[...]
        pending = []

        def work(slot, row):
            number = len(pending)
            y[number] = gather.product(slot)
            copy = pltpu.make_async_copy(
                y.at[number], y_ref.at[:, lanes(row, size)], y_sem.at[number]
            )
            copy.start()
            pending.append(copy)

        gather.run(work)
        for copy in pending:
            copy.wait()

    return call(
        kernel, (struct((rows, 4 * size), BF16), struct((feats, 4 * size), F32)),
        (ANY, ANY), [VM, ANY],
        [pltpu.VMEM((4, feats, size), F32), DMA((4,))]
        + gather_scratch(rows, size, feats, 2 * feats), cid,
    )(cot, weight)


def gather_hidden(tokens, proj_out, cols, bias, act_grad, weight, width, cid):
    rows, size = tokens.shape
    feats = weight.shape[1] // 2

    def kernel(
        t_ref, p_ref, c_ref, b_ref, g_ref, w_ref,
        all_ref, act_ref, hid_ref, mid_ref, st_ref, sum_ref,
        act, hid, swap_send, swap_recv, swap_out, grads, g_sem, grad_sum, tb, ts, *refs,
    ):
        place = Place()
        place.barrier(place.square())
        mate = place.mate()
        g_load = pltpu.make_async_copy(g_ref, grads, g_sem)
        g_load.start()
        gather = Gather(place, all_ref, w_ref, (0, feats), refs)
        middle = t_ref[...].astype(F32) + p_ref[...] + c_ref[:, 2:3]
        mid_ref[...] = middle
        average, rstd = moments(Totals(place, tb, ts), middle, width)
        keep_moments(st_ref, average, rstd)
        gather.got[0, 0] = ((middle - average) * rstd * c_ref[:, 3:4] + c_ref[:, 4:5]).astype(BF16)
        pending = []
        mine = pl.ds(pl.multiple_of(place.c * feats, GRAIN), feats)

        def work(slot, row):
            number = len(pending)
            if number == 0:
                g_load.wait()
            p = gather.product(slot) + b_ref[...]
            square = p * p
            t = jnp.tanh(0.7978845608028654 * (p + 0.044715 * (square * p)))
            act[number] = (0.5 * p * (1.0 + t)).astype(BF16)
            slope = 0.5 * (1.0 + t) + 0.5 * p * (1.0 - t * t) * (
                0.7978845608028654 * (1.0 + 3.0 * 0.044715 * square)
            )
            grad = grads[:, lanes(row, size)] * slope
            hid[number] = grad.astype(BF16)
            copies = []
            for k, (buf, out) in enumerate(((act, act_ref), (hid, hid_ref))):
                there = out.at[mine, lanes(row, size)]
                out_copy = pltpu.make_async_copy(buf.at[number], there, swap_out.at[k, number])
                swap = rcopy(
                    buf.at[number], there, swap_send.at[k, number], swap_recv.at[k, number], mate
                )
                out_copy.start()
                swap.start()
                copies += [out_copy, swap]
            grad_sum[...] = grad if number == 0 else grad_sum[...] + grad
            pending.append(copies)

        gather.run(work)
        sum_ref[0:1] = col_sums(grad_sum[...])
        for copies in pending:
            for copy in copies:
                copy.wait()

    full = struct((2 * feats, 4 * size), BF16)
    return call(
        kernel,
        (
            struct((rows, 4 * size), BF16), full, full, struct((rows, size), F32),
            struct((8, size), F32), struct((8, feats), F32),
        ),
        (ANY, ANY, ANY, VM, VM, VM), [VM] * 4 + [ANY, ANY],
        [pltpu.VMEM((4, feats, size), BF16)] * 2 + [DMA((2, 4))] * 3
        + [pltpu.VMEM((feats, 4 * size), F32), DMA, pltpu.VMEM((feats, size), F32)]
        + Totals.scratch + gather_scratch(rows, size, feats, 2 * feats), cid,
    )(tokens, proj_out, cols, bias, act_grad, weight)


def gather_middle(grad_in, middle, stats, cot, cols, weight, start, step, width, cid):
    rows, size = cot.shape
    feats = 4 * HEAD_DIM

    def kernel(
        s_ref, m_ref, st_ref, x_ref, c_ref, w_ref, all_ref, y_ref, mg_ref, sum_ref, tb, ts, *refs
    ):
        place = Place()
        place.barrier(place.square())
        gather = Gather(place, all_ref, w_ref, (start[0] + start[1] * place.r, step), refs)
        rstd = st_ref[1:2]
        hat = (m_ref[...] - st_ref[0:1]) * rstd
        back = norm_back(Totals(place, tb, ts), s_ref[...], hat, rstd, c_ref[:, 3:4], width)
        mg_ref[...] = x_ref[...].astype(F32) + back
        gather.got[0, 0] = mg_ref[...].astype(BF16)

        def idle():
            hat = (m_ref[...] - st_ref[0:1]) * st_ref[1:2]
            sum_ref[0:1] = col_sums(s_ref[...] * hat)
            sum_ref[1:2] = col_sums(s_ref[...])
            sum_ref[2:3] = col_sums(mg_ref[...])
            sum_ref[3:4] = col_sums(x_ref[...])

        def work(slot, row):
            y_ref[:, lanes(row, size)] = gather.product(slot).astype(BF16)

        gather.run(work, idle)

    return call(
        kernel,
        (
            struct((rows, 4 * size), BF16), struct((feats, 4 * size), BF16),
            struct((rows, size), F32), struct((8, rows), F32),
        ),
        (ANY, VM, VM, VM), [VM] * 5 + [ANY],
        Totals.scratch + gather_scratch(rows, size, feats, weight.shape[1]), cid,
    )(grad_in, middle, stats, cot, cols, weight)


def scatter_scratch(rows, cols):
    count = len(chunks(rows))
    return [
        pltpu.VMEM((3, rows, cols), BF16), pltpu.VMEM((3, rows, cols), BF16),
        DMA((3, count)), DMA((3, count)), pltpu.VMEM((rows, cols), F32),
    ]


def run_scatter(place, block, refs):
    outbox, inbox, send, recv, passed = refs
    parts = list(enumerate(chunks(outbox.shape[1])))

    def move(number, device):
        return [
            rcopy(
                outbox.at[number, part], inbox.at[number, part],
                send.at[number, k], recv.at[number, k], device,
            )
            for k, part in parts
        ]

    first = move(0, place.dev(place.ra))
    second = move(1, place.dev(place.ra))
    third = move(2, place.dev(place.rb))
    outbox[0] = block(place.r3).astype(BF16)
    for copy in first:
        copy.start()
    passed[...] = block(place.rb)
    outbox[1] = block(place.ra).astype(BF16)
    for copy in second:
        copy.start()
    for k, part in parts:
        first[k].wait_recv()
        outbox[2, part] = (passed[part] + inbox[0, part].astype(F32)).astype(BF16)
        third[k].start()
    passed[...] = block(place.r)
    for copy in second:
        copy.wait_recv()
    passed[...] += inbox[1].astype(F32)
    for copy in third:
        copy.wait_recv()
    total = passed[...] + inbox[2].astype(F32)
    for copies in (first, second, third):
        for copy in copies:
            copy.wait_send()
    return total


def load_scratch(weight, left):
    return [pltpu.VMEM(weight.shape, BF16), pltpu.VMEM(left.shape, BF16), DMA((5,))]


def loaded_block(place, l_ref, w_ref, weight, left, sems, size):
    w_load = pltpu.make_async_copy(w_ref, weight, sems.at[4])
    w_load.start()
    loads = []
    for k, row in enumerate((place.r3, place.rb, place.ra, place.r)):
        span = lanes(row, size)
        loads.append(pltpu.make_async_copy(l_ref.at[:, span], left.at[:, span], sems.at[k]))
        loads[-1].start()

    def block(row):
        if len(loads) == 4:
            w_load.wait()
        loads.pop(0).wait()
        return dot(weight[...], left[:, lanes(row, size)], NN)

    return block


def hidden_scatter(left, weight, cid):
    rows, size = weight.shape[0], left.shape[1] // 4

    def kernel(l_ref, w_ref, out_ref, w, l, l_sem, *refs):
        place = Place()
        block = loaded_block(place, l_ref, w_ref, w, l, l_sem, size)
        place.barrier([place.dev(place.ra), place.dev(place.rb)])
        out_ref[...] = run_scatter(place, block, refs)

    return call(
        kernel, struct((rows, size), F32), VM, [ANY] * 2,
        load_scratch(weight, left) + scatter_scratch(rows, size), cid,
    )(left, weight)


def output_scatter(left, weight, middle, cols, cid):
    rows, size = middle.shape

    def kernel(l_ref, w_ref, m_ref, c_ref, out_ref, w, l, l_sem, *refs):
        place = Place()
        block = loaded_block(place, l_ref, w_ref, w, l, l_sem, size)
        place.barrier([place.dev(place.ra), place.dev(place.rb)])
        total = run_scatter(place, block, refs)
        out_ref[...] = (m_ref[...] + total + c_ref[:, 5:6]).astype(BF16)

    return call(
        kernel, struct((rows, size), BF16), VM, [ANY, ANY, VM, VM],
        load_scratch(weight, left) + scatter_scratch(rows, size), cid,
    )(left, weight, middle, cols)


def attended_scatter(heads, weight, cid):
    feats, rows = weight.shape
    tokens = heads.shape[1]
    size = tokens // 4

    def kernel(h_ref, w_ref, all_ref, out_ref, full, gs, gr, kept_sem, *refs):
        place = Place()
        place.barrier(place.group())
        me = 2 * place.r + place.c
        count = jnp.where(me == 7, 4, 3) * (HEAD_DIM // GRAIN)

        def send_grain(j, carry):
            feature = 3 * HEAD_DIM * me + GRAIN * j
            owner = feature // feats
            src = h_ref.at[pl.ds(pl.multiple_of(GRAIN * j, GRAIN), GRAIN)]
            dst = full.at[pl.ds(pl.multiple_of(feature - owner * feats, GRAIN), GRAIN)]
            rcopy(src, dst, gs, gr, (place.d, owner, 1 - place.c)).start()

            @pl.when(owner == place.r)
            def _():
                pltpu.make_async_copy(src, dst, gr).start()

            @pl.when(owner != place.r)
            def _():
                rcopy(src, dst, gs, gr, (place.d, owner, place.c)).start()

            return carry

        lax.fori_loop(0, count, send_grain, 0)

        def drain(j, carry):
            feature = 3 * HEAD_DIM * me + GRAIN * j
            src = h_ref.at[pl.ds(0, GRAIN)]
            pltpu.make_async_copy(src, src, gs).wait()

            @pl.when(feature // feats != place.r)
            def _():
                pltpu.make_async_copy(src, src, gs).wait()

            return carry

        lax.fori_loop(0, count, drain, 0)
        pltpu.make_async_copy(full, full, gr).wait()
        kept = pltpu.make_async_copy(full, all_ref, kept_sem)
        kept.start()
        out_ref[...] = run_scatter(
            place, lambda row: dot(w_ref[...], full[:, lanes(row, size)], TN), refs
        )
        kept.wait()

    return call(
        kernel, (struct((feats, tokens), BF16), struct((rows, size), F32)),
        (ANY, VM), [ANY, VM],
        [pltpu.VMEM((feats, tokens), BF16), DMA, DMA, DMA] + scatter_scratch(rows, size), cid,
    )(heads, weight)


def triple_scatter(heads, weight, tokens, stats, middle_grad, cols, width, cid):
    rows, feats = weight.shape
    count_tokens = heads.shape[1]
    size = count_tokens // 4
    per = 3 * HEAD_DIM
    low = (feats // GRAIN + 1) // 2 * GRAIN

    def kernel(
        h_ref, w_ref, t_ref, st_ref, mg_ref, c_ref, all_ref, out_ref, sum_ref, bias_ref,
        full, w, w_sem, tb, ts, gs, gr, ms, mr, kept_sem, *refs,
    ):
        place = Place()
        w_load = pltpu.make_async_copy(w_ref, w, w_sem)
        w_load.start()
        place.barrier(place.group())
        me = 2 * place.r + place.c
        count = jnp.where(me == 7, 4, 3) * (per // GRAIN)

        def target(j):
            row = GRAIN * j
            head = row // per
            rest = row - head * per
            part = rest // HEAD_DIM
            feature = part * width + (3 * me + head) * HEAD_DIM + rest - part * HEAD_DIM
            owner = feature // feats
            inner = feature - owner * feats
            return 2 * owner + inner // low, inner

        def send_grain(j, carry):
            owner, inner = target(j)
            src = h_ref.at[pl.ds(pl.multiple_of(GRAIN * j, GRAIN), GRAIN)]
            dst = full.at[pl.ds(pl.multiple_of(inner, GRAIN), GRAIN)]

            @pl.when(owner == me)
            def _():
                pltpu.make_async_copy(src, dst, gr).start()

            @pl.when(owner != me)
            def _():
                rcopy(src, dst, gs, gr, (place.d, owner // 2, lax.rem(owner, 2))).start()

            return carry

        lax.fori_loop(0, count, send_grain, 0)

        def drain(j, carry):
            @pl.when(target(j)[0] != me)
            def _():
                src = h_ref.at[pl.ds(0, GRAIN)]
                pltpu.make_async_copy(src, src, gs).wait()

            return carry

        lax.fori_loop(0, count, drain, 0)
        lower, upper = full.at[pl.ds(0, low)], full.at[pl.ds(low, feats - low)]

        def swap(mine, theirs):
            pltpu.make_async_copy(mine, mine, gr).wait()
            copy = rcopy(mine, mine, ms, mr, place.mate())
            copy.start()
            copy.wait_send()
            pltpu.make_async_copy(theirs, theirs, mr).wait()

        @pl.when(place.c == 0)
        def _():
            swap(lower, upper)

        @pl.when(place.c == 1)
        def _():
            swap(upper, lower)

        kept = pltpu.make_async_copy(full, all_ref, kept_sem)
        kept.start()
        w_load.wait()
        grad = run_scatter(place, lambda row: dot(w[...], full[:, lanes(row, size)], NN), refs)
        rstd = st_ref[1:2]
        hat = (t_ref[...].astype(F32) - st_ref[0:1]) * rstd
        back = norm_back(Totals(place, tb, ts), grad, hat, rstd, c_ref[:, 0:1], width)
        out_ref[...] = mg_ref[...] + back
        sum_ref[0:1] = col_sums(grad * hat)
        sum_ref[1:2] = col_sums(grad)
        bias_ref[0:1] = col_sums(full[...])
        kept.wait()

    return call(
        kernel,
        (
            struct((feats, count_tokens), BF16), struct((rows, size), F32),
            struct((8, rows), F32), struct((8, feats), F32),
        ),
        (ANY, VM, VM, VM), [ANY, ANY] + [VM] * 4,
        [pltpu.VMEM((feats, count_tokens), BF16), pltpu.VMEM(weight.shape, BF16), DMA]
        + Totals.scratch + [DMA] * 5
        + scatter_scratch(rows, size), cid,
    )(heads, weight, tokens, stats, middle_grad, cols)


def attention_bias(seg_col, seg_row, bias_ref):
    tokens = seg_row.shape[1]
    key = lax.broadcasted_iota(jnp.int32, (tokens, tokens), 0)
    query = lax.broadcasted_iota(jnp.int32, (tokens, tokens), 1)
    allowed = (seg_col[...] == seg_row[...]) & (key <= query)
    bias_ref[...] = jnp.where(allowed, 0.0, NEG)


def holds(head):
    return (head < 3) | ((lax.axis_index("row") == 3) & (lax.axis_index("col") == 1))


def attention_forward(triple, seg_col, seg_row):
    per = 3 * HEAD_DIM
    tokens = triple.shape[1]
    span = tokens // 4

    def kernel(sc_ref, sr_ref, t_ref, o_ref, l_ref, bias_ref):
        @pl.when(pl.program_id(0) == 0)
        def _():
            attention_bias(sc_ref, sr_ref, bias_ref)

        @pl.when(holds(pl.program_id(0)))
        def _():
            for j in range(4):
                reach, here = (j + 1) * span, slice(j * span, (j + 1) * span)
                query = t_ref[0:HEAD_DIM, here] * BF16(HEAD_DIM ** (-0.5))
                score = dot(t_ref[HEAD_DIM : 2 * HEAD_DIM, 0:reach], query, TN)
                score = score + bias_ref[0:reach, here]
                top = jnp.max(score, axis=0, keepdims=True)
                weight = jnp.exp(score - top)
                total = jnp.sum(weight, axis=0, keepdims=True)
                mixed = dot(t_ref[2 * HEAD_DIM : per, 0:reach], weight.astype(BF16), NN)
                o_ref[:, here] = (mixed / total).astype(BF16)
                l_ref[0, :, here] = top + jnp.log(total)

    return pl.pallas_call(
        kernel,
        grid=(4,),
        out_shape=(
            jax.ShapeDtypeStruct((4 * HEAD_DIM, tokens), BF16),
            jax.ShapeDtypeStruct((4, 1, tokens), F32),
        ),
        in_specs=[
            pl.BlockSpec((tokens, 1), lambda h: (0, 0)),
            pl.BlockSpec((1, tokens), lambda h: (0, 0)),
            pl.BlockSpec((per, tokens), lambda h: (h, 0)),
        ],
        out_specs=(
            pl.BlockSpec((HEAD_DIM, tokens), lambda h: (h, 0)),
            pl.BlockSpec((1, 1, tokens), lambda h: (h, 0, 0)),
        ),
        scratch_shapes=[pltpu.VMEM((tokens, tokens), F32)],
        compiler_params=pltpu.CompilerParams(vmem_limit_bytes=VMEM_BYTES),
    )(seg_col, seg_row, triple)


def attention_backward(triple, seg_col, seg_row, attended, attended_grad, lse):
    per = 3 * HEAD_DIM
    tokens = triple.shape[1]
    span = tokens // 4

    def kernel(sc_ref, sr_ref, t_ref, o_ref, g_ref, l_ref, d_ref, bias_ref, kg_ref, vg_ref):
        @pl.when(pl.program_id(0) == 0)
        def _():
            attention_bias(sc_ref, sr_ref, bias_ref)

        @pl.when(holds(pl.program_id(0)))
        def _():
            kg_ref[...] = jnp.zeros_like(kg_ref)
            vg_ref[...] = jnp.zeros_like(vg_ref)
            for j in range(4):
                reach, here = (j + 1) * span, slice(j * span, (j + 1) * span)
                query = t_ref[0:HEAD_DIM, here] * BF16(HEAD_DIM ** (-0.5))
                key = t_ref[HEAD_DIM : 2 * HEAD_DIM, 0:reach]
                grad = g_ref[:, here]
                delta = jnp.sum(
                    grad.astype(F32) * o_ref[:, here].astype(F32), axis=0, keepdims=True
                )
                score = dot(key, query, TN) + bias_ref[0:reach, here]
                prob = jnp.exp(score - l_ref[0, :, here])
                vg_ref[:, 0:reach] += dot(grad, prob.astype(BF16), NT)
                back = dot(t_ref[2 * HEAD_DIM : per, 0:reach], grad, TN)
                mix = (prob * (back - delta)).astype(BF16)
                d_ref[0:HEAD_DIM, here] = (dot(key, mix, NN) * HEAD_DIM ** (-0.5)).astype(BF16)
                kg_ref[:, 0:reach] += dot(query, mix, NT)
            d_ref[HEAD_DIM : 2 * HEAD_DIM, :] = kg_ref[...].astype(BF16)
            d_ref[2 * HEAD_DIM : per, :] = vg_ref[...].astype(BF16)

    return pl.pallas_call(
        kernel,
        grid=(4,),
        out_shape=jax.ShapeDtypeStruct((4 * per, tokens), BF16),
        in_specs=[
            pl.BlockSpec((tokens, 1), lambda h: (0, 0)),
            pl.BlockSpec((1, tokens), lambda h: (0, 0)),
            pl.BlockSpec((per, tokens), lambda h: (h, 0)),
            pl.BlockSpec((HEAD_DIM, tokens), lambda h: (h, 0)),
            pl.BlockSpec((HEAD_DIM, tokens), lambda h: (h, 0)),
            pl.BlockSpec((1, 1, tokens), lambda h: (h, 0, 0)),
        ],
        out_specs=pl.BlockSpec((per, tokens), lambda h: (h, 0)),
        scratch_shapes=[
            pltpu.VMEM((tokens, tokens), F32),
            pltpu.VMEM((HEAD_DIM, tokens), F32),
            pltpu.VMEM((HEAD_DIM, tokens), F32),
        ],
        compiler_params=pltpu.CompilerParams(vmem_limit_bytes=VMEM_BYTES),
    )(seg_col, seg_row, triple, attended, attended_grad, lse)


def sum_all(pieces, sizes, cid):
    count = pieces.shape[0]
    rows, cols = sizes

    def kernel(x_ref, out_ref, inbox, piece, sems):
        me = (lax.axis_index("dp") * rows + lax.axis_index("row")) * cols + lax.axis_index("col")

        def dev(step):
            flat = lax.rem(me + step, count)
            return flat, (flat // (rows * cols), lax.rem(flat // cols, rows), lax.rem(flat, cols))

        semaphore = pltpu.get_barrier_semaphore()

        def greet(step, carry):
            pl.semaphore_signal(semaphore, inc=1, device_id=dev(step)[1], device_id_type=MESH)
            return carry

        lax.fori_loop(1, count, greet, 0)
        pl.semaphore_wait(semaphore, count - 1)

        def spread(step, carry):
            flat, device = dev(step)
            rcopy(x_ref.at[flat], inbox.at[me], sems.at[0], sems.at[1], device).start()
            return carry

        lax.fori_loop(1, count, spread, 0)
        inbox[me] = x_ref[me]
        rest = inbox.at[pl.ds(0, count - 1)]
        pltpu.make_async_copy(rest, rest, sems.at[1]).wait()
        pltpu.make_async_copy(rest, rest, sems.at[0]).wait()
        piece[...] = jnp.sum(inbox[...], axis=0)

        def share(step, carry):
            rcopy(piece, out_ref.at[me], sems.at[2], sems.at[3], dev(step)[1]).start()
            return carry

        lax.fori_loop(1, count, share, 0)
        out_ref[me] = piece[...]
        rest = out_ref.at[pl.ds(0, count - 1)]
        pltpu.make_async_copy(rest, rest, sems.at[3]).wait()
        pltpu.make_async_copy(rest, rest, sems.at[2]).wait()

    return call(
        kernel, jax.ShapeDtypeStruct(pieces.shape, F32), VM, [VM],
        [pltpu.VMEM(pieces.shape, F32), pltpu.VMEM(pieces.shape[1:], F32), DMA((4,))], cid,
    )(pieces)


def shards(
    tokens, segment_ids, first_gain, first_shift, triple_weight, query_bias, value_bias,
    proj_weight, proj_bias, second_gain, second_shift, expand_weight, expand_bias,
    shrink_weight, shrink_bias, cotangent, *, axis_sizes,
):
    width = HEADS * HEAD_DIM
    dp_count, row_count, col_count = axis_sizes
    row, col = lax.axis_index("row"), lax.axis_index("col")
    col_width = tokens.shape[1]
    triple_width = triple_weight.shape[1]
    proj_rows = proj_weight.shape[0]
    hidden = expand_weight.shape[1] // 2
    core_feats = (triple_width // GRAIN + 1) // 2 * GRAIN

    stacked = jnp.concatenate(
        [first_gain, first_shift, proj_bias, second_gain, second_shift, shrink_bias]
    ).reshape(6, width)
    cols = lax.dynamic_slice_in_dim(stacked, col * col_width, col_width, 1).T
    full_bias = jnp.concatenate([query_bias, jnp.zeros((width,), F32), value_bias])
    core_bias = lax.dynamic_slice_in_dim(
        full_bias, row * triple_width + col * (triple_width - core_feats), core_feats
    )[:, None]
    core_expand_bias = lax.dynamic_slice_in_dim(
        expand_bias, (row * 2 + col) * hidden, hidden
    )[:, None]
    tokens_t, cot_t = tokens.T, cotangent.T
    seg_row = segment_ids
    seg_col = segment_ids.reshape(-1, 1)

    first_all, triple, first_stats = gather_triple(
        tokens_t, cols, core_bias, triple_weight, width, core_feats, 0
    )
    cot_all, act_grad = gather_cotangent(cot_t, shrink_weight.T, 1)
    attended, lse = attention_forward(triple, seg_col, seg_row)
    attended_all, proj_out = attended_scatter(attended, proj_weight, 2)
    second_all, act_all, hid_all, middle, second_stats, expand_bias_part = gather_hidden(
        tokens_t, proj_out, cols, core_expand_bias, act_grad, expand_weight, width, 3
    )

    def product(left, right):
        return lax.dot_general(left, right, NT, preferred_element_type=F32).astype(BF16)

    def owned(grad):
        parts = grad.reshape(dp_count, -1, grad.shape[1])
        summed = lax.psum_scatter(parts, "dp", scatter_dimension=0, tiled=True)
        return summed.reshape(1, -1, grad.shape[1])

    shrink_grad = product(act_all, cot_all)
    hid_all, shrink_grad = lax.optimization_barrier((hid_all, shrink_grad))
    shrink_owned = owned(shrink_grad)

    second_normed_grad = hidden_scatter(hid_all, expand_weight, 4)
    head_rows = 3 * HEAD_DIM
    lag = (row_count - 1) * (proj_rows - 2 * head_rows)
    before = lax.ppermute(
        proj_weight[proj_rows - lag :], "row", [(i, i + 1) for i in range(row_count - 1)]
    )
    padded = jnp.concatenate(
        [before, proj_weight, jnp.zeros((2 * HEAD_DIM, col_width), BF16)], axis=0
    )
    middle_all, attended_grad, middle_grad, second_sums = gather_middle(
        second_normed_grad, middle, second_stats, cot_t, cols, padded.T,
        (lag, 2 * head_rows - proj_rows), head_rows, width, 5,
    )
    proj_grad = product(attended_all, middle_all)
    pieces = [
        product(second_all, hid_all[:hidden]),
        product(second_all, hid_all[hidden:]),
        proj_grad,
    ]
    both_grad = jnp.concatenate(
        [piece.reshape(dp_count, -1, piece.shape[1]) for piece in pieces], axis=1
    )
    attended_grad, shrink_owned, both_grad = lax.optimization_barrier(
        (attended_grad, shrink_owned, both_grad)
    )
    both_owned = owned(both_grad.reshape(-1, col_width))
    triple_head_grad = attention_backward(
        triple, seg_col, seg_row, attended, attended_grad, lse
    )
    triple_all, input_grad, first_sums, bias_sums = triple_scatter(
        triple_head_grad, triple_weight, tokens_t, first_stats, middle_grad, cols, width, 6
    )
    triple_grad = product(first_all, triple_all)
    act_all, triple_grad, both_owned, first_sums = lax.optimization_barrier(
        (act_all, triple_grad, both_owned, first_sums)
    )
    part = col_width // dp_count
    expand_owned = jnp.concatenate([both_owned[:, :part], both_owned[:, part : 2 * part]], axis=2)
    proj_owned = both_owned[:, 2 * part :]
    triple_owned = owned(triple_grad)
    block_out = output_scatter(act_all, shrink_weight.T, middle, cols, 7)

    by_col = jnp.concatenate([first_sums[:2], second_sums[:4]])
    is_col = (jnp.arange(2) == col).astype(F32)
    by_col = by_col[:, None, :] * is_col[None, :, None]
    is_core = (jnp.arange(2 * row_count) == 2 * row + col).astype(F32)
    by_core = expand_bias_part[0] * is_core[:, None]
    is_row = ((jnp.arange(row_count) == row) & (col == 0)).astype(F32)
    by_row = bias_sums[0][None, :] * is_row[:, None]
    vector = jnp.concatenate([by_col.reshape(-1), by_core.reshape(-1), by_row.reshape(-1)])
    devices = dp_count * row_count * col_count
    tile = 8 * 128
    size = -(-vector.shape[0] // (devices * tile)) * tile
    vector = jnp.pad(vector, (0, devices * size - vector.shape[0]))
    total = sum_all(
        vector.reshape(devices, size // 128, 128), (row_count, col_count), 8
    ).reshape(-1)
    col_totals = total[: 6 * width].reshape(6, width)
    expand_bias_grad = total[6 * width : 6 * width + 2 * row_count * hidden]
    rest = total[6 * width + 2 * row_count * hidden :]
    return (
        block_out.T,
        input_grad.T,
        col_totals[0],
        col_totals[1],
        triple_owned.astype(F32),
        rest[:width],
        rest[2 * width : 3 * width],
        proj_owned.astype(F32),
        col_totals[4],
        col_totals[2],
        col_totals[3],
        expand_owned.astype(F32),
        expand_bias_grad,
        shrink_owned.astype(F32),
        col_totals[5],
    )


def solution(mesh):
    assert mesh.shape["row"] == 4 and mesh.shape["col"] == 2
    sizes = tuple(mesh.shape[name] for name in AXES)
    tok, mat, mat_t = P(("dp", "row"), "col"), P("row", "col"), P("col", "row")
    in_specs = (
        tok, P("dp", None), P(), P(), mat_t, P(), P(), mat, P(), P(), P(), mat_t, P(), mat, P(), tok,
    )
    grad, grad_t = P("row", "dp", "col"), P("col", "dp", "row")
    out_specs = (
        tok, tok, P(), P(), grad_t, P(), P(), grad, P(), P(), P(), grad_t, P(), grad, P(),
    )
    return jax.shard_map(
        functools.partial(shards, axis_sizes=sizes),
        mesh=mesh, in_specs=in_specs, out_specs=out_specs, check_vma=False,
    )
```

time: 508 us -> 352 us (0.69)
  waiting for transfers between devices: 71.5 us -> 2.69 us
  blocking collectives: 45.6 us -> 0 us
  local copies, waits for them, and re-layouts: 51.3 us -> 29.6 us
  other arithmetic: 23.1 us -> 11.5 us
    reduce_scatter x2 -> x3, waiting for transfers between devices: 55.5 us -> 2.64 us  [owned(): summed = lax.psum_scatter(parts, 'dp', scatter_dimension=0, tiled=True)]
    unnamed x1 -> x0, blocking collectives: 29.1 us -> none
    psum x4 -> x0, blocking collectives: 16.5 us -> none  [feature_totals(): lax.psum((jnp.sum(first_term, axis=1, keepdims=True), jnp.sum(second_term...]
    unnamed x5 -> x3, waiting for transfers between devices: 16 us -> 0.05 us
    dynamic_slice x11 -> x1, local copies, waits for them, and re-layouts: 14.4 us -> 0.08 us  [shards(): cols = lax.dynamic_slice_in_dim(stacked, col * col_width, col_width, 1).T]
    unnamed x51 -> x28, local copies, waits for them, and re-layouts: 19.9 us -> 6.72 us
    reduce_sum x6 -> x0, other arithmetic: 8.97 us -> none  [the longest x1 2.46 us: shards(): jnp.sum(middle_grad, axis=0)]
    broadcast_in_dim x4 -> x0, other arithmetic: 6.67 us -> none  [the longest x1 2.3 us: shards(): shrink_owned[None]]
  transfers between devices with their start and end apart: 9 -> 4, of which waited for: 2 -> 1; matrix products, arithmetic and copies ran while one was open for 22% -> 12% of each run, Pallas kernels for 38% -> 41%
where the time goes in v2:
time: 352 us; the launch traced here: 345 us
  Pallas kernels  261 us (74%)
  local copies, waits for them, and re-layouts  29.6 us (8%)
  matrix products  21.9 us (6%)
  between operations  14.6 us (4%)
  other arithmetic  11.5 us (3%)
    pallas_call x1, Pallas kernels, triple_scatter(): call(kernel, (struct((feats, count_tokens), BF16), struct((rows, size), F...  41.5 us
    pallas_call x1, Pallas kernels, gather_triple(): call(kernel, (struct((rows, 4 * size), BF16), struct((4 * per, 4 * size),...  33.5 us
    pallas_call x1, Pallas kernels, gather_hidden(): call(kernel, (struct((rows, 4 * size), BF16), full, full, struct((rows, s...  30.4 us
    pallas_call x1, Pallas kernels, gather_middle(): call(kernel, (struct((rows, 4 * size), BF16), struct((feats, 4 * size), B...  24.9 us
    pallas_call x1, Pallas kernels, attended_scatter(): call(kernel, (struct((feats, tokens), BF16), struct((rows, size), F32)),...  24.6 us
    pallas_call x1, Pallas kernels, gather_cotangent(): call(kernel, (struct((rows, 4 * size), BF16), struct((feats, 4 * size), F...  22.3 us
    pallas_call x1, Pallas kernels, sum_all(): call(kernel, jax.ShapeDtypeStruct(pieces.shape, F32), VM, [VM], [pltpu.VM...  22.3 us
    pallas_call x1, Pallas kernels, output_scatter(): call(kernel, struct((rows, size), BF16), VM, [ANY, ANY, VM, VM], load_scr...  22.2 us
  transfers between devices with their start and end apart: 4, of which 1 were waited for; matrix products, arithmetic and copies ran while one was open for 12% of the time, Pallas kernels for 41%

profile of v2, /device:TPU:25, one launch (start us, length us, event | category | flops | bytes accessed | tf_op | source)
XLA Modules:
  0.0 344.7 jit_solution(8669501311311009824)
XLA Ops:
  7.3 0.8 concatenate.30
  8.1 0.9 broadcast_in_dim.20.b_ref
  9.0 0.9 concatenate.29
  10.0 0.9 copy.57
  11.0 1.7 copy.46.sc_ref
  12.7 0.8 dynamic_slice.11
  13.4 0.9 broadcast_in_dim.21.b_ref
  14.4 33.5 %shard_map.271 = (bf16[800,1024]{1,0:T(8,128)(2,1)}, bf16[768,1024]{1,0:T(8,128)(2,1)}, f32[8,256]{1,0:T(8,128)}) custom-call(bf16[800,256]{1,0:T(8,128)(2,1)} %bitcast.32, f32[800,6]{1,0:T(8,128)} %bitcast.24, f32[608,1]{1,0:T(8,128)} %broadcast_in_dim.20.b_ref, bf16[800,1200]{1,0:T(8,128)(2,1)} %w_ref.9), custom_call_target="tpu_custom_call" | custom-call | tf_op jit(solution)/shard_map/pallas_call | solution.py:314
  47.9 8.3 %shard_map.272 = (bf16[256,1024]{1,0:T(8,128)(2,1)}, f32[4,1,1024]{2,1,0:T(1,128)}) custom-call(s32[1024,1]{1,0:T(8,128)} %copy.46.sc_ref, s32[1,1024]{1,0:T(1,128)} %sr_ref.3, bf16[768,1024]{1,0:T(8,128)(2,1)} %get-tuple-element.47.t_ref), custom_call_target="tpu_custom_call" | custom-call | tf_op jit(solution)/shard_map/pallas_call | solution.py:754
  56.2 24.6 %shard_map.273 = (bf16[400,1024]{1,0:T(8,128)(2,1)}, f32[800,256]{1,0:T(8,128)}) custom-call(bf16[256,1024]{1,0:T(8,128)(2,1)} %get-tuple-element.48.h_ref.o_ref, bf16[400,800]{1,0:T(8,128)(2,1)} %w_ref.6), custom_call_target="tpu_custom_call" | custom-call | tf_op jit(solution)/shard_map/pallas_call | solution.py:614
  80.8 22.3 %shard_map.274 = (bf16[800,1024]{1,0:T(8,128)(2,1)}, f32[800,1024]{1,0:T(8,128)}) custom-call(bf16[800,256]{1,0:T(8,128)(2,1)} %bitcast.36, bf16[800,1600]{1,0:T(8,128)(2,1)} %bitcast.30), custom_call_target="tpu_custom_call" | custom-call | tf_op jit(solution)/shard_map/pallas_call | solution.py:347
  103.1 30.4 %shard_map.275 = (bf16[800,1024]{1,0:T(8,128)(2,1)}, bf16[1600,1024]{1,0:T(8,128)(2,1)}, bf16[1600,1024]{1,0:T(8,128)(2,1)}, f32[800,256]{1,0:T(8,128)}, f32[8,256]{1,0:T(8,128)}, /*index=5*/f32[8,800]{1,0:T(8,128)}) custom-call(bf16[800,256]{1,0:T(8,128)(2,1)} %bitcast.33, f32[800,256]{1,0:T(8,128)} %get-tuple-element.49.p_ref, f32[800,6]{1,0:T(8,128)} %bitcast.25, ...), custom_call_target="tpu_custom_call" | custom-call | tf_op jit(solution)/shard_map/pallas_call | solution.py:411
  133.5 5.6 %convolution_convert_fusion = bf16[1600,800]{0,1:T(8,128)(2,1)S(1)} fusion(bf16[1600,1024]{1,0:T(8,128)(2,1)} %get-tuple-element.70.l_ref, bf16[800,1024]{1,0:T(8,128)(2,1)} %get-tuple-element.54), kind=kOutput, calls=%fused_computation | convolution fusion | flops 2622720000 | bytes 7475200 | tf_op jit(solution)/shard_map/dot_general | solution.py:917
  139.1 3.6 %copy.50 = bf16[1600,800]{1,0:T(8,128)(2,1)} copy(bf16[1600,800]{0,1:T(8,128)(2,1)S(1)} %convolution_convert_fusion) | data formatting | bytes 5120000 | tf_op jit(solution)/shard_map/optimization_barrier | solution.py:925
  142.7 1.0 copy-done.2
  143.7 0.3 copy.48
  144.0 1.0 slice.92
  145.0 3.4 collective-permute-start
  148.4 4.4 %convolution_convert_fusion.3 = bf16[800,800]{1,0:T(8,128)(2,1)S(1)} fusion(bf16[800,1024]{1,0:T(8,128)(2,1)} %get-tuple-element.60, bf16[1600,1024]{1,0:T(8,128)(2,1)} %get-tuple-element.55.l_ref), kind=kOutput, calls=%fused_computation.4 | convolution fusion | flops 1311360000 | bytes 4556800 | tf_op jit(solution)/shard_map/dot_general | solution.py:917
  152.8 3.0 convolution_convert_fusion.2
  155.8 19.6 %shard_map.276.s_ref = f32[800,256]{1,0:T(8,128)} custom-call(bf16[1600,1024]{1,0:T(8,128)(2,1)} %get-tuple-element.55.l_ref, bf16[800,1600]{1,0:T(8,128)(2,1)} %w_ref.8), custom_call_target="tpu_custom_call" | custom-call | tf_op jit(solution)/shard_map/pallas_call | solution.py:542
  175.3 1.0 copy.51
  176.3 1.8 copy.52
  178.2 2.7 maximum_bitcast_fusion.w_ref
  180.9 24.9 %shard_map.277 = (bf16[800,1024]{1,0:T(8,128)(2,1)}, bf16[256,1024]{1,0:T(8,128)(2,1)}, f32[800,256]{1,0:T(8,128)}, f32[8,800]{1,0:T(8,128)}) custom-call(f32[800,256]{1,0:T(8,128)} %shard_map.276.s_ref, f32[800,256]{1,0:T(8,128)} %get-tuple-element.56.m_ref, f32[8,256]{1,0:T(8,128)} %get-tuple-element.57.st_ref, bf16[800,256]{1,0:T(8,128)(2,1)} %bitcast.37, ...), custom_call_target="tpu_custom_call" | custom-call | tf_op jit(solution)/shard_map/pallas_call | solution.py:452
  205.7 3.6 %convolution_convert_fusion.4 = bf16[400,800]{1,0:T(8,128)(2,1)} fusion(bf16[400,1024]{1,0:T(8,128)(2,1)} %get-tuple-element.61, bf16[800,1024]{1,0:T(8,128)(2,1)} %get-tuple-element.62), kind=kOutput, calls=%fused_computation.7 | convolution fusion | flops 655680000 | bytes 3097600 | tf_op jit(solution)/shard_map/dot_general | solution.py:917
  209.3 2.1 reshape.132
  211.5 2.4 copy.53
  213.8 4.4 %pad_maximum_fusion = bf16[4,500,800]{1,2,0:T(8,128)(2,1)} fusion(bf16[4,100,800]{1,2,0:T(8,128)(2,1)} %copy.53, bf16[4,200,800]{1,2,0:T(8,128)(2,1)S(1)} %copy.52, bf16[4,200,800]{1,2,0:T(8,128)(2,1)S(1)} %copy.51), kind=kLoop, calls=%fused_computation.2 | loop fusion | flops 9600000 | bytes 6400000 | tf_op jit(solution)/shard_map/concatenate | solution.py:947
  218.3 11.5 %shard_map.278.h_ref = bf16[768,1024]{1,0:T(8,128)(2,1)} custom-call(s32[1024,1]{1,0:T(8,128)} %copy.46.sc_ref, s32[1,1024]{1,0:T(1,128)} %sr_ref.3, bf16[768,1024]{1,0:T(8,128)(2,1)} %get-tuple-element.47.t_ref, bf16[256,1024]{1,0:T(8,128)(2,1)} %get-tuple-element.48.h_ref.o_ref, bf16[256,1024]{1,0:T(8,128)(2,1)} %get-tuple-element.63.g_ref, ...), custom_call_target="tpu_custom_call" | custom-call | tf_op jit(solution)/shard_map/pallas_call | solution.py:807
  229.8 41.5 %shard_map.279 = (bf16[1200,1024]{1,0:T(8,128)(2,1)}, f32[800,256]{1,0:T(8,128)}, f32[8,800]{1,0:T(8,128)}, f32[8,1200]{1,0:T(8,128)}) custom-call(bf16[768,1024]{1,0:T(8,128)(2,1)} %shard_map.278.h_ref, bf16[800,1200]{1,0:T(8,128)(2,1)} %w_ref.9, bf16[800,256]{1,0:T(8,128)(2,1)} %bitcast.34, f32[8,256]{1,0:T(8,128)} %get-tuple-element.65.st_ref, ...), custom_call_target="tpu_custom_call" | custom-call | tf_op jit(solution)/shard_map/pallas_call | solution.py:705
  271.3 5.3 %convolution_convert_fusion.1 = bf16[800,1200]{1,0:T(8,128)(2,1)} fusion(bf16[800,1024]{1,0:T(8,128)(2,1)S(1)} %copy-done.9, bf16[1200,1024]{1,0:T(8,128)(2,1)} %get-tuple-element.67), kind=kOutput, calls=%fused_computation.1 | convolution fusion | flops 1967040000 | bytes 6016000 | tf_op jit(solution)/shard_map/dot_general | solution.py:917
  276.7 2.6 reduce-scatter.6.cloned.1.call-done
  279.3 0.8 slice_reduce_fusion.1
  280.4 0.8 slice_reduce_fusion
  281.4 1.2 convert_element_type.69
  282.6 0.2 fusion.3
  282.9 1.6 copy.56
  284.4 0.8 slice.76
  285.4 0.7 fusion.2.x_ref
  286.0 22.3 %shard_map.281 = f32[32,8,128]{2,1,0:T(8,128)} custom-call(f32[32,8,128]{2,1,0:T(8,128)} %fusion.2.x_ref), custom_call_target="tpu_custom_call" | custom-call | tf_op jit(solution)/shard_map/pallas_call | solution.py:871
  308.3 1.4 slice.100
  309.7 22.2 %shard_map.280 = bf16[800,256]{1,0:T(8,128)(2,1)} custom-call(bf16[1600,1024]{1,0:T(8,128)(2,1)} %get-tuple-element.70.l_ref, bf16[800,1600]{1,0:T(8,128)(2,1)} %bitcast.31, f32[800,256]{1,0:T(8,128)} %get-tuple-element.56.m_ref, f32[800,6]{1,0:T(8,128)} %bitcast.28), custom_call_target="tpu_custom_call" | custom-call | tf_op jit(solution)/shard_map/pallas_call | solution.py:558
  332.1 1.2 copy.55
  333.3 0.7 fusion.4
  334.0 2.1 convert_element_type.66
  336.0 0.8 copy.60
  336.8 0.9 copy.61
  (49 shorter events, 1.3 us)
Async XLA Ops:
  7.2 211.1 %reduce-scatter.4.cloned.1.call-start = ((), (), s32[]{:S(2)}) async-start(), calls=%async_computation.3 | async-start | bytes 3584000 | tf_op jit(solution)/shard_map/reduce_scatter | solution.py:921
  142.6 1.1 copy-start.2
  142.6 136.7 %reduce-scatter.6.cloned.1.call-start = ((), (), s32[]{:S(2)}) async-start(), calls=%async_computation.4 | async-start | bytes 4096000 | tf_op jit(solution)/shard_map/reduce_scatter | solution.py:921
  144.0 8.7 %copy-start = (bf16[400,800]{0,1:T(8,128)(2,1)}, bf16[400,800]{0,1:T(8,128)(2,1)S(1)}, u32[]{:S(2)}) copy-start(bf16[400,800]{0,1:T(8,128)(2,1)S(1)} %copy.48) | copy-start | bytes 1920004
  145.0 33.2 %collective-permute-start = (bf16[48,800]{0,1:T(8,128)(2,1)}, bf16[48,800]{0,1:T(8,128)(2,1)S(1)}, u32[]{:S(2)}, u32[]{:S(2)}) collective-permute-start(bf16[48,800]{0,1:T(8,128)(2,1)} %slice.92), channel_id=1, source_target_pairs={{0,2},{2,4},{4,6},{1,3},{3,5},{5,7},{8,10},{10,12},{12,14},{9,11},... | collective-permute-start | bytes 230408 | tf_op jit(solution)/shard_map/ppermute | solution.py:931
  148.4 4.4 %copy-start.1 = (bf16[1600,1024]{1,0:T(8,128)(2,1)S(1)}, bf16[1600,1024]{1,0:T(8,128)(2,1)}, u32[]{:S(2)}) copy-start(bf16[1600,1024]{1,0:T(8,128)(2,1)} %get-tuple-element.55.l_ref) | copy-start | bytes 9830404
  148.4 4.4 %copy-start.10 = (bf16[800,1024]{1,0:T(8,128)(2,1)S(1)}, bf16[800,1024]{1,0:T(8,128)(2,1)}, u32[]{:S(2)}) copy-start(bf16[800,1024]{1,0:T(8,128)(2,1)} %get-tuple-element.60) | copy-start | bytes 4915204
  218.3 115.7 %reduce-scatter.8.cloned.1.call-start = ((), (), s32[]{:S(2)}) async-start(), calls=%async_computation.5 | async-start | bytes 2560000 | tf_op jit(solution)/shard_map/reduce_scatter | solution.py:921
  229.8 41.5 %copy-start.9 = (bf16[800,1024]{1,0:T(8,128)(2,1)S(1)}, bf16[800,1024]{1,0:T(8,128)(2,1)}, u32[]{:S(2)}) copy-start(bf16[800,1024]{1,0:T(8,128)(2,1)} %get-tuple-element.52) | copy-start | bytes 4915204
  276.7 3.7 %copy-start.8 = (f32[8,800]{1,0:T(8,128)S(1)}, f32[8,800]{1,0:T(8,128)}, u32[]{:S(2)}) copy-start(f32[8,800]{1,0:T(8,128)} %get-tuple-element.73) | copy-start | bytes 76804
  276.7 4.7 %copy-start.6 = (bf16[1,400,800]{2,1,0:T(8,128)(2,1)S(1)}, bf16[1,400,800]{2,1,0:T(8,128)(2,1)}, u32[]{:S(2)}) copy-start(bf16[1,400,800]{2,1,0:T(8,128)(2,1)} %reduce-scatter.4.cloned.1.call-done) | copy-start | bytes 1920004
  279.3 3.3 copy-start.4
  309.7 23.6 %copy-start.7 = (f32[32,8,128]{2,1,0:T(8,128)S(1)}, f32[32,8,128]{2,1,0:T(8,128)}, u32[]{:S(2)}) copy-start(f32[32,8,128]{2,1,0:T(8,128)} %shard_map.281) | copy-start | bytes 393220
  331.9 4.1 %copy-start.3 = (bf16[800,256]{1,0:T(8,128)(2,1)S(1)}, bf16[800,256]{1,0:T(8,128)(2,1)}, u32[]{:S(2)}) copy-start(bf16[800,256]{1,0:T(8,128)(2,1)} %shard_map.280) | copy-start | bytes 1228804
  331.9 4.9 %copy-start.5 = (f32[800,256]{1,0:T(8,128)S(1)}, f32[800,256]{1,0:T(8,128)}, u32[]{:S(2)}) copy-start(f32[800,256]{1,0:T(8,128)} %get-tuple-element.71) | copy-start | bytes 2457604
Sparse Core Ops, SparseCore 0:
  142.8 54.6 reduce-scatter.3
  218.4 60.8 reduce-scatter.5
  281.6 46.7 reduce-scatter.7

commit v3 on v2

--- a/solution.py
+++ b/solution.py
@@ -145,35 +145,47 @@
     return rstd * (scaled - total / width - hat * mixed / width)
 
 
-def gather_scratch(rows, cols, feats, turned):
+def weight_scratch(rows, feats, turned):
+    return [
+        pltpu.VMEM((rows, turned), BF16), pltpu.VMEM((turned, rows), BF16),
+        pltpu.VMEM((feats, rows), BF16), DMA((3,)),
+    ]
+
+
+def gather_scratch(rows, cols):
     count = len(chunks(rows))
     return [
         pltpu.VMEM((2, 4, rows, cols), BF16), DMA((7, count)), DMA((2, 4, count)), DMA((4,)),
-        pltpu.VMEM((rows, turned), BF16), pltpu.VMEM((turned, rows), BF16),
-        pltpu.VMEM((feats, rows), BF16), DMA((3,)),
     ]
 
 
+class PairWeight:
+    def __init__(self, place, w_ref, step, refs):
+        self.flat, self.turned, self.other, sems = refs
+        self.load = pltpu.make_async_copy(w_ref, self.flat, sems.at[2])
+        self.load.start()
+        feats = self.other.shape[0]
+        self.own = self.turned.at[pl.ds(pl.multiple_of(step * place.c, GRAIN), feats)]
+        theirs = self.turned.at[
+            pl.ds(pl.multiple_of(step * (1 - place.c), GRAIN), feats)
+        ]
+        self.copy = rcopy(theirs, self.other, sems.at[0], sems.at[1], place.mate())
+
+    def share(self):
+        self.load.wait()
+        self.turned[...] = self.flat[...].T
+        self.copy.start()
+
+    def product(self, own, other):
+        return dot(self.own[...], own, NN) + dot(self.other[...], other, NN)
+
+
 class Gather:
-    def __init__(self, place, all_ref, w_ref, w_step, refs):
+    def __init__(self, place, all_ref, refs):
         self.place, self.all_ref = place, all_ref
-        self.got, self.send, self.recv, self.out_sem = refs[:4]
-        self.w_flat, self.turned, self.w_oth, w_sem = refs[4:]
-        self.w_load = pltpu.make_async_copy(w_ref, self.w_flat, w_sem.at[2])
-        self.w_load.start()
-        feats = self.w_oth.shape[0]
-        start = w_step[0] + w_step[1] * place.c
-        other = w_step[0] + w_step[1] * (1 - place.c)
-        self.w_own = self.turned.at[pl.ds(pl.multiple_of(start, GRAIN), feats)]
-        theirs = self.turned.at[pl.ds(pl.multiple_of(other, GRAIN), feats)]
-        self.w_copy = rcopy(theirs, self.w_oth, w_sem.at[0], w_sem.at[1], place.mate())
-
-    def product(self, slot):
-        return dot(self.w_own[...], self.got[0, slot], NN) + dot(
-            self.w_oth[...], self.got[1, slot], NN
-        )
-
-    def run(self, work, idle=None):
+        self.got, self.send, self.recv, self.out_sem = refs
+
+    def run(self, work, idle):
         place, got, send, recv = self.place, self.got, self.send, self.recv
         mate, size = place.mate(), got.shape[3]
         parts = list(enumerate(chunks(got.shape[2])))
@@ -206,12 +218,7 @@
             for copy in copies:
                 copy.start()
         kept = [keep(0, place.r, 0)]
-        self.w_load.wait()
-        self.turned[...] = self.w_flat[...].T
-        self.w_copy.start()
-        if idle is not None:
-            idle()
-        self.w_copy.wait()
+        idle()
         for copy in to_mate:
             copy.wait_recv()
         work(0, place.r)
@@ -255,7 +262,8 @@
         place = Place()
         place.barrier(place.group())
         me = 2 * place.r + place.c
-        gather = Gather(place, all_ref, w_ref, (0, shift), refs)
+        weight = PairWeight(place, w_ref, shift, refs[:4])
+        gather = Gather(place, all_ref, refs[4:])
         wide = x_ref[...].astype(F32)
         average, rstd = moments(Totals(place, tb, ts), wide, width)
         keep_moments(st_ref, average, rstd)
@@ -271,7 +279,8 @@
             return owner, pl.ds(pl.multiple_of(row, GRAIN), GRAIN)
 
         def work(slot, row):
-            tt[:, lanes(row, size)] = (gather.product(slot) + b_ref[...]).astype(BF16)
+            total = weight.product(gather.got[0, slot], gather.got[1, slot])
+            tt[:, lanes(row, size)] = (total + b_ref[...]).astype(BF16)
 
             def send_grain(j, carry):
                 owner, place_rows = target(j)
@@ -290,7 +299,11 @@
 
             lax.fori_loop(place.c, grains, send_grain, 0)
 
-        gather.run(work)
+        def idle():
+            weight.share()
+            weight.copy.wait()
+
+        gather.run(work, idle)
 
         def drain(j, carry):
             @pl.when(target(j)[0] != me)
@@ -316,57 +329,30 @@
         (struct((rows, 4 * size), BF16), struct((4 * per, 4 * size), BF16), struct((8, size), F32)),
         (ANY, ANY, VM), [VM] * 3 + [ANY],
         [pltpu.VMEM((feats, 4 * size), BF16)] + Totals.scratch + [DMA, DMA]
-        + gather_scratch(rows, size, feats, triple_width), cid,
+        + weight_scratch(rows, feats, triple_width) + gather_scratch(rows, size), cid,
     )(tokens, cols, bias, weight)
 
 
-def gather_cotangent(cot, weight, cid):
-    rows, size = cot.shape
-    feats = weight.shape[1] // 2
-
-    def kernel(x_ref, w_ref, all_ref, y_ref, y, y_sem, *refs):
-        place = Place()
-        place.barrier(place.square())
-        gather = Gather(place, all_ref, w_ref, (0, feats), refs)
-        gather.got[0, 0] = x_ref[...]
-        pending = []
-
-        def work(slot, row):
-            number = len(pending)
-            y[number] = gather.product(slot)
-            copy = pltpu.make_async_copy(
-                y.at[number], y_ref.at[:, lanes(row, size)], y_sem.at[number]
-            )
-            copy.start()
-            pending.append(copy)
-
-        gather.run(work)
-        for copy in pending:
-            copy.wait()
-
-    return call(
-        kernel, (struct((rows, 4 * size), BF16), struct((feats, 4 * size), F32)),
-        (ANY, ANY), [VM, ANY],
-        [pltpu.VMEM((4, feats, size), F32), DMA((4,))]
-        + gather_scratch(rows, size, feats, 2 * feats), cid,
-    )(cot, weight)
-
-
-def gather_hidden(tokens, proj_out, cols, bias, act_grad, weight, width, cid):
+def gather_hidden(tokens, proj_out, cols, bias, cot, weight, back_weight, width, cid):
     rows, size = tokens.shape
     feats = weight.shape[1] // 2
+    tokens_all = 4 * size
 
     def kernel(
-        t_ref, p_ref, c_ref, b_ref, g_ref, w_ref,
-        all_ref, act_ref, hid_ref, mid_ref, st_ref, sum_ref,
-        act, hid, swap_send, swap_recv, swap_out, grads, g_sem, grad_sum, tb, ts, *refs,
+        t_ref, p_ref, c_ref, b_ref, x_ref, w_ref, v_ref,
+        all_ref, act_ref, hid_ref, mid_ref, st_ref, sum_ref, grad_ref,
+        act, hid, swap_send, swap_recv, swap_out, cots, cot_sems, grads, grad_sum,
+        tb, ts, *refs,
     ):
         place = Place()
+        cot_load = pltpu.make_async_copy(x_ref, cots.at[0], cot_sems.at[2])
+        cot_load.start()
         place.barrier(place.square())
         mate = place.mate()
-        g_load = pltpu.make_async_copy(g_ref, grads, g_sem)
-        g_load.start()
-        gather = Gather(place, all_ref, w_ref, (0, feats), refs)
+        back = PairWeight(place, v_ref, feats, refs[:4])
+        ahead = PairWeight(place, w_ref, feats, refs[4:8])
+        gather = Gather(place, all_ref, refs[8:])
+        cot_swap = rcopy(x_ref, cots.at[1], cot_sems.at[0], cot_sems.at[1], mate)
         middle = t_ref[...].astype(F32) + p_ref[...] + c_ref[:, 2:3]
         mid_ref[...] = middle
         average, rstd = moments(Totals(place, tb, ts), middle, width)
@@ -375,62 +361,117 @@
         pending = []
         mine = pl.ds(pl.multiple_of(place.c * feats, GRAIN), feats)
 
+        def idle():
+            back.share()
+            cot_swap.start()
+            ahead.share()
+            cot_load.wait()
+            back.copy.wait()
+            cot_swap.wait()
+
+            def one(row, carry):
+                grads[row] = back.product(cots[0, row], cots[1, row])
+                return carry
+
+            lax.fori_loop(0, 4, one, 0)
+            ahead.copy.wait()
+
         def work(slot, row):
             number = len(pending)
-            if number == 0:
-                g_load.wait()
-            p = gather.product(slot) + b_ref[...]
+            p = ahead.product(gather.got[0, slot], gather.got[1, slot]) + b_ref[...]
             square = p * p
             t = jnp.tanh(0.7978845608028654 * (p + 0.044715 * (square * p)))
-            act[number] = (0.5 * p * (1.0 + t)).astype(BF16)
+            span = lanes(row, size)
+            act[mine, span] = (0.5 * p * (1.0 + t)).astype(BF16)
             slope = 0.5 * (1.0 + t) + 0.5 * p * (1.0 - t * t) * (
                 0.7978845608028654 * (1.0 + 3.0 * 0.044715 * square)
             )
-            grad = grads[:, lanes(row, size)] * slope
+            grad = grads[row] * slope
             hid[number] = grad.astype(BF16)
-            copies = []
-            for k, (buf, out) in enumerate(((act, act_ref), (hid, hid_ref))):
-                there = out.at[mine, lanes(row, size)]
-                out_copy = pltpu.make_async_copy(buf.at[number], there, swap_out.at[k, number])
-                swap = rcopy(
-                    buf.at[number], there, swap_send.at[k, number], swap_recv.at[k, number], mate
-                )
-                out_copy.start()
-                swap.start()
-                copies += [out_copy, swap]
+            there = hid_ref.at[mine, span]
+            copies = [
+                rcopy(
+                    act.at[mine, span], act.at[mine, span],
+                    swap_send.at[0, number], swap_recv.at[0, number], mate,
+                ),
+                rcopy(
+                    hid.at[number], there, swap_send.at[1, number], swap_recv.at[1, number], mate
+                ),
+                pltpu.make_async_copy(hid.at[number], there, swap_out.at[number]),
+            ]
+            for copy in copies:
+                copy.start()
             grad_sum[...] = grad if number == 0 else grad_sum[...] + grad
             pending.append(copies)
 
-        gather.run(work)
+        gather.run(work, idle)
         sum_ref[0:1] = col_sums(grad_sum[...])
         for copies in pending:
-            for copy in copies:
+            copies[0].wait()
+        act_out = pltpu.make_async_copy(act, act_ref, swap_out.at[4])
+        act_out.start()
+        part = feats // 2
+
+        def some(k, carry):
+            here = pl.ds(pl.multiple_of(k * part, GRAIN), part)
+            total = dot(act[here, 0:size], cots[0, 0], NT)
+            for row in range(1, 4):
+                total += dot(act[here, row * size : (row + 1) * size], cots[0, row], NT)
+            grad_ref[here] = total.astype(BF16)
+            return carry
+
+        lax.fori_loop(0, 4, some, 0)
+        for copies in pending:
+            for copy in copies[1:]:
                 copy.wait()
-
-    full = struct((2 * feats, 4 * size), BF16)
+        act_out.wait()
+
+    full = struct((2 * feats, tokens_all), BF16)
     return call(
         kernel,
         (
-            struct((rows, 4 * size), BF16), full, full, struct((rows, size), F32),
-            struct((8, size), F32), struct((8, feats), F32),
+            struct((rows, tokens_all), BF16), full, full, struct((rows, size), F32),
+            struct((8, size), F32), struct((8, feats), F32), struct((2 * feats, rows), BF16),
         ),
-        (ANY, ANY, ANY, VM, VM, VM), [VM] * 4 + [ANY, ANY],
-        [pltpu.VMEM((4, feats, size), BF16)] * 2 + [DMA((2, 4))] * 3
-        + [pltpu.VMEM((feats, 4 * size), F32), DMA, pltpu.VMEM((feats, size), F32)]
-        + Totals.scratch + gather_scratch(rows, size, feats, 2 * feats), cid,
-    )(tokens, proj_out, cols, bias, act_grad, weight)
-
-
-def gather_middle(grad_in, middle, stats, cot, cols, weight, start, step, width, cid):
+        (ANY, ANY, ANY, VM, VM, VM, VM), [VM] * 4 + [ANY] * 3,
+        [pltpu.VMEM((2 * feats, tokens_all), BF16), pltpu.VMEM((4, feats, size), BF16)]
+        + [DMA((2, 4)), DMA((2, 4)), DMA((5,))]
+        + [pltpu.VMEM((2, 4, rows, size), BF16), DMA((3,))]
+        + [pltpu.VMEM((4, feats, size), F32), pltpu.VMEM((feats, size), F32)]
+        + Totals.scratch + weight_scratch(rows, feats, 2 * feats) * 2
+        + gather_scratch(rows, size), cid,
+    )(tokens, proj_out, cols, bias, cot, weight, back_weight)
+
+
+def gather_middle(grad_in, middle, stats, cot, cols, weight, width, cid):
     rows, size = cot.shape
+    owned = weight.shape[0]
     feats = 4 * HEAD_DIM
+    step = 3 * HEAD_DIM
+    lag = 3 * (owned - 2 * step)
+    whole = lag + owned + 2 * HEAD_DIM
 
     def kernel(
-        s_ref, m_ref, st_ref, x_ref, c_ref, w_ref, all_ref, y_ref, mg_ref, sum_ref, tb, ts, *refs
+        s_ref, m_ref, st_ref, x_ref, c_ref, w_ref, all_ref, y_ref, mg_ref, sum_ref,
+        wide, other, w_sems, tb, ts, *refs,
     ):
         place = Place()
-        place.barrier(place.square())
-        gather = Gather(place, all_ref, w_ref, (start[0] + start[1] * place.r, step), refs)
+        load = pltpu.make_async_copy(w_ref, wide.at[pl.ds(lag, owned)], w_sems.at[0])
+        load.start()
+        place.barrier(place.group())
+        before = rcopy(
+            w_ref.at[pl.ds(owned - lag, lag)], wide.at[pl.ds(0, lag)], w_sems.at[1], w_sems.at[2],
+            place.dev(lax.rem(place.r + 1, 4)),
+        )
+        before.start()
+        wide[lag + owned : whole] = jnp.zeros((2 * HEAD_DIM, rows), BF16)
+        first = lag - (owned - 2 * step) * place.r
+
+        def heads(col):
+            return wide.at[pl.ds(pl.multiple_of(first + step * col, GRAIN), feats)]
+
+        swap = rcopy(heads(1 - place.c), other, w_sems.at[3], w_sems.at[4], place.mate())
+        gather = Gather(place, all_ref, refs)
         rstd = st_ref[1:2]
         hat = (m_ref[...] - st_ref[0:1]) * rstd
         back = norm_back(Totals(place, tb, ts), s_ref[...], hat, rstd, c_ref[:, 3:4], width)
@@ -438,14 +479,20 @@
         gather.got[0, 0] = mg_ref[...].astype(BF16)
 
         def idle():
+            load.wait()
+            before.wait()
+            swap.start()
             hat = (m_ref[...] - st_ref[0:1]) * st_ref[1:2]
             sum_ref[0:1] = col_sums(s_ref[...] * hat)
             sum_ref[1:2] = col_sums(s_ref[...])
             sum_ref[2:3] = col_sums(mg_ref[...])
             sum_ref[3:4] = col_sums(x_ref[...])
+            swap.wait()
 
         def work(slot, row):
-            y_ref[:, lanes(row, size)] = gather.product(slot).astype(BF16)
+            total = dot(heads(place.c)[...], gather.got[0, slot], NN)
+            total += dot(other[...], gather.got[1, slot], NN)
+            y_ref[:, lanes(row, size)] = total.astype(BF16)
 
         gather.run(work, idle)
 
@@ -456,7 +503,8 @@
             struct((rows, size), F32), struct((8, rows), F32),
         ),
         (ANY, VM, VM, VM), [VM] * 5 + [ANY],
-        Totals.scratch + gather_scratch(rows, size, feats, weight.shape[1]), cid,
+        [pltpu.VMEM((whole, rows), BF16), pltpu.VMEM((feats, rows), BF16), DMA((5,))]
+        + Totals.scratch + gather_scratch(rows, size), cid,
     )(grad_in, middle, stats, cot, cols, weight)
 
 
@@ -884,7 +932,6 @@
     row, col = lax.axis_index("row"), lax.axis_index("col")
     col_width = tokens.shape[1]
     triple_width = triple_weight.shape[1]
-    proj_rows = proj_weight.shape[0]
     hidden = expand_weight.shape[1] // 2
     core_feats = (triple_width // GRAIN + 1) // 2 * GRAIN
 
@@ -906,11 +953,15 @@
     first_all, triple, first_stats = gather_triple(
         tokens_t, cols, core_bias, triple_weight, width, core_feats, 0
     )
-    cot_all, act_grad = gather_cotangent(cot_t, shrink_weight.T, 1)
+    triple, cot_later = lax.optimization_barrier((triple, cot_t))
+    cot_rows = lax.all_gather(cot_later, "row")
     attended, lse = attention_forward(triple, seg_col, seg_row)
     attended_all, proj_out = attended_scatter(attended, proj_weight, 2)
-    second_all, act_all, hid_all, middle, second_stats, expand_bias_part = gather_hidden(
-        tokens_t, proj_out, cols, core_expand_bias, act_grad, expand_weight, width, 3
+    (
+        second_all, act_all, hid_all, middle, second_stats, expand_bias_part, shrink_grad
+    ) = gather_hidden(
+        tokens_t, proj_out, cols, core_expand_bias, cot_rows, expand_weight, shrink_weight.T,
+        width, 3,
     )
 
     def product(left, right):
@@ -921,22 +972,11 @@
         summed = lax.psum_scatter(parts, "dp", scatter_dimension=0, tiled=True)
         return summed.reshape(1, -1, grad.shape[1])
 
-    shrink_grad = product(act_all, cot_all)
-    hid_all, shrink_grad = lax.optimization_barrier((hid_all, shrink_grad))
     shrink_owned = owned(shrink_grad)
 
     second_normed_grad = hidden_scatter(hid_all, expand_weight, 4)
-    head_rows = 3 * HEAD_DIM
-    lag = (row_count - 1) * (proj_rows - 2 * head_rows)
-    before = lax.ppermute(
-        proj_weight[proj_rows - lag :], "row", [(i, i + 1) for i in range(row_count - 1)]
-    )
-    padded = jnp.concatenate(
-        [before, proj_weight, jnp.zeros((2 * HEAD_DIM, col_width), BF16)], axis=0
-    )
     middle_all, attended_grad, middle_grad, second_sums = gather_middle(
-        second_normed_grad, middle, second_stats, cot_t, cols, padded.T,
-        (lag, 2 * head_rows - proj_rows), head_rows, width, 5,
+        second_normed_grad, middle, second_stats, cot_t, cols, proj_weight, width, 5
     )
     proj_grad = product(attended_all, middle_all)
     pieces = [
@@ -944,9 +984,10 @@
         product(second_all, hid_all[hidden:]),
         proj_grad,
     ]
-    both_grad = jnp.concatenate(
-        [piece.reshape(dp_count, -1, piece.shape[1]) for piece in pieces], axis=1
-    )
+    pieces = [piece.reshape(dp_count, -1, col_width) for piece in pieces]
+    joint = sum(piece.shape[1] for piece in pieces)
+    pieces.append(jnp.zeros((dp_count, -joint % 32, col_width), BF16))
+    both_grad = jnp.concatenate(pieces, axis=1)
     attended_grad, shrink_owned, both_grad = lax.optimization_barrier(
         (attended_grad, shrink_owned, both_grad)
     )
@@ -963,7 +1004,7 @@
     )
     part = col_width // dp_count
     expand_owned = jnp.concatenate([both_owned[:, :part], both_owned[:, part : 2 * part]], axis=2)
-    proj_owned = both_owned[:, 2 * part :]
+    proj_owned = both_owned[:, 2 * part : joint]
     triple_owned = owned(triple_grad)
     block_out = output_scatter(act_all, shrink_weight.T, middle, cols, 7)
 

time: 352 us -> 324 us (0.920)
  local copies, waits for them, and re-layouts: 29.6 us -> 17 us
  matrix products: 21.9 us -> 14.5 us
  waiting for transfers between devices: 2.69 us -> 9.31 us
  Pallas kernels: 261 us -> 257 us
  other arithmetic: 11.5 us -> 7.77 us
    pallas_call x2 -> x1, Pallas kernels: 52.7 us -> 38.2 us  [gather_hidden(): call(kernel, (struct((rows, tokens_all), BF16), full, full, struct((rows,...]
    pallas_call x1, Pallas kernels: 24.6 us -> 33.3 us  [attended_scatter(): call(kernel, (struct((feats, tokens), BF16), struct((rows, size), F32)),...]
    dot_general x5 -> x4, matrix products: 21.9 us -> 14.5 us  [product(): lax.dot_general(left, right, NT, preferred_element_type=F32).astype(BF16)]
    reduce_scatter x3, waiting for transfers between devices: 2.64 us -> 9.22 us  [owned(): summed = lax.psum_scatter(parts, 'dp', scatter_dimension=0, tiled=True)]
    reshape x4 -> x1, local copies, waits for them, and re-layouts: 7.25 us -> 2.13 us  [shards(): pieces = [piece.reshape(dp_count, -1, col_width) for piece in pieces]]
    optimization_barrier x1 -> x0, local copies, waits for them, and re-layouts: 3.55 us -> none  [shards(): hid_all, shrink_grad = lax.optimization_barrier((hid_all, shrink_grad))]
  transfers between devices with their start and end apart: 4 -> 4, of which waited for: 1 -> 1; matrix products, arithmetic and copies ran while one was open for 12% -> 10% of each run, Pallas kernels for 41% -> 58%
where the time goes in v3:
time: 324 us; the launch traced here: 320 us
  Pallas kernels  257 us (79%)
  local copies, waits for them, and re-layouts  17 us (5%)
  matrix products  14.5 us (4%)
  between operations  14.3 us (4%)
  waiting for transfers between devices  9.31 us (3%)
  other arithmetic  7.77 us (2%)
    pallas_call x1, Pallas kernels, triple_scatter(): call(kernel, (struct((feats, count_tokens), BF16), struct((rows, size), F...  40.5 us
    pallas_call x1, Pallas kernels, gather_hidden(): call(kernel, (struct((rows, tokens_all), BF16), full, full, struct((rows,...  38.2 us
    pallas_call x1, Pallas kernels, gather_triple(): call(kernel, (struct((rows, 4 * size), BF16), struct((4 * per, 4 * size),...  33.5 us
    pallas_call x1, Pallas kernels, attended_scatter(): call(kernel, (struct((feats, tokens), BF16), struct((rows, size), F32)),...  33.3 us
    pallas_call x1, Pallas kernels, gather_middle(): call(kernel, (struct((rows, 4 * size), BF16), struct((feats, 4 * size), B...  24.9 us
    pallas_call x1, Pallas kernels, sum_all(): call(kernel, jax.ShapeDtypeStruct(pieces.shape, F32), VM, [VM], [pltpu.VM...  24.2 us
    pallas_call x1, Pallas kernels, output_scatter(): call(kernel, struct((rows, size), BF16), VM, [ANY, ANY, VM, VM], load_scr...  21.7 us
    pallas_call x1, Pallas kernels, hidden_scatter(): call(kernel, struct((rows, size), F32), VM, [ANY] * 2, load_scratch(weigh...  20.7 us
  transfers between devices with their start and end apart: 4, of which 1 were waited for; matrix products, arithmetic and copies ran while one was open for 10% of the time, Pallas kernels for 58%

profile of v3, /device:TPU:25, one launch (start us, length us, event | category | flops | bytes accessed | tf_op | source)
XLA Modules:
  0.0 319.8 jit_solution(16832305272544433512)
XLA Ops:
  7.2 0.9 concatenate.26
  8.1 0.1 reshape.128
  8.2 0.8 concatenate.27
  9.0 0.1 dynamic_slice.10
  9.1 0.9 broadcast_in_dim.20.b_ref
  9.9 0.1 constant_dynamic-slice_fusion
  10.0 0.9 copy.38
  11.0 33.5 %shard_map.271 = (bf16[800,1024]{1,0:T(8,128)(2,1)}, bf16[768,1024]{1,0:T(8,128)(2,1)}, f32[8,256]{1,0:T(8,128)}) custom-call(bf16[800,256]{1,0:T(8,128)(2,1)} %bitcast.28, f32[800,6]{1,0:T(8,128)} %bitcast.21, f32[608,1]{1,0:T(8,128)} %broadcast_in_dim.20.b_ref, bf16[800,1200]{1,0:T(8,128)(2,1)} %w_ref.11), custom_call_target="tpu_custom_call" | custom-call | tf_op jit(solution)/shard_map/pallas_call | solution.py:327
  44.6 0.8 dynamic_slice.11
  45.3 0.9 broadcast_in_dim.21.b_ref
  46.3 1.0 copy.34.sc_ref
  47.3 8.5 %shard_map.272 = (bf16[256,1024]{1,0:T(8,128)(2,1)}, f32[4,1,1024]{2,1,0:T(1,128)}) custom-call(s32[1024,1]{1,0:T(8,128)} %copy.34.sc_ref, s32[1,1024]{1,0:T(1,128)} %sr_ref.3, bf16[768,1024]{1,0:T(8,128)(2,1)} %get-tuple-element.47.t_ref), custom_call_target="tpu_custom_call" | custom-call | tf_op jit(solution)/shard_map/pallas_call | solution.py:802
  55.8 33.3 %shard_map.273 = (bf16[400,1024]{1,0:T(8,128)(2,1)}, f32[800,256]{1,0:T(8,128)}) custom-call(bf16[256,1024]{1,0:T(8,128)(2,1)} %get-tuple-element.48.h_ref.o_ref, bf16[400,800]{1,0:T(8,128)(2,1)} %w_ref.10), custom_call_target="tpu_custom_call" | custom-call | tf_op jit(solution)/shard_map/pallas_call | solution.py:662
  89.1 38.2 %shard_map.274 = (bf16[800,1024]{1,0:T(8,128)(2,1)}, bf16[1600,1024]{1,0:T(8,128)(2,1)}, bf16[1600,1024]{1,0:T(8,128)(2,1)}, f32[800,256]{1,0:T(8,128)}, f32[8,2...) custom-call(bf16[800,256]{1,0:T(8,128)(2,1)} %bitcast.29, f32[800,256]{1,0:T(8,128)} %get-tuple-element.49.p_ref, ...), custom_call_target="tpu_custom_call" | custom-call | tf_op jit(solution)/shard_map/pallas_call | solution.py:430
  127.4 0.1 pad.15.clone
  127.5 20.7 %shard_map.275.s_ref = f32[800,256]{1,0:T(8,128)} custom-call(bf16[1600,1024]{1,0:T(8,128)(2,1)} %get-tuple-element.53.l_ref, bf16[800,1600]{1,0:T(8,128)(2,1)} %w_ref.9), custom_call_target="tpu_custom_call" | custom-call | tf_op jit(solution)/shard_map/pallas_call | solution.py:590
  148.1 24.9 %shard_map.276 = (bf16[800,1024]{1,0:T(8,128)(2,1)}, bf16[256,1024]{1,0:T(8,128)(2,1)}, f32[800,256]{1,0:T(8,128)}, f32[8,800]{1,0:T(8,128)}) custom-call(f32[800,256]{1,0:T(8,128)} %shard_map.275.s_ref, f32[800,256]{1,0:T(8,128)} %get-tuple-element.54.m_ref, f32[8,256]{1,0:T(8,128)} %get-tuple-element.55.st_ref, bf16[800,256]{1,0:T(8,128)(2,1)} %bitcast.34, ...), custom_call_target="tpu_custom_call" | custom-call | tf_op jit(solution)/shard_map/pallas_call | solution.py:499
  173.0 3.8 %convolution_convert_fusion.3 = bf16[400,800]{1,0:T(8,128)(2,1)} fusion(bf16[400,1024]{1,0:T(8,128)(2,1)} %get-tuple-element.59, bf16[800,1024]{1,0:T(8,128)(2,1)} %get-tuple-element.60), kind=kOutput, calls=%fused_computation.6 | convolution fusion | flops 655680000 | bytes 3097600 | tf_op jit(solution)/shard_map/dot_general | solution.py:968
  176.8 2.1 reshape.132
  179.0 3.4 %convolution_convert_fusion.1 = bf16[800,800]{1,0:T(8,128)(2,1)S(1)} fusion(bf16[800,1024]{1,0:T(8,128)(2,1)} %get-tuple-element.58, bf16[1600,1024]{1,0:T(8,128)(2,1)S(1)} %copy-done), kind=kOutput, calls=%fused_computation.2 | convolution fusion | flops 1311360000 | bytes 4556800 | tf_op jit(solution)/shard_map/dot_general | solution.py:968
  182.4 1.9 convolution_convert_fusion.2
  184.4 2.2 maximum_maximum_fusion
  186.7 0.2 reduce-scatter.8.cloned.1.call-start
  186.9 11.2 %shard_map.277.h_ref = bf16[768,1024]{1,0:T(8,128)(2,1)} custom-call(s32[1024,1]{1,0:T(8,128)} %copy.34.sc_ref, s32[1,1024]{1,0:T(1,128)} %sr_ref.3, bf16[768,1024]{1,0:T(8,128)(2,1)} %get-tuple-element.47.t_ref, bf16[256,1024]{1,0:T(8,128)(2,1)} %get-tuple-element.48.h_ref.o_ref, bf16[256,1024]{1,0:T(8,128)(2,1)} %get-tuple-element.61.g_ref, ...), custom_call_target="tpu_custom_call" | custom-call | tf_op jit(solution)/shard_map/pallas_call | solution.py:855
  198.1 40.5 %shard_map.278 = (bf16[1200,1024]{1,0:T(8,128)(2,1)}, f32[800,256]{1,0:T(8,128)}, f32[8,800]{1,0:T(8,128)}, f32[8,1200]{1,0:T(8,128)}) custom-call(bf16[768,1024]{1,0:T(8,128)(2,1)} %shard_map.277.h_ref, bf16[800,1200]{1,0:T(8,128)(2,1)} %w_ref.11, bf16[800,256]{1,0:T(8,128)(2,1)} %bitcast.30, f32[8,256]{1,0:T(8,128)} %get-tuple-element.63.st_ref, ...), custom_call_target="tpu_custom_call" | custom-call | tf_op jit(solution)/shard_map/pallas_call | solution.py:753
  238.7 5.3 %convolution_convert_fusion = bf16[800,1200]{1,0:T(8,128)(2,1)} fusion(bf16[800,1024]{1,0:T(8,128)(2,1)S(1)} %copy-done.8, bf16[1200,1024]{1,0:T(8,128)(2,1)} %get-tuple-element.65), kind=kOutput, calls=%fused_computation.1 | convolution fusion | flops 1967040000 | bytes 6016000 | tf_op jit(solution)/shard_map/dot_general | solution.py:968
  244.0 9.2 %reduce-scatter.6.cloned.1.call-done = bf16[1,512,800]{2,1,0:T(8,128)(2,1)} async-done(((bf16[4,512,800]{2,1,0:T(8,128)(2,1)}), bf16[1,512,800]{2,1,0:T(8,128)(2,1)}) %reduce-scatter.6.cloned.1.call-update) | async-done | bytes 819216 | tf_op jit(solution)/shard_map/reduce_scatter | solution.py:972
  253.3 0.8 slice_reduce_fusion.1
  254.0 0.1 broadcast_multiply_fusion.1
  254.1 0.1 mul.84
  254.2 0.8 slice_reduce_fusion
  255.0 0.1 broadcast_multiply_fusion.2
  255.1 0.1 mul.89
  255.2 1.2 convert_element_type.65
  256.4 21.7 %shard_map.279 = bf16[800,256]{1,0:T(8,128)(2,1)} custom-call(bf16[1600,1024]{1,0:T(8,128)(2,1)} %get-tuple-element.68.l_ref, bf16[800,1600]{1,0:T(8,128)(2,1)} %bitcast.27, f32[800,256]{1,0:T(8,128)} %get-tuple-element.54.m_ref, f32[800,6]{1,0:T(8,128)} %bitcast.25), custom_call_target="tpu_custom_call" | custom-call | tf_op jit(solution)/shard_map/pallas_call | solution.py:606
  278.1 0.8 slice.72
  278.9 0.1 broadcast_multiply_fusion
  279.0 0.1 mul.79
  279.1 0.7 fusion.2.x_ref
  279.7 24.2 %shard_map.280 = f32[32,8,128]{2,1,0:T(8,128)} custom-call(f32[32,8,128]{2,1,0:T(8,128)} %fusion.2.x_ref), custom_call_target="tpu_custom_call" | custom-call | tf_op jit(solution)/shard_map/pallas_call | solution.py:919
  303.9 1.4 slice.95
  305.3 1.1 copy.37
  306.4 1.5 fusion.4
  308.0 0.1 fusion.3
  308.0 1.2 maximum_convert_fusion
  309.3 2.1 convert_element_type.62
  311.4 0.8 copy.41
  312.2 0.9 copy.42
  (38 shorter events, 0.3 us)
Async XLA Ops:
  7.2 81.9 %all-gather.3.cloned.1.call-start = ((), (), s32[]{:S(2)}) async-start(), calls=%async_computation.6 | async-start | bytes 2048000 | tf_op jit(solution)/shard_map/all_gather | solution.py:957
  11.0 35.3 %copy-start.6 = (s32[1,1024]{1,0:T(1,128)S(1)}, s32[1,1024]{1,0:T(1,128)}, u32[]{:S(2)}) copy-start(s32[1,1024]{1,0:T(1,128)} %sr_ref.3) | copy-start | bytes 12292
  44.5 142.1 %reduce-scatter.4.cloned.1.call-start = ((), (), s32[]{:S(2)}) async-start(), calls=%async_computation.3 | async-start | bytes 3584000 | tf_op jit(solution)/shard_map/reduce_scatter | solution.py:972
  127.3 125.9 %reduce-scatter.6.cloned.1.call-start = ((), (), s32[]{:S(2)}) async-start(), calls=%async_computation.4 | async-start | bytes 4587520 | tf_op jit(solution)/shard_map/reduce_scatter | solution.py:972
  173.0 5.9 %copy-start = (bf16[1600,1024]{1,0:T(8,128)(2,1)S(1)}, bf16[1600,1024]{1,0:T(8,128)(2,1)}, u32[]{:S(2)}) copy-start(bf16[1600,1024]{1,0:T(8,128)(2,1)} %get-tuple-element.53.l_ref) | copy-start | bytes 9830404
  179.0 3.5 %copy-start.9 = (bf16[800,1024]{1,0:T(8,128)(2,1)S(1)}, bf16[800,1024]{1,0:T(8,128)(2,1)}, u32[]{:S(2)}) copy-start(bf16[800,1024]{1,0:T(8,128)(2,1)} %get-tuple-element.58) | copy-start | bytes 4915204
  182.4 2.0 copy-start.1
  186.7 122.6 %reduce-scatter.8.cloned.1.call-start = ((), (), s32[]{:S(2)}) async-start(), calls=%async_computation.5 | async-start | bytes 2560000 | tf_op jit(solution)/shard_map/reduce_scatter | solution.py:972
  198.1 40.5 %copy-start.8 = (bf16[800,1024]{1,0:T(8,128)(2,1)S(1)}, bf16[800,1024]{1,0:T(8,128)(2,1)}, u32[]{:S(2)}) copy-start(bf16[800,1024]{1,0:T(8,128)(2,1)} %get-tuple-element.52) | copy-start | bytes 4915204
  244.0 10.2 %copy-start.7 = (f32[8,800]{1,0:T(8,128)S(1)}, f32[8,800]{1,0:T(8,128)}, u32[]{:S(2)}) copy-start(f32[8,800]{1,0:T(8,128)} %get-tuple-element.71) | copy-start | bytes 76804
  244.0 11.2 %copy-start.5 = (bf16[1,400,800]{2,1,0:T(8,128)(2,1)S(1)}, bf16[1,400,800]{2,1,0:T(8,128)(2,1)}, u32[]{:S(2)}) copy-start(bf16[1,400,800]{2,1,0:T(8,128)(2,1)} %reduce-scatter.4.cloned.1.call-done) | copy-start | bytes 1920004
  256.4 48.9 %copy-start.3 = (bf16[1,512,800]{2,1,0:T(8,128)(2,1)S(1)}, bf16[1,512,800]{2,1,0:T(8,128)(2,1)}, u32[]{:S(2)}) copy-start(bf16[1,512,800]{2,1,0:T(8,128)(2,1)} %reduce-scatter.6.cloned.1.call-done) | copy-start | bytes 2457604
  308.0 3.4 %copy-start.2 = (bf16[800,256]{1,0:T(8,128)(2,1)S(1)}, bf16[800,256]{1,0:T(8,128)(2,1)}, u32[]{:S(2)}) copy-start(bf16[800,256]{1,0:T(8,128)(2,1)} %shard_map.279) | copy-start | bytes 1228804
  309.3 2.9 copy-start.4
Sparse Core Ops, SparseCore 0:
  44.6 39.0 all-gather.2
  127.4 54.4 reduce-scatter.3
  186.8 66.3 reduce-scatter.5
  255.4 46.7 reduce-scatter.7

commit v4 on v3

--- a/solution.py
+++ b/solution.py
@@ -71,6 +71,10 @@
     )
 
 
+def pick(k, zero, one, two, three):
+    return jnp.where(k == 0, zero, jnp.where(k == 1, one, jnp.where(k == 2, two, three)))
+
+
 def lanes(index, size):
     return pl.ds(pl.multiple_of(index * size, size), size)
 
@@ -201,11 +205,9 @@
             ]
 
         def keep(slot, row, number):
-            copy = pltpu.make_async_copy(
+            return pltpu.make_async_copy(
                 got.at[0, slot], self.all_ref.at[:, lanes(row, size)], self.out_sem.at[number]
             )
-            copy.start()
-            return copy
 
         to_a = move(0, (0, 0), (0, place.a), dev_a)
         to_b = move(1, (0, 0), (0, place.b), dev_b)
@@ -217,38 +219,55 @@
         for copies in (to_a, to_b, to_mate):
             for copy in copies:
                 copy.start()
-        kept = [keep(0, place.r, 0)]
+        keep(0, place.r, 0).start()
         idle()
-        for copy in to_mate:
-            copy.wait_recv()
-        work(0, place.r)
-        for k, copy in enumerate(to_a):
-            copy.wait_recv()
-            relay[k].start()
-            fwd_a[k].start()
-        kept.append(keep(place.a, place.ra, 1))
-        for k, copy in enumerate(to_b):
-            copy.wait_recv()
-            fwd_b[k].start()
-        kept.append(keep(place.b, place.rb, 2))
-        for copy in fwd_b:
-            copy.wait_recv()
-        work(place.b, place.rb)
-        for copy in fwd_a:
-            copy.wait_recv()
-        work(place.a, place.ra)
-        for k, copy in enumerate(relay):
-            copy.wait_recv()
-            fwd_3[k].start()
-        kept.append(keep(3, place.r3, 3))
-        for copy in fwd_3:
-            copy.wait_recv()
-        work(3, place.r3)
+
+        def phase(k, carry):
+            @pl.when(k == 0)
+            def _():
+                for copy in to_mate:
+                    copy.wait_recv()
+
+            @pl.when(k == 1)
+            def _():
+                for n, copy in enumerate(to_a):
+                    copy.wait_recv()
+                    relay[n].start()
+                    fwd_a[n].start()
+                keep(place.a, place.ra, 1).start()
+                for n, copy in enumerate(to_b):
+                    copy.wait_recv()
+                    fwd_b[n].start()
+                keep(place.b, place.rb, 2).start()
+                for copy in fwd_b:
+                    copy.wait_recv()
+
+            @pl.when(k == 2)
+            def _():
+                for copy in fwd_a:
+                    copy.wait_recv()
+
+            @pl.when(k == 3)
+            def _():
+                for n, copy in enumerate(relay):
+                    copy.wait_recv()
+                    fwd_3[n].start()
+                keep(3, place.r3, 3).start()
+                for copy in fwd_3:
+                    copy.wait_recv()
+
+            slot = pick(k, 0, place.b, place.a, 3)
+            work(k, slot, pick(k, place.r, place.rb, place.ra, place.r3))
+            return carry
+
+        lax.fori_loop(0, 4, phase, 0)
         for copies in (to_mate, to_a, to_b, relay, fwd_a, fwd_b, fwd_3):
             for copy in copies:
                 copy.wait_send()
-        for copy in kept:
-            copy.wait()
+        for slot, row, number in (
+            (0, place.r, 0), (place.a, place.ra, 1), (place.b, place.rb, 2), (3, place.r3, 3)
+        ):
+            keep(slot, row, number).wait()
 
 
 def gather_triple(tokens, cols, bias, weight, width, feats, cid):
@@ -278,7 +297,7 @@
             row = (head - 3 * owner) * per + part * HEAD_DIM + (inner - head * HEAD_DIM)
             return owner, pl.ds(pl.multiple_of(row, GRAIN), GRAIN)
 
-        def work(slot, row):
+        def work(k, slot, row):
             total = weight.product(gather.got[0, slot], gather.got[1, slot])
             tt[:, lanes(row, size)] = (total + b_ref[...]).astype(BF16)
 
@@ -358,8 +377,21 @@
         average, rstd = moments(Totals(place, tb, ts), middle, width)
         keep_moments(st_ref, average, rstd)
         gather.got[0, 0] = ((middle - average) * rstd * c_ref[:, 3:4] + c_ref[:, 4:5]).astype(BF16)
-        pending = []
         mine = pl.ds(pl.multiple_of(place.c * feats, GRAIN), feats)
+        grad_sum[...] = jnp.zeros_like(grad_sum)
+
+        def moves(k, row):
+            span = lanes(row, size)
+            index = row
+            there = hid_ref.at[mine, span]
+            return (
+                rcopy(
+                    act.at[mine, span], act.at[mine, span],
+                    swap_send.at[0, k], swap_recv.at[0, index], mate,
+                ),
+                rcopy(hid.at[k], there, swap_send.at[1, k], swap_recv.at[1, index], mate),
+                pltpu.make_async_copy(hid.at[k], there, swap_out.at[k]),
+            )
 
         def idle():
             back.share()
@@ -376,38 +408,25 @@
             lax.fori_loop(0, 4, one, 0)
             ahead.copy.wait()
 
-        def work(slot, row):
-            number = len(pending)
+        def work(k, slot, row):
             p = ahead.product(gather.got[0, slot], gather.got[1, slot]) + b_ref[...]
             square = p * p
             t = jnp.tanh(0.7978845608028654 * (p + 0.044715 * (square * p)))
-            span = lanes(row, size)
-            act[mine, span] = (0.5 * p * (1.0 + t)).astype(BF16)
+            act[mine, lanes(row, size)] = (0.5 * p * (1.0 + t)).astype(BF16)
             slope = 0.5 * (1.0 + t) + 0.5 * p * (1.0 - t * t) * (
                 0.7978845608028654 * (1.0 + 3.0 * 0.044715 * square)
             )
             grad = grads[row] * slope
-            hid[number] = grad.astype(BF16)
-            there = hid_ref.at[mine, span]
-            copies = [
-                rcopy(
-                    act.at[mine, span], act.at[mine, span],
-                    swap_send.at[0, number], swap_recv.at[0, number], mate,
-                ),
-                rcopy(
-                    hid.at[number], there, swap_send.at[1, number], swap_recv.at[1, number], mate
-                ),
-                pltpu.make_async_copy(hid.at[number], there, swap_out.at[number]),
-            ]
-            for copy in copies:
+            hid[k] = grad.astype(BF16)
+            for copy in moves(k, row):
                 copy.start()
-            grad_sum[...] = grad if number == 0 else grad_sum[...] + grad
-            pending.append(copies)
+            grad_sum[...] += grad
 
         gather.run(work, idle)
         sum_ref[0:1] = col_sums(grad_sum[...])
-        for copies in pending:
-            copies[0].wait()
+        order = [place.r, place.rb, place.ra, place.r3]
+        for k, row in enumerate(order):
+            moves(k, row)[0].wait()
         act_out = pltpu.make_async_copy(act, act_ref, swap_out.at[4])
         act_out.start()
         part = feats // 2
@@ -421,8 +440,8 @@
             return carry
 
         lax.fori_loop(0, 4, some, 0)
-        for copies in pending:
-            for copy in copies[1:]:
+        for k, row in enumerate(order):
+            for copy in moves(k, row)[1:]:
                 copy.wait()
         act_out.wait()
 
@@ -489,7 +508,7 @@
             sum_ref[3:4] = col_sums(x_ref[...])
             swap.wait()
 
-        def work(slot, row):
+        def work(k, slot, row):
             total = dot(heads(place.c)[...], gather.got[0, slot], NN)
             total += dot(other[...], gather.got[1, slot], NN)
             y_ref[:, lanes(row, size)] = total.astype(BF16)
@@ -532,18 +551,36 @@
     first = move(0, place.dev(place.ra))
     second = move(1, place.dev(place.ra))
     third = move(2, place.dev(place.rb))
-    outbox[0] = block(place.r3).astype(BF16)
-    for copy in first:
-        copy.start()
-    passed[...] = block(place.rb)
-    outbox[1] = block(place.ra).astype(BF16)
-    for copy in second:
-        copy.start()
-    for k, part in parts:
-        first[k].wait_recv()
-        outbox[2, part] = (passed[part] + inbox[0, part].astype(F32)).astype(BF16)
-        third[k].start()
-    passed[...] = block(place.r)
+
+    def phase(k, carry):
+        @pl.when(k == 3)
+        def _():
+            for n, part in parts:
+                first[n].wait_recv()
+                outbox[2, part] = (passed[part] + inbox[0, part].astype(F32)).astype(BF16)
+                third[n].start()
+
+        total = block(k, pick(k, place.r3, place.rb, place.ra, place.r))
+
+        @pl.when((k == 1) | (k == 3))
+        def _():
+            passed[...] = total
+
+        @pl.when(k == 0)
+        def _():
+            outbox[0] = total.astype(BF16)
+            for copy in first:
+                copy.start()
+
+        @pl.when(k == 2)
+        def _():
+            outbox[1] = total.astype(BF16)
+            for copy in second:
+                copy.start()
+
+        return carry
+
+    lax.fori_loop(0, 4, phase, 0)
     for copy in second:
         copy.wait_recv()
     passed[...] += inbox[1].astype(F32)
@@ -563,16 +600,20 @@
 def loaded_block(place, l_ref, w_ref, weight, left, sems, size):
     w_load = pltpu.make_async_copy(w_ref, weight, sems.at[4])
     w_load.start()
-    loads = []
+
+    def load(k, row):
+        span = lanes(row, size)
+        return pltpu.make_async_copy(l_ref.at[:, span], left.at[:, span], sems.at[k])
+
     for k, row in enumerate((place.r3, place.rb, place.ra, place.r)):
-        span = lanes(row, size)
-        loads.append(pltpu.make_async_copy(l_ref.at[:, span], left.at[:, span], sems.at[k]))
-        loads[-1].start()
-
-    def block(row):
-        if len(loads) == 4:
+        load(k, row).start()
+
+    def block(k, row):
+        @pl.when(k == 0)
+        def _():
             w_load.wait()
-        loads.pop(0).wait()
+
+        load(k, row).wait()
         return dot(weight[...], left[:, lanes(row, size)], NN)
 
     return block
@@ -655,7 +696,7 @@
         kept = pltpu.make_async_copy(full, all_ref, kept_sem)
         kept.start()
         out_ref[...] = run_scatter(
-            place, lambda row: dot(w_ref[...], full[:, lanes(row, size)], TN), refs
+            place, lambda k, row: dot(w_ref[...], full[:, lanes(row, size)], TN), refs
         )
         kept.wait()
 
@@ -666,7 +707,8 @@
     )(heads, weight)
 
 
-def triple_scatter(heads, weight, tokens, stats, middle_grad, cols, width, cid):
+def triple_scatter(heads, weight, tokens, stats, middle_grad, cols, pieces, width, cid):
+    groups = pieces.shape[0]
     rows, feats = weight.shape
     count_tokens = heads.shape[1]
     size = count_tokens // 4
@@ -674,13 +716,16 @@
     low = (feats // GRAIN + 1) // 2 * GRAIN
 
     def kernel(
-        h_ref, w_ref, t_ref, st_ref, mg_ref, c_ref, all_ref, out_ref, sum_ref, bias_ref,
-        full, w, w_sem, tb, ts, gs, gr, ms, mr, kept_sem, *refs,
+        h_ref, w_ref, p_ref, t_ref, st_ref, mg_ref, c_ref,
+        all_ref, got_ref, out_ref, sum_ref, bias_ref, full, w, w_sem, p_sems, tb, ts, gs, gr, ms, mr, kept_sem, *refs,
     ):
         place = Place()
         w_load = pltpu.make_async_copy(w_ref, w, w_sem)
         w_load.start()
-        place.barrier(place.group())
+        peers = [
+            (lax.rem(place.d + step, groups), place.r, place.c) for step in range(1, groups)
+        ]
+        place.barrier(place.group() + peers)
         me = 2 * place.r + place.c
         count = jnp.where(me == 7, 4, 3) * (per // GRAIN)
 
@@ -710,6 +755,19 @@
             return carry
 
         lax.fori_loop(0, count, send_grain, 0)
+        traded = [
+            rcopy(
+                p_ref.at[peer[0]], got_ref.at[place.d],
+                p_sems.at[0, k], p_sems.at[1, k], peer,
+            )
+            for k, peer in enumerate(peers)
+        ]
+        for copy in traded:
+            copy.start()
+        own_piece = pltpu.make_async_copy(
+            p_ref.at[place.d], got_ref.at[place.d], p_sems.at[0, groups - 1]
+        )
+        own_piece.start()
 
         def drain(j, carry):
             @pl.when(target(j)[0] != me)
@@ -740,7 +798,7 @@
         kept = pltpu.make_async_copy(full, all_ref, kept_sem)
         kept.start()
         w_load.wait()
-        grad = run_scatter(place, lambda row: dot(w[...], full[:, lanes(row, size)], NN), refs)
+        grad = run_scatter(place, lambda k, row: dot(w[...], full[:, lanes(row, size)], NN), refs)
         rstd = st_ref[1:2]
         hat = (t_ref[...].astype(F32) - st_ref[0:1]) * rstd
         back = norm_back(Totals(place, tb, ts), grad, hat, rstd, c_ref[:, 0:1], width)
@@ -749,18 +807,22 @@
         sum_ref[1:2] = col_sums(grad)
         bias_ref[0:1] = col_sums(full[...])
         kept.wait()
+        own_piece.wait()
+        for copy in traded:
+            copy.wait()
 
     return call(
         kernel,
         (
-            struct((feats, count_tokens), BF16), struct((rows, size), F32),
-            struct((8, rows), F32), struct((8, feats), F32),
+            struct((feats, count_tokens), BF16), struct(pieces.shape, BF16),
+            struct((rows, size), F32), struct((8, rows), F32), struct((8, feats), F32),
         ),
-        (ANY, VM, VM, VM), [ANY, ANY] + [VM] * 4,
+        (ANY, ANY, VM, VM, VM), [ANY] * 3 + [VM] * 4,
         [pltpu.VMEM((feats, count_tokens), BF16), pltpu.VMEM(weight.shape, BF16), DMA]
+        + [DMA((2, groups))]
         + Totals.scratch + [DMA] * 5
         + scatter_scratch(rows, size), cid,
-    )(heads, weight, tokens, stats, middle_grad, cols)
+    )(heads, weight, pieces, tokens, stats, middle_grad, cols)
 
 
 def attention_bias(seg_col, seg_row, bias_ref):
@@ -979,32 +1041,23 @@
         second_normed_grad, middle, second_stats, cot_t, cols, proj_weight, width, 5
     )
     proj_grad = product(attended_all, middle_all)
-    pieces = [
-        product(second_all, hid_all[:hidden]),
-        product(second_all, hid_all[hidden:]),
-        proj_grad,
-    ]
-    pieces = [piece.reshape(dp_count, -1, col_width) for piece in pieces]
-    joint = sum(piece.shape[1] for piece in pieces)
-    pieces.append(jnp.zeros((dp_count, -joint % 32, col_width), BF16))
-    both_grad = jnp.concatenate(pieces, axis=1)
-    attended_grad, shrink_owned, both_grad = lax.optimization_barrier(
-        (attended_grad, shrink_owned, both_grad)
-    )
-    both_owned = owned(both_grad.reshape(-1, col_width))
+    expand_grad = product(second_all, hid_all)
+    attended_grad, shrink_owned, expand_grad = lax.optimization_barrier(
+        (attended_grad, shrink_owned, expand_grad)
+    )
+    expand_owned = owned(expand_grad)
     triple_head_grad = attention_backward(
         triple, seg_col, seg_row, attended, attended_grad, lse
     )
-    triple_all, input_grad, first_sums, bias_sums = triple_scatter(
-        triple_head_grad, triple_weight, tokens_t, first_stats, middle_grad, cols, width, 6
+    triple_all, proj_parts, input_grad, first_sums, bias_sums = triple_scatter(
+        triple_head_grad, triple_weight, tokens_t, first_stats, middle_grad, cols,
+        proj_grad.reshape(dp_count, -1, col_width), width, 6,
     )
     triple_grad = product(first_all, triple_all)
-    act_all, triple_grad, both_owned, first_sums = lax.optimization_barrier(
-        (act_all, triple_grad, both_owned, first_sums)
-    )
-    part = col_width // dp_count
-    expand_owned = jnp.concatenate([both_owned[:, :part], both_owned[:, part : 2 * part]], axis=2)
-    proj_owned = both_owned[:, 2 * part : joint]
+    act_all, triple_grad, expand_owned, first_sums, proj_parts = lax.optimization_barrier(
+        (act_all, triple_grad, expand_owned, first_sums, proj_parts)
+    )
+    proj_owned = jnp.sum(proj_parts.astype(F32), axis=0, keepdims=True)
     triple_owned = owned(triple_grad)
     block_out = output_scatter(act_all, shrink_weight.T, middle, cols, 7)
 

time: 324 us -> 314 us (0.969); the launches traced: 320 us -> 314 us
  waiting for transfers between devices: 9.31 us -> 5.2 us
  Pallas kernels: 257 us -> 261 us
    pallas_call x1, Pallas kernels: 40.5 us -> 47.6 us  [triple_scatter(): call(kernel, (struct((feats, count_tokens), BF16), struct(pieces.shape, B...]
    reduce_scatter x3 -> x2, waiting for transfers between devices: 9.22 us -> 3.48 us  [owned(): summed = lax.psum_scatter(parts, 'dp', scatter_dimension=0, tiled=True)]
    pallas_call x1, Pallas kernels: 24.2 us -> 28.7 us  [sum_all(): call(kernel, jax.ShapeDtypeStruct(pieces.shape, F32), VM, [VM], [pltpu.VM...]
    dot_general x4 -> x3, matrix products: 14.5 us -> 12.5 us  [product(): lax.dot_general(left, right, NT, preferred_element_type=F32).astype(BF16)]
  transfers between devices with their start and end apart: 4 -> 4, of which waited for: 1 -> 2; matrix products, arithmetic and copies ran while one was open for 10% -> 8% of each run, Pallas kernels for 58% -> 61%
where the time goes in v4:
time: 314 us
  Pallas kernels  261 us (83%)
  local copies, waits for them, and re-layouts  14.9 us (5%)
  between operations  14.1 us (4%)
  matrix products  12.5 us (4%)
  other arithmetic  5.43 us (2%)
  waiting for transfers between devices  5.2 us (2%)
    pallas_call x1, Pallas kernels, triple_scatter(): call(kernel, (struct((feats, count_tokens), BF16), struct(pieces.shape, B...  47.6 us
    pallas_call x1, Pallas kernels, gather_hidden(): call(kernel, (struct((rows, tokens_all), BF16), full, full, struct((rows,...  35.4 us
    pallas_call x1, Pallas kernels, attended_scatter(): call(kernel, (struct((feats, tokens), BF16), struct((rows, size), F32)),...  33.1 us
    pallas_call x1, Pallas kernels, gather_triple(): call(kernel, (struct((rows, 4 * size), BF16), struct((4 * per, 4 * size),...  33.1 us
    pallas_call x1, Pallas kernels, sum_all(): call(kernel, jax.ShapeDtypeStruct(pieces.shape, F32), VM, [VM], [pltpu.VM...  28.7 us
    pallas_call x1, Pallas kernels, gather_middle(): call(kernel, (struct((rows, 4 * size), BF16), struct((feats, 4 * size), B...  24.6 us
    pallas_call x1, Pallas kernels, hidden_scatter(): call(kernel, struct((rows, size), F32), VM, [ANY] * 2, load_scratch(weigh...  20.2 us
    pallas_call x1, Pallas kernels, output_scatter(): call(kernel, struct((rows, size), BF16), VM, [ANY, ANY, VM, VM], load_scr...  18.6 us
  transfers between devices with their start and end apart: 4, of which 2 were waited for; matrix products, arithmetic and copies ran while one was open for 8% of the time, Pallas kernels for 61%

profile of v4, /device:TPU:25, one launch (start us, length us, event | category | flops | bytes accessed | tf_op | source)
XLA Modules:
  0.0 313.6 jit_solution(13319028366013593850)
XLA Ops:
  7.2 0.9 concatenate.12
  8.1 0.1 reshape.97
  8.2 0.8 concatenate.13
  9.0 0.1 dynamic_slice.10
  9.1 0.9 broadcast_in_dim.20.b_ref
  9.9 0.1 constant_dynamic-slice_fusion
  10.0 0.9 copy.41
  11.0 33.1 %shard_map.271 = (bf16[800,1024]{1,0:T(8,128)(2,1)}, bf16[768,1024]{1,0:T(8,128)(2,1)}, f32[8,256]{1,0:T(8,128)}) custom-call(bf16[800,256]{1,0:T(8,128)(2,1)} %bitcast.28, f32[800,6]{1,0:T(8,128)} %bitcast.21, f32[608,1]{1,0:T(8,128)} %broadcast_in_dim.20.b_ref, bf16[800,1200]{1,0:T(8,128)(2,1)} %w_ref.11), custom_call_target="tpu_custom_call" | custom-call | tf_op jit(solution)/shard_map/pallas_call | solution.py:346
  44.1 0.0 reduce-scatter.6.cloned.1.call-start
  44.1 0.8 dynamic_slice.11
  44.9 0.9 broadcast_in_dim.21.b_ref
  45.8 1.0 copy.38.sc_ref
  46.8 8.3 %shard_map.272 = (bf16[256,1024]{1,0:T(8,128)(2,1)}, f32[4,1,1024]{2,1,0:T(1,128)}) custom-call(s32[1024,1]{1,0:T(8,128)} %copy.38.sc_ref, s32[1,1024]{1,0:T(1,128)} %sr_ref.3, bf16[768,1024]{1,0:T(8,128)(2,1)} %get-tuple-element.49.t_ref), custom_call_target="tpu_custom_call" | custom-call | tf_op jit(solution)/shard_map/pallas_call | solution.py:864
  55.2 33.1 %shard_map.273 = (bf16[400,1024]{1,0:T(8,128)(2,1)}, f32[800,256]{1,0:T(8,128)}) custom-call(bf16[256,1024]{1,0:T(8,128)(2,1)} %get-tuple-element.50.h_ref.o_ref, bf16[400,800]{1,0:T(8,128)(2,1)} %w_ref.10), custom_call_target="tpu_custom_call" | custom-call | tf_op jit(solution)/shard_map/pallas_call | solution.py:703
  88.3 35.4 %shard_map.274 = (bf16[800,1024]{1,0:T(8,128)(2,1)}, bf16[1600,1024]{1,0:T(8,128)(2,1)}, bf16[1600,1024]{1,0:T(8,128)(2,1)}, f32[800,256]{1,0:T(8,128)}, f32[8,2...) custom-call(bf16[800,256]{1,0:T(8,128)(2,1)} %bitcast.29, f32[800,256]{1,0:T(8,128)} %get-tuple-element.51.p_ref, ...), custom_call_target="tpu_custom_call" | custom-call | tf_op jit(solution)/shard_map/pallas_call | solution.py:449
  123.7 0.2 reduce-scatter.10.cloned.1.call-start
  123.9 20.2 %shard_map.275.s_ref = f32[800,256]{1,0:T(8,128)} custom-call(bf16[1600,1024]{1,0:T(8,128)(2,1)} %get-tuple-element.55.l_ref, bf16[800,1600]{1,0:T(8,128)(2,1)} %w_ref.9), custom_call_target="tpu_custom_call" | custom-call | tf_op jit(solution)/shard_map/pallas_call | solution.py:631
  144.2 24.6 %shard_map.276 = (bf16[800,1024]{1,0:T(8,128)(2,1)}, bf16[256,1024]{1,0:T(8,128)(2,1)}, f32[800,256]{1,0:T(8,128)}, f32[8,800]{1,0:T(8,128)}) custom-call(f32[800,256]{1,0:T(8,128)} %shard_map.275.s_ref, f32[800,256]{1,0:T(8,128)} %get-tuple-element.56.m_ref, f32[8,256]{1,0:T(8,128)} %get-tuple-element.57.st_ref, bf16[800,256]{1,0:T(8,128)(2,1)} %bitcast.35, ...), custom_call_target="tpu_custom_call" | custom-call | tf_op jit(solution)/shard_map/pallas_call | solution.py:518
  168.8 6.1 %convolution_convert_fusion = bf16[800,1600]{1,0:T(8,128)(2,1)} fusion(bf16[800,1024]{1,0:T(8,128)(2,1)} %get-tuple-element.60, bf16[1600,1024]{1,0:T(8,128)(2,1)S(1)} %copy-done), kind=kOutput, calls=%fused_computation | convolution fusion | flops 2622720000 | bytes 7475200 | tf_op jit(solution)/shard_map/dot_general | solution.py:1030
  174.9 3.5 %reduce-scatter.6.cloned.1.call-done = bf16[1,400,800]{2,1,0:T(8,128)(2,1)} async-done(((bf16[4,400,800]{2,1,0:T(8,128)(2,1)}), bf16[1,400,800]{2,1,0:T(8,128)(2,1)}) %reduce-scatter.6.cloned.1.call-update) | async-done | bytes 640016 | tf_op jit(solution)/shard_map/reduce_scatter | solution.py:1034
  178.4 0.3 reduce-scatter.8.cloned.1.call-start
  178.7 1.0 convolution_convert_fusion.2
  179.8 1.0 reshape.99.p_ref
  180.8 11.2 %shard_map.277.h_ref = bf16[768,1024]{1,0:T(8,128)(2,1)} custom-call(s32[1024,1]{1,0:T(8,128)} %copy.38.sc_ref, s32[1,1024]{1,0:T(1,128)} %sr_ref.3, bf16[768,1024]{1,0:T(8,128)(2,1)} %get-tuple-element.49.t_ref, bf16[256,1024]{1,0:T(8,128)(2,1)} %get-tuple-element.50.h_ref.o_ref, bf16[256,1024]{1,0:T(8,128)(2,1)} %get-tuple-element.61.g_ref, ...), custom_call_target="tpu_custom_call" | custom-call | tf_op jit(solution)/shard_map/pallas_call | solution.py:917
  192.0 47.6 %shard_map.278 = (bf16[1200,1024]{1,0:T(8,128)(2,1)}, bf16[4,100,800]{2,1,0:T(8,128)(2,1)}, f32[800,256]{1,0:T(8,128)}, f32[8,800]{1,0:T(8,128)}, f32[8,1200]{1,0:T(8,128)}) custom-call(bf16[768,1024]{1,0:T(8,128)(2,1)} %shard_map.277.h_ref, bf16[800,1200]{1,0:T(8,128)(2,1)} %w_ref.11, bf16[4,100,800]{2,1,0:T(8,128)(2,1)} %reshape.99.p_ref, ...), custom_call_target="tpu_custom_call" | custom-call | tf_op jit(solution)/shard_map/pallas_call | solution.py:814
  239.6 5.4 %convolution_convert_fusion.1 = bf16[800,1200]{1,0:T(8,128)(2,1)} fusion(bf16[800,1024]{1,0:T(8,128)(2,1)S(1)} %copy-done.9, bf16[1200,1024]{1,0:T(8,128)(2,1)} %get-tuple-element.67), kind=kOutput, calls=%fused_computation.1 | convolution fusion | flops 1967040000 | bytes 6016000 | tf_op jit(solution)/shard_map/dot_general | solution.py:1030
  245.0 1.6 reduce-scatter.10.cloned.1.call-done
  246.7 0.8 slice_reduce_fusion.1
  247.5 0.1 broadcast_multiply_fusion.1
  247.6 0.1 mul.84
  247.7 0.8 slice_reduce_fusion
  248.5 0.1 broadcast_multiply_fusion.2
  248.5 0.1 mul.89
  248.7 1.2 convert_element_type.53
  249.8 18.6 %shard_map.279 = bf16[800,256]{1,0:T(8,128)(2,1)} custom-call(bf16[1600,1024]{1,0:T(8,128)(2,1)} %get-tuple-element.71.l_ref, bf16[800,1600]{1,0:T(8,128)(2,1)} %bitcast.27, f32[800,256]{1,0:T(8,128)} %get-tuple-element.56.m_ref, f32[800,6]{1,0:T(8,128)} %bitcast.25), custom_call_target="tpu_custom_call" | custom-call | tf_op jit(solution)/shard_map/pallas_call | solution.py:647
  268.5 0.8 slice.55
  269.3 0.1 broadcast_multiply_fusion
  269.4 0.1 mul.79
  269.5 0.7 fusion.x_ref
  270.2 28.7 %shard_map.280 = f32[32,8,128]{2,1,0:T(8,128)} custom-call(f32[32,8,128]{2,1,0:T(8,128)} %fusion.x_ref), custom_call_target="tpu_custom_call" | custom-call | tf_op jit(solution)/shard_map/pallas_call | solution.py:981
  298.9 1.4 slice.75
  300.4 0.1 convert_reduce_fusion
  300.5 1.0 broadcast_in_dim.19
  301.5 1.2 convert_element_type.52
  302.6 0.7 fusion.1
  303.3 2.1 convert_element_type.50
  305.4 0.8 copy.44
  306.1 0.9 copy.45
  (37 shorter events, 0.2 us)
Async XLA Ops:
  7.2 81.1 %all-gather.3.cloned.1.call-start = ((), (), s32[]{:S(2)}) async-start(), calls=%async_computation.5 | async-start | bytes 2048000 | tf_op jit(solution)/shard_map/all_gather | solution.py:1019
  11.0 34.9 %copy-start.7 = (s32[1,1024]{1,0:T(1,128)S(1)}, s32[1,1024]{1,0:T(1,128)}, u32[]{:S(2)}) copy-start(s32[1,1024]{1,0:T(1,128)} %sr_ref.3) | copy-start | bytes 12292
  44.1 134.4 %reduce-scatter.6.cloned.1.call-start = ((), (), s32[]{:S(2)}) async-start(), calls=%async_computation.3 | async-start | bytes 3584000 | tf_op jit(solution)/shard_map/reduce_scatter | solution.py:1034
  123.7 123.0 %reduce-scatter.10.cloned.1.call-start = ((), (), s32[]{:S(2)}) async-start(), calls=%async_computation.6 | async-start | bytes 3328000
  123.9 44.9 %copy-start = (bf16[1600,1024]{1,0:T(8,128)(2,1)S(1)}, bf16[1600,1024]{1,0:T(8,128)(2,1)}, u32[]{:S(2)}) copy-start(bf16[1600,1024]{1,0:T(8,128)(2,1)} %get-tuple-element.55.l_ref) | copy-start | bytes 9830404
  174.9 3.8 %copy-start.10 = (bf16[800,1024]{1,0:T(8,128)(2,1)S(1)}, bf16[800,1024]{1,0:T(8,128)(2,1)}, u32[]{:S(2)}) copy-start(bf16[800,1024]{1,0:T(8,128)(2,1)} %get-tuple-element.64) | copy-start | bytes 4915204
  174.9 3.8 %copy-start.11 = (bf16[400,1024]{1,0:T(8,128)(2,1)S(1)}, bf16[400,1024]{1,0:T(8,128)(2,1)}, u32[]{:S(2)}) copy-start(bf16[400,1024]{1,0:T(8,128)(2,1)} %get-tuple-element.63) | copy-start | bytes 2457604
  178.4 124.9 %reduce-scatter.8.cloned.1.call-start = ((), (), s32[]{:S(2)}) async-start(), calls=%async_computation.4 | async-start | bytes 2560000 | tf_op jit(solution)/shard_map/reduce_scatter | solution.py:1034
  192.0 47.6 %copy-start.9 = (bf16[800,1024]{1,0:T(8,128)(2,1)S(1)}, bf16[800,1024]{1,0:T(8,128)(2,1)}, u32[]{:S(2)}) copy-start(bf16[800,1024]{1,0:T(8,128)(2,1)} %get-tuple-element.54) | copy-start | bytes 4915204
  245.0 2.6 copy-start.8
  245.0 3.6 %copy-start.4 = (bf16[1,400,800]{2,1,0:T(8,128)(2,1)S(1)}, bf16[1,400,800]{2,1,0:T(8,128)(2,1)}, u32[]{:S(2)}) copy-start(bf16[1,400,800]{2,1,0:T(8,128)(2,1)} %reduce-scatter.6.cloned.1.call-done) | copy-start | bytes 1920004
  249.8 50.5 %copy-start.3 = (bf16[4,100,800]{2,1,0:T(8,128)(2,1)S(1)}, bf16[4,100,800]{2,1,0:T(8,128)(2,1)}, u32[]{:S(2)}) copy-start(bf16[4,100,800]{2,1,0:T(8,128)(2,1)} %get-tuple-element.78) | copy-start | bytes 1920004
  268.5 33.0 %copy-start.5 = (bf16[1,200,1600]{2,1,0:T(8,128)(2,1)S(1)}, bf16[1,200,1600]{2,1,0:T(8,128)(2,1)}, u32[]{:S(2)}) copy-start(bf16[1,200,1600]{2,1,0:T(8,128)(2,1)} %reduce-scatter.10.cloned.1.call-done) | copy-start | bytes 1920004
  298.9 3.7 %copy-start.6 = (f32[32,8,128]{2,1,0:T(8,128)S(1)}, f32[32,8,128]{2,1,0:T(8,128)}, u32[]{:S(2)}) copy-start(f32[32,8,128]{2,1,0:T(8,128)} %shard_map.280) | copy-start | bytes 393220
  300.5 4.9 %copy-start.1 = (bf16[800,256]{1,0:T(8,128)(2,1)S(1)}, bf16[800,256]{1,0:T(8,128)(2,1)}, u32[]{:S(2)}) copy-start(bf16[800,256]{1,0:T(8,128)(2,1)} %shard_map.279) | copy-start | bytes 1228804
  301.5 4.7 %copy-start.2 = (f32[800,256]{1,0:T(8,128)S(1)}, f32[800,256]{1,0:T(8,128)}, u32[]{:S(2)}) copy-start(f32[800,256]{1,0:T(8,128)} %get-tuple-element.72) | copy-start | bytes 2457604
Sparse Core Ops, SparseCore 0:
  44.2 39.6 all-gather.2
  123.8 54.5 reduce-scatter.5
  180.7 65.8 reduce-scatter.9
  248.8 48.3 reduce-scatter.7

commit v5 on v4

--- a/solution.py
+++ b/solution.py
@@ -102,7 +102,7 @@
 
 
 def chunks(size):
-    count = next(n for n in (5, 4, 2, 1) if size % (n * GRAIN) == 0)
+    count = next(n for n in (2, 1) if size % (n * GRAIN) == 0)
     return [pl.ds(k * (size // count), size // count) for k in range(count)]
 
 
@@ -650,21 +650,27 @@
     )(left, weight, middle, cols)
 
 
-def attended_scatter(heads, weight, cid):
+def attention_scatter(triple, seg_col, seg_row, weight, cid):
     feats, rows = weight.shape
-    tokens = heads.shape[1]
+    tokens = triple.shape[1]
     size = tokens // 4
-
-    def kernel(h_ref, w_ref, all_ref, out_ref, full, gs, gr, kept_sem, *refs):
+    per = 3 * HEAD_DIM
+
+    def kernel(
+        t_ref, sc_ref, sr_ref, w_ref, o_ref, l_ref, all_ref, out_ref,
+        bias_ref, full, gs, gr, kept_sem, *refs,
+    ):
         place = Place()
         place.barrier(place.group())
         me = 2 * place.r + place.c
-        count = jnp.where(me == 7, 4, 3) * (HEAD_DIM // GRAIN)
+        heads = jnp.where(me == 7, 4, 3)
+        grains = HEAD_DIM // GRAIN
+        attention_bias(sc_ref, sr_ref, bias_ref)
 
         def send_grain(j, carry):
             feature = 3 * HEAD_DIM * me + GRAIN * j
             owner = feature // feats
-            src = h_ref.at[pl.ds(pl.multiple_of(GRAIN * j, GRAIN), GRAIN)]
+            src = o_ref.at[pl.ds(pl.multiple_of(GRAIN * j, GRAIN), GRAIN)]
             dst = full.at[pl.ds(pl.multiple_of(feature - owner * feats, GRAIN), GRAIN)]
             rcopy(src, dst, gs, gr, (place.d, owner, 1 - place.c)).start()
 
@@ -678,11 +684,29 @@
 
             return carry
 
-        lax.fori_loop(0, count, send_grain, 0)
+        def one_head(h, carry):
+            def rows_of(part):
+                return pl.ds(pl.multiple_of(per * h + HEAD_DIM * part, GRAIN), HEAD_DIM)
+
+            for j in range(4):
+                reach, here = (j + 1) * size, slice(j * size, (j + 1) * size)
+                query = t_ref[rows_of(0), here] * BF16(HEAD_DIM ** (-0.5))
+                score = dot(t_ref[rows_of(1), 0:reach], query, TN) + bias_ref[0:reach, here]
+                top = jnp.max(score, axis=0, keepdims=True)
+                each = jnp.exp(score - top)
+                total = jnp.sum(each, axis=0, keepdims=True)
+                mixed = dot(t_ref[rows_of(2), 0:reach], each.astype(BF16), NN)
+                out_rows = pl.ds(pl.multiple_of(HEAD_DIM * h, GRAIN), HEAD_DIM)
+                o_ref[out_rows, here] = (mixed / total).astype(BF16)
+                l_ref[h, :, here] = top + jnp.log(total)
+            lax.fori_loop(grains * h, grains * (h + 1), send_grain, 0)
+            return carry
+
+        lax.fori_loop(0, heads, one_head, 0)
 
         def drain(j, carry):
             feature = 3 * HEAD_DIM * me + GRAIN * j
-            src = h_ref.at[pl.ds(0, GRAIN)]
+            src = o_ref.at[pl.ds(0, GRAIN)]
             pltpu.make_async_copy(src, src, gs).wait()
 
             @pl.when(feature // feats != place.r)
@@ -691,7 +715,7 @@
 
             return carry
 
-        lax.fori_loop(0, count, drain, 0)
+        lax.fori_loop(0, heads * grains, drain, 0)
         pltpu.make_async_copy(full, full, gr).wait()
         kept = pltpu.make_async_copy(full, all_ref, kept_sem)
         kept.start()
@@ -701,10 +725,15 @@
         kept.wait()
 
     return call(
-        kernel, (struct((feats, tokens), BF16), struct((rows, size), F32)),
-        (ANY, VM), [ANY, VM],
-        [pltpu.VMEM((feats, tokens), BF16), DMA, DMA, DMA] + scatter_scratch(rows, size), cid,
-    )(heads, weight)
+        kernel,
+        (
+            struct((4 * HEAD_DIM, tokens), BF16), struct((4, 1, tokens), F32),
+            struct((feats, tokens), BF16), struct((rows, size), F32),
+        ),
+        (VM, VM, ANY, VM), [VM] * 4,
+        [pltpu.VMEM((tokens, tokens), F32), pltpu.VMEM((feats, tokens), BF16), DMA, DMA, DMA]
+        + scatter_scratch(rows, size), cid,
+    )(triple, seg_col, seg_row, weight)
 
 
 def triple_scatter(heads, weight, tokens, stats, middle_grad, cols, pieces, width, cid):
@@ -835,51 +864,6 @@
 
 def holds(head):
     return (head < 3) | ((lax.axis_index("row") == 3) & (lax.axis_index("col") == 1))
-
-
-def attention_forward(triple, seg_col, seg_row):
-    per = 3 * HEAD_DIM
-    tokens = triple.shape[1]
-    span = tokens // 4
-
-    def kernel(sc_ref, sr_ref, t_ref, o_ref, l_ref, bias_ref):
-        @pl.when(pl.program_id(0) == 0)
-        def _():
-            attention_bias(sc_ref, sr_ref, bias_ref)
-
-        @pl.when(holds(pl.program_id(0)))
-        def _():
-            for j in range(4):
-                reach, here = (j + 1) * span, slice(j * span, (j + 1) * span)
-                query = t_ref[0:HEAD_DIM, here] * BF16(HEAD_DIM ** (-0.5))
-                score = dot(t_ref[HEAD_DIM : 2 * HEAD_DIM, 0:reach], query, TN)
-                score = score + bias_ref[0:reach, here]
-                top = jnp.max(score, axis=0, keepdims=True)
-                weight = jnp.exp(score - top)
-                total = jnp.sum(weight, axis=0, keepdims=True)
-                mixed = dot(t_ref[2 * HEAD_DIM : per, 0:reach], weight.astype(BF16), NN)
-                o_ref[:, here] = (mixed / total).astype(BF16)
-                l_ref[0, :, here] = top + jnp.log(total)
-
-    return pl.pallas_call(
-        kernel,
-        grid=(4,),
-        out_shape=(
-            jax.ShapeDtypeStruct((4 * HEAD_DIM, tokens), BF16),
-            jax.ShapeDtypeStruct((4, 1, tokens), F32),
-        ),
-        in_specs=[
-            pl.BlockSpec((tokens, 1), lambda h: (0, 0)),
-            pl.BlockSpec((1, tokens), lambda h: (0, 0)),
-            pl.BlockSpec((per, tokens), lambda h: (h, 0)),
-        ],
-        out_specs=(
-            pl.BlockSpec((HEAD_DIM, tokens), lambda h: (h, 0)),
-            pl.BlockSpec((1, 1, tokens), lambda h: (h, 0, 0)),
-        ),
-        scratch_shapes=[pltpu.VMEM((tokens, tokens), F32)],
-        compiler_params=pltpu.CompilerParams(vmem_limit_bytes=VMEM_BYTES),
-    )(seg_col, seg_row, triple)
 
 
 def attention_backward(triple, seg_col, seg_row, attended, attended_grad, lse):
@@ -1017,8 +1001,9 @@
     )
     triple, cot_later = lax.optimization_barrier((triple, cot_t))
     cot_rows = lax.all_gather(cot_later, "row")
-    attended, lse = attention_forward(triple, seg_col, seg_row)
-    attended_all, proj_out = attended_scatter(attended, proj_weight, 2)
+    attended, lse, attended_all, proj_out = attention_scatter(
+        triple, seg_col, seg_row, proj_weight, 2
+    )
     (
         second_all, act_all, hid_all, middle, second_stats, expand_bias_part, shrink_grad
     ) = gather_hidden(

time: 314 us -> 311 us (level)
  Pallas kernels: 261 us -> 257 us
    pallas_call x2 -> x1, Pallas kernels: 41.4 us -> 37.6 us  [attention_scatter(): call(kernel, (struct((4 * HEAD_DIM, tokens), BF16), struct((4, 1, tokens)...]
  transfers between devices with their start and end apart: 4 -> 4, of which waited for: 2 -> 3; matrix products, arithmetic and copies ran while one was open for 8% -> 8% of each run, Pallas kernels for 61% -> 61%
where the time goes in v5:
time: 311 us; the launch traced here: 310 us
  Pallas kernels  257 us (83%)
  local copies, waits for them, and re-layouts  14.9 us (5%)
  between operations  14.1 us (5%)
  matrix products  12.6 us (4%)
  waiting for transfers between devices  5.87 us (2%)
  other arithmetic  5.43 us (2%)
    pallas_call x1, Pallas kernels, triple_scatter(): call(kernel, (struct((feats, count_tokens), BF16), struct(pieces.shape, B...  47.4 us
    pallas_call x1, Pallas kernels, attention_scatter(): call(kernel, (struct((4 * HEAD_DIM, tokens), BF16), struct((4, 1, tokens)...  37.6 us
    pallas_call x1, Pallas kernels, gather_hidden(): call(kernel, (struct((rows, tokens_all), BF16), full, full, struct((rows,...  36.1 us
    pallas_call x1, Pallas kernels, gather_triple(): call(kernel, (struct((rows, 4 * size), BF16), struct((4 * per, 4 * size),...  32.6 us
    pallas_call x1, Pallas kernels, sum_all(): call(kernel, jax.ShapeDtypeStruct(pieces.shape, F32), VM, [VM], [pltpu.VM...  27.2 us
    pallas_call x1, Pallas kernels, gather_middle(): call(kernel, (struct((rows, 4 * size), BF16), struct((feats, 4 * size), B...  25.2 us
    pallas_call x1, Pallas kernels, output_scatter(): call(kernel, struct((rows, size), BF16), VM, [ANY, ANY, VM, VM], load_scr...  20.1 us
    pallas_call x1, Pallas kernels, hidden_scatter(): call(kernel, struct((rows, size), F32), VM, [ANY] * 2, load_scratch(weigh...  19.3 us
  transfers between devices with their start and end apart: 4, of which 3 were waited for; matrix products, arithmetic and copies ran while one was open for 8% of the time, Pallas kernels for 61%

profile of v5, /device:TPU:25, one launch (start us, length us, event | category | flops | bytes accessed | tf_op | source)
XLA Modules:
  0.0 310.2 jit_solution(4534032667175402547)
XLA Ops:
  7.2 0.9 concatenate.12
  8.1 0.1 reshape.96
  8.2 0.8 concatenate.13
  9.0 0.1 dynamic_slice.10
  9.1 0.9 broadcast_in_dim.20.b_ref
  9.9 0.1 constant_dynamic-slice_fusion
  10.0 0.9 copy.41
  11.0 32.6 %shard_map.271 = (bf16[800,1024]{1,0:T(8,128)(2,1)}, bf16[768,1024]{1,0:T(8,128)(2,1)}, f32[8,256]{1,0:T(8,128)}) custom-call(bf16[800,256]{1,0:T(8,128)(2,1)} %bitcast.28, f32[800,6]{1,0:T(8,128)} %bitcast.21, f32[608,1]{1,0:T(8,128)} %broadcast_in_dim.20.b_ref, bf16[800,1200]{1,0:T(8,128)(2,1)} %w_ref.11), custom_call_target="tpu_custom_call" | custom-call | tf_op jit(solution)/shard_map/pallas_call | solution.py:346
  43.6 0.0 reduce-scatter.6.cloned.1.call-start
  43.7 0.8 dynamic_slice.11
  44.4 0.9 broadcast_in_dim.21.b_ref
  45.4 1.0 copy.38.sc_ref
  46.4 37.6 %shard_map.272 = (bf16[256,1024]{1,0:T(8,128)(2,1)}, f32[4,1,1024]{2,1,0:T(1,128)}, bf16[400,1024]{1,0:T(8,128)(2,1)}, f32[800,256]{1,0:T(8,128)}) custom-call(bf16[768,1024]{1,0:T(8,128)(2,1)} %get-tuple-element.49.t_ref, s32[1024,1]{1,0:T(8,128)} %copy.38.sc_ref, s32[1,1024]{1,0:T(1,128)} %sr_ref.3, bf16[400,800]{1,0:T(8,128)(2,1)} %w_ref.10), custom_call_target="tpu_custom_call" | custom-call | tf_op jit(solution)/shard_map/pallas_call | solution.py:727
  84.0 0.2 all-gather.3.cloned.1.call-done
  84.3 36.1 %shard_map.273 = (bf16[800,1024]{1,0:T(8,128)(2,1)}, bf16[1600,1024]{1,0:T(8,128)(2,1)}, bf16[1600,1024]{1,0:T(8,128)(2,1)}, f32[800,256]{1,0:T(8,128)}, f32[8,2...) custom-call(bf16[800,256]{1,0:T(8,128)(2,1)} %bitcast.29, f32[800,256]{1,0:T(8,128)} %get-tuple-element.50.p_ref, ...), custom_call_target="tpu_custom_call" | custom-call | tf_op jit(solution)/shard_map/pallas_call | solution.py:449
  120.4 0.2 reduce-scatter.10.cloned.1.call-start
  120.7 19.3 %shard_map.274.s_ref = f32[800,256]{1,0:T(8,128)} custom-call(bf16[1600,1024]{1,0:T(8,128)(2,1)} %get-tuple-element.55.l_ref, bf16[800,1600]{1,0:T(8,128)(2,1)} %w_ref.9), custom_call_target="tpu_custom_call" | custom-call | tf_op jit(solution)/shard_map/pallas_call | solution.py:631
  140.0 25.2 %shard_map.275 = (bf16[800,1024]{1,0:T(8,128)(2,1)}, bf16[256,1024]{1,0:T(8,128)(2,1)}, f32[800,256]{1,0:T(8,128)}, f32[8,800]{1,0:T(8,128)}) custom-call(f32[800,256]{1,0:T(8,128)} %shard_map.274.s_ref, f32[800,256]{1,0:T(8,128)} %get-tuple-element.56.m_ref, f32[8,256]{1,0:T(8,128)} %get-tuple-element.57.st_ref, bf16[800,256]{1,0:T(8,128)(2,1)} %bitcast.35, ...), custom_call_target="tpu_custom_call" | custom-call | tf_op jit(solution)/shard_map/pallas_call | solution.py:518
  165.2 6.1 %convolution_convert_fusion = bf16[800,1600]{1,0:T(8,128)(2,1)} fusion(bf16[800,1024]{1,0:T(8,128)(2,1)} %get-tuple-element.60, bf16[1600,1024]{1,0:T(8,128)(2,1)S(1)} %copy-done), kind=kOutput, calls=%fused_computation | convolution fusion | flops 2622720000 | bytes 7475200 | tf_op jit(solution)/shard_map/dot_general | solution.py:1015
  171.3 3.8 %reduce-scatter.6.cloned.1.call-done = bf16[1,400,800]{2,1,0:T(8,128)(2,1)} async-done(((bf16[4,400,800]{2,1,0:T(8,128)(2,1)}), bf16[1,400,800]{2,1,0:T(8,128)(2,1)}) %reduce-scatter.6.cloned.1.call-update) | async-done | bytes 640016 | tf_op jit(solution)/shard_map/reduce_scatter | solution.py:1019
  175.2 0.3 reduce-scatter.8.cloned.1.call-start
  175.4 1.0 convolution_convert_fusion.2
  176.5 1.0 reshape.99.p_ref
  177.5 11.2 %shard_map.276.h_ref = bf16[768,1024]{1,0:T(8,128)(2,1)} custom-call(s32[1024,1]{1,0:T(8,128)} %copy.38.sc_ref, s32[1,1024]{1,0:T(1,128)} %sr_ref.3, bf16[768,1024]{1,0:T(8,128)(2,1)} %get-tuple-element.49.t_ref, bf16[256,1024]{1,0:T(8,128)(2,1)} %get-tuple-element.54.o_ref, bf16[256,1024]{1,0:T(8,128)(2,1)} %get-tuple-element.61.g_ref, ...), custom_call_target="tpu_custom_call" | custom-call | tf_op jit(solution)/shard_map/pallas_call | solution.py:901
  188.7 47.4 %shard_map.277 = (bf16[1200,1024]{1,0:T(8,128)(2,1)}, bf16[4,100,800]{2,1,0:T(8,128)(2,1)}, f32[800,256]{1,0:T(8,128)}, f32[8,800]{1,0:T(8,128)}, f32[8,1200]{1,0:T(8,128)}) custom-call(bf16[768,1024]{1,0:T(8,128)(2,1)} %shard_map.276.h_ref, bf16[800,1200]{1,0:T(8,128)(2,1)} %w_ref.11, bf16[4,100,800]{2,1,0:T(8,128)(2,1)} %reshape.99.p_ref, ...), custom_call_target="tpu_custom_call" | custom-call | tf_op jit(solution)/shard_map/pallas_call | solution.py:843
  236.2 5.4 %convolution_convert_fusion.1 = bf16[800,1200]{1,0:T(8,128)(2,1)} fusion(bf16[800,1024]{1,0:T(8,128)(2,1)S(1)} %copy-done.9, bf16[1200,1024]{1,0:T(8,128)(2,1)} %get-tuple-element.67), kind=kOutput, calls=%fused_computation.1 | convolution fusion | flops 1967040000 | bytes 6016000 | tf_op jit(solution)/shard_map/dot_general | solution.py:1015
  241.6 1.8 reduce-scatter.10.cloned.1.call-done
  243.4 0.8 slice_reduce_fusion.1
  244.2 0.1 broadcast_multiply_fusion.1
  244.3 0.1 mul.84
  244.4 0.8 slice_reduce_fusion
  245.2 0.1 broadcast_multiply_fusion.2
  245.2 0.1 mul.89
  245.3 1.2 convert_element_type.53
  246.5 20.1 %shard_map.278 = bf16[800,256]{1,0:T(8,128)(2,1)} custom-call(bf16[1600,1024]{1,0:T(8,128)(2,1)} %get-tuple-element.71.l_ref, bf16[800,1600]{1,0:T(8,128)(2,1)} %bitcast.27, f32[800,256]{1,0:T(8,128)} %get-tuple-element.56.m_ref, f32[800,6]{1,0:T(8,128)} %bitcast.25), custom_call_target="tpu_custom_call" | custom-call | tf_op jit(solution)/shard_map/pallas_call | solution.py:647
  266.7 0.8 slice.55
  267.5 0.1 broadcast_multiply_fusion
  267.6 0.1 mul.79
  267.7 0.7 fusion.x_ref
  268.4 27.2 %shard_map.279 = f32[32,8,128]{2,1,0:T(8,128)} custom-call(f32[32,8,128]{2,1,0:T(8,128)} %fusion.x_ref), custom_call_target="tpu_custom_call" | custom-call | tf_op jit(solution)/shard_map/pallas_call | solution.py:965
  295.6 1.4 slice.75
  297.0 0.1 convert_reduce_fusion
  297.2 1.0 broadcast_in_dim.19
  298.1 1.2 convert_element_type.52
  299.3 0.7 fusion.1
  300.0 2.1 convert_element_type.50
  302.1 0.8 copy.44
  302.8 0.9 copy.45
  (36 shorter events, 0.2 us)
Async XLA Ops:
  7.2 77.1 %all-gather.3.cloned.1.call-start = ((), (), s32[]{:S(2)}) async-start(), calls=%async_computation.5 | async-start | bytes 2048000 | tf_op jit(solution)/shard_map/all_gather | solution.py:1003
  11.0 34.4 %copy-start.7 = (s32[1,1024]{1,0:T(1,128)S(1)}, s32[1,1024]{1,0:T(1,128)}, u32[]{:S(2)}) copy-start(s32[1,1024]{1,0:T(1,128)} %sr_ref.3) | copy-start | bytes 12292
  43.6 131.5 %reduce-scatter.6.cloned.1.call-start = ((), (), s32[]{:S(2)}) async-start(), calls=%async_computation.3 | async-start | bytes 3584000 | tf_op jit(solution)/shard_map/reduce_scatter | solution.py:1019
  120.4 122.9 %reduce-scatter.10.cloned.1.call-start = ((), (), s32[]{:S(2)}) async-start(), calls=%async_computation.6 | async-start | bytes 3328000
  120.7 44.5 %copy-start = (bf16[1600,1024]{1,0:T(8,128)(2,1)S(1)}, bf16[1600,1024]{1,0:T(8,128)(2,1)}, u32[]{:S(2)}) copy-start(bf16[1600,1024]{1,0:T(8,128)(2,1)} %get-tuple-element.55.l_ref) | copy-start | bytes 9830404
  171.3 4.1 %copy-start.10 = (bf16[800,1024]{1,0:T(8,128)(2,1)S(1)}, bf16[800,1024]{1,0:T(8,128)(2,1)}, u32[]{:S(2)}) copy-start(bf16[800,1024]{1,0:T(8,128)(2,1)} %get-tuple-element.64) | copy-start | bytes 4915204
  171.3 4.1 %copy-start.11 = (bf16[400,1024]{1,0:T(8,128)(2,1)S(1)}, bf16[400,1024]{1,0:T(8,128)(2,1)}, u32[]{:S(2)}) copy-start(bf16[400,1024]{1,0:T(8,128)(2,1)} %get-tuple-element.63) | copy-start | bytes 2457604
  175.2 124.8 %reduce-scatter.8.cloned.1.call-start = ((), (), s32[]{:S(2)}) async-start(), calls=%async_computation.4 | async-start | bytes 2560000 | tf_op jit(solution)/shard_map/reduce_scatter | solution.py:1019
  188.7 47.5 %copy-start.9 = (bf16[800,1024]{1,0:T(8,128)(2,1)S(1)}, bf16[800,1024]{1,0:T(8,128)(2,1)}, u32[]{:S(2)}) copy-start(bf16[800,1024]{1,0:T(8,128)(2,1)} %get-tuple-element.53) | copy-start | bytes 4915204
  241.6 2.8 copy-start.8
  241.6 3.7 %copy-start.4 = (bf16[1,400,800]{2,1,0:T(8,128)(2,1)S(1)}, bf16[1,400,800]{2,1,0:T(8,128)(2,1)}, u32[]{:S(2)}) copy-start(bf16[1,400,800]{2,1,0:T(8,128)(2,1)} %reduce-scatter.6.cloned.1.call-done) | copy-start | bytes 1920004
  246.5 50.5 %copy-start.3 = (bf16[4,100,800]{2,1,0:T(8,128)(2,1)S(1)}, bf16[4,100,800]{2,1,0:T(8,128)(2,1)}, u32[]{:S(2)}) copy-start(bf16[4,100,800]{2,1,0:T(8,128)(2,1)} %get-tuple-element.78) | copy-start | bytes 1920004
  266.7 31.5 %copy-start.5 = (bf16[1,200,1600]{2,1,0:T(8,128)(2,1)S(1)}, bf16[1,200,1600]{2,1,0:T(8,128)(2,1)}, u32[]{:S(2)}) copy-start(bf16[1,200,1600]{2,1,0:T(8,128)(2,1)} %reduce-scatter.10.cloned.1.call-done) | copy-start | bytes 1920004
  295.6 3.7 %copy-start.6 = (f32[32,8,128]{2,1,0:T(8,128)S(1)}, f32[32,8,128]{2,1,0:T(8,128)}, u32[]{:S(2)}) copy-start(f32[32,8,128]{2,1,0:T(8,128)} %shard_map.279) | copy-start | bytes 393220
  297.1 4.9 %copy-start.1 = (bf16[800,256]{1,0:T(8,128)(2,1)S(1)}, bf16[800,256]{1,0:T(8,128)(2,1)}, u32[]{:S(2)}) copy-start(bf16[800,256]{1,0:T(8,128)(2,1)} %shard_map.278) | copy-start | bytes 1228804
  298.1 4.7 %copy-start.2 = (f32[800,256]{1,0:T(8,128)S(1)}, f32[800,256]{1,0:T(8,128)}, u32[]{:S(2)}) copy-start(f32[800,256]{1,0:T(8,128)} %get-tuple-element.72) | copy-start | bytes 2457604
Sparse Core Ops, SparseCore 0:
  43.7 40.4 all-gather.2
  120.5 54.5 reduce-scatter.5
  177.5 65.8 reduce-scatter.9
  245.5 48.3 reduce-scatter.7
